TPU v7x, 8 devices: a whole 2x2x1 slice. The times are simulated.
8 devices in a mesh: tp: 2 (over z, y), dp: 4 (over x, core).
Axes of the slice: x: 2, y: 2, z: 1, core: 2. Of those that a mesh axis runs over, the one named last changes fastest.
Arguments:
- hidden: bfloat16 [4, 512, 1024], P('dp')
- residual: float32 [4, 512, 1024], P('dp')
- targets: int32 [4, 512], P('dp')
- embedding: bfloat16 [50280, 1024], P('tp')
- norm_w: float32 [1024], replicated
Outputs:
- output 1: float32 [], replicated
- output 2: float32 [4, 512, 1024], P('dp')
- output 3: float32 [50280, 1024], P('tp')
- output 4: float32 [1024], replicated
All inputs are finite; a program needn't handle non-finite values.
Results may differ from a plain program's by a relative error of at most 0.001.
Values sent between devices are 32-bit elements.
A program may use at most 1 GiB of HBM per device.

v0:
```python
import jax
import jax.numpy as jnp
from jax import lax
from jax.sharding import PartitionSpec as P

NORM_EPS = 1e-5


def solution(mesh):
    def program(hidden, residual, targets, embedding, norm_w):
        inv_n = 1.0 / (hidden.shape[0] * hidden.shape[1])

        def local_part(hid_loc, res_loc, tgt_loc, emb_loc, norm_vec):
            n_batch, n_seq, d_model = hid_loc.shape
            n_rows = n_batch * n_seq
            vocab_loc = emb_loc.shape[0]
            resid = (res_loc + hid_loc.astype(jnp.float32)).reshape(n_rows, d_model)
            tgt_rows = tgt_loc.reshape(n_rows)
            inv_rms = lax.rsqrt(jnp.mean(resid * resid, axis=-1, keepdims=True) + NORM_EPS)
            scaled_r = resid * inv_rms
            h_act = (scaled_r * norm_vec).astype(jnp.bfloat16)
            logits = jnp.einsum('td,vd->tv', h_act, emb_loc, preferred_element_type=jnp.float32)
            row_max = lax.pmax(jnp.max(logits, axis=-1, keepdims=True), 'tp')
            exp_shift = jnp.exp(logits - row_max)
            local_ids = tgt_rows - lax.axis_index('tp') * vocab_loc
            is_target = lax.broadcasted_iota(jnp.int32, (1, vocab_loc), 1) == local_ids[:, None]
            part_stats = jnp.stack([jnp.sum(exp_shift, axis=-1), jnp.sum(jnp.where(is_target, logits, 0.0), axis=-1)], axis=-1)
            tok_stats = lax.psum(part_stats, 'tp')
            sum_exp = tok_stats[:, 0:1]
            loss_part = jnp.sum(row_max[:, 0] + jnp.log(tok_stats[:, 0]) - tok_stats[:, 1]) * inv_n
            prob_rows = exp_shift / sum_exp
            dlogits = (jnp.where(is_target, prob_rows - 1.0, prob_rows) * inv_n).astype(jnp.bfloat16)
            grad_h = lax.psum(jnp.einsum('tv,vd->td', dlogits, emb_loc, preferred_element_type=jnp.float32), 'tp')
            grad_emb = lax.psum(jnp.einsum('tv,td->vd', dlogits, h_act, preferred_element_type=jnp.float32), 'dp')
            grad_scaled = grad_h * norm_vec
            grad_r = inv_rms * (grad_scaled - scaled_r * jnp.mean(grad_scaled * scaled_r, axis=-1, keepdims=True))
            grad_w, loss_mean = lax.psum((jnp.sum(grad_h * scaled_r, axis=0), loss_part), 'dp')
            return loss_mean, grad_r.reshape(n_batch, n_seq, d_model), grad_emb, grad_w

        sharded = jax.shard_map(
            local_part, mesh=mesh,
            in_specs=(P('dp', None, None), P('dp', None, None), P('dp', None), P('tp', None), P(None)),
            out_specs=(P(), P('dp', None, None), P('tp', None), P(None)),
            check_vma=False)
        return sharded(hidden, residual, targets, embedding, norm_w)

    return program
```

profile of v0, /device:TPU:0, one launch (start us, length us, event | category | flops | bytes accessed | tf_op | source)
XLA Modules:
  0.0 1955.5 jit_solution(5043800180979453566)
XLA Ops:
  7.2 0.0 all-reduce.4.cloned.1.call-start
  7.2 2.2 fusion.3
  9.4 0.0 copy-start.1
  9.4 43.1 %fusion.7 = (f32[512]{0:T(512)S(1)}, f32[512,25140]{0,1:T(8,128)}) fusion(bf16[25140,1024]{1,0:T(8,128)(2,1)} %param.8, f32[1,512,1024]{2,1,0:T(8,128)S(1)} %get-tuple-element.11, f32[1024]{0:T(1024)} %param.9, f32[512]{0:T(512)S(1)} %add_rsqrt_fusion), kind=kOutput, calls=%fused_computation.23 | convolution fusion | flops 26375645184 | bytes 105078784 | tf_op jit(solution)/shard_map/td,vd->tv/dot_general | solution.py:22
  52.6 6.2 pmax.7
  58.8 0.0 copy-done.1
  58.8 22.3 %fusion.2 = (f32[512]{0:T(512)S(1)}, f32[512]{0:T(512)S(1)}) fusion(f32[512,25140]{0,1:T(8,128)} %get-tuple-element.15, f32[512]{0:T(512)S(1)} %pmax.7, s32[512]{0:T(512)S(1)} %bitcast.31), kind=kLoop, calls=%fused_computation.6 | loop fusion | flops 64357376 | bytes 51494912 | tf_op jit(solution)/shard_map/reduce_sum | solution.py:27
  81.2 4.9 psum.35
  86.1 26.5 %fusion.1 = bf16[512,25140]{0,1:T(8,128)(2,1)} fusion(f32[512,25140]{0,1:T(8,128)} %get-tuple-element.15, f32[512]{0:T(512)S(1)} %bitcast.33, s32[512]{0:T(512)S(1)} %bitcast.32, f32[512]{0:T(512)S(1)} %pmax.7), kind=kLoop, calls=%fused_computation.2 | loop fusion | flops 90101760 | bytes 77236224 | tf_op jit(solution)/shard_map/convert_element_type | solution.py:32
  112.6 0.0 copy-start
  112.6 37.0 %fusion.8 = f32[512,1024]{1,0:T(8,128)} fusion(bf16[512,25140]{0,1:T(8,128)(2,1)} %fusion.1, bf16[25140,1024]{1,0:T(8,128)(2,1)} %param.8), kind=kOutput, calls=%fused_computation.24 | convolution fusion | flops 26361200640 | bytes 79327232 | tf_op jit(solution)/shard_map/tv,vd->td/dot_general | solution.py:33
  149.6 0.0 all-reduce.4.cloned.1.call-update
  149.6 0.3 all-reduce.6.cloned.1.call-start
  149.9 0.0 copy-done
  149.9 46.0 %fusion.4 = f32[25140,1024]{1,0:T(8,128)} fusion(bf16[512,25140]{0,1:T(8,128)(2,1)} %fusion.1, f32[1,512,1024]{2,1,0:T(8,128)S(1)} %get-tuple-element.11, f32[1024]{0:T(1024)S(1)} %copy-done, f32[512]{0:T(512)S(1)} %add_rsqrt_fusion), kind=kOutput, calls=%fused_computation.20 | convolution fusion | flops 26362773504 | bytes 130820096 | tf_op jit(solution)/shard_map/tv,td->vd/dot_general | solution.py:34
  195.9 0.0 all-reduce.6.cloned.1.call-update
  195.9 0.6 subtract_reduce_fusion
  197.2 11.2 all-reduce.4.cloned.1.call-done
  208.4 2.2 multiply_reduce_fusion
  210.6 7.2 all-reduce
  217.8 3.3 multiply_bitcast_fusion
  221.1 1660.6 %all-reduce.6.cloned.1.call-done = f32[25140,1024]{1,0:T(8,128)} async-done(((f32[25140,1024]{1,0:T(8,128)}), f32[25140,1024]{1,0:T(8,128)}) %all-reduce.6.cloned.1.call-update) | async-done | bytes 102973456 | tf_op jit(solution)/shard_map/psum | solution.py:34
  1881.7 67.0 %copy.11 = f32[25140,1024]{1,0:T(8,128)} copy(f32[25140,1024]{1,0:T(8,128)} %all-reduce.6.cloned.1.call-done) | data formatting | bytes 205946880
  (5 shorter events, 0.0 us)
Async XLA Ops:
  7.2 201.2 %all-reduce.4.cloned.1.call-start = ((), (), s32[]{:S(2)}) async-start(), calls=%async_computation | async-start | bytes 4194304 | tf_op jit(solution)/shard_map/psum | solution.py:33
  9.4 49.4 %copy-start.1 = (s32[1,512]{1,0:T(1,128)S(1)}, s32[1,512]{1,0:T(1,128)}, u32[]{:S(2)}) copy-start(s32[1,512]{1,0:T(1,128)} %param.7) | copy-start | bytes 6148
  112.6 37.3 %copy-start = (f32[1024]{0:T(1024)S(1)}, f32[1024]{0:T(1024)}, u32[]{:S(2)}) copy-start(f32[1024]{0:T(1024)} %param.9) | copy-start | bytes 12292
  149.6 1732.0 %all-reduce.6.cloned.1.call-start = ((), (), s32[]{:S(2)}) async-start(), calls=%async_computation.1 | async-start | bytes 205979648 | tf_op jit(solution)/shard_map/psum | solution.py:34
Sparse Core Ops, SparseCore 0:
  149.8 58.6 all-reduce.3
  211.5 1670.1 all-reduce.5
where the time goes:
time: 1960 us
  waiting for transfers between devices  1670 us (85%)
  matrix products  126 us (6%)
  local copies, waits for them, and re-layouts  67.1 us (3%)
  other arithmetic  57.2 us (3%)
    psum x1, waiting for transfers between devices, local_part(): lax.psum(jnp.einsum('tv,td->vd', dlogits, h_act, preferred_element_type=j...  1660 us
    unnamed x5, local copies, waits for them, and re-layouts  67 us
    dot_general x1, matrix products, local_part(): jnp.einsum('tv,td->vd', dlogits, h_act, preferred_element_type=jnp.float32)  46 us
    dot_general x1, matrix products, local_part(): jnp.einsum('td,vd->tv', h_act, emb_loc, preferred_element_type=jnp.float32)  43.1 us
  transfers between devices with their start and end apart: 2, of which 2 were waited for; matrix products, arithmetic and copies ran while one was open for 3% of the time, Pallas kernels for 0%

commit v1 on v0

v1 whole, which is shorter than its diff:
```python
import jax
import jax.numpy as jnp
from jax import lax
from jax.sharding import PartitionSpec as P

NORM_EPS = 1e-5


def solution(mesh):
    def program(hidden, residual, targets, embedding, norm_w):
        inv_n = 1.0 / (hidden.shape[0] * hidden.shape[1])

        def local_part(hid_loc, res_loc, tgt_loc, emb_loc, norm_vec):
            n_batch, n_seq, d_model = hid_loc.shape
            n_rows = n_batch * n_seq
            vocab_loc = emb_loc.shape[0]
            resid = (res_loc + hid_loc.astype(jnp.float32)).reshape(n_rows, d_model)
            inv_rms = lax.rsqrt(jnp.mean(resid * resid, axis=-1, keepdims=True) + NORM_EPS)
            scaled_r = resid * inv_rms
            scaled_all = lax.all_gather(scaled_r, 'dp', tiled=True)
            tgt_all = lax.all_gather(tgt_loc.reshape(n_rows), 'dp', tiled=True)
            h_act = (scaled_all * norm_vec).astype(jnp.bfloat16)
            logits = jnp.einsum('td,vd->tv', h_act, emb_loc, preferred_element_type=jnp.float32)
            part_max = jnp.max(logits, axis=-1, keepdims=True)
            local_ids = tgt_all - lax.axis_index('tp') * vocab_loc
            is_target = lax.broadcasted_iota(jnp.int32, (1, vocab_loc), 1) == local_ids[:, None]
            part_sum = jnp.sum(jnp.exp(logits - part_max), axis=-1, keepdims=True)
            part_tgt = jnp.sum(jnp.where(is_target, logits, 0.0), axis=-1, keepdims=True)
            parts = lax.all_gather(jnp.concatenate([part_max, part_sum, part_tgt], axis=-1), 'tp')
            row_max = jnp.max(parts[:, :, 0:1], axis=0)
            sum_exp = jnp.sum(parts[:, :, 1:2] * jnp.exp(parts[:, :, 0:1] - row_max), axis=0)
            tgt_logit = jnp.sum(parts[:, :, 2:3], axis=0)
            loss_mean = jnp.sum(row_max + jnp.log(sum_exp) - tgt_logit) * inv_n
            prob_rows = jnp.exp(logits - row_max) / sum_exp
            dlogits = (jnp.where(is_target, prob_rows - 1.0, prob_rows) * inv_n).astype(jnp.bfloat16)
            my_rows = lax.dynamic_slice_in_dim(dlogits, lax.axis_index('dp') * n_rows, n_rows, 0)
            grad_h = lax.psum(jnp.einsum('tv,vd->td', my_rows, emb_loc, preferred_element_type=jnp.float32), 'tp')
            grad_emb = jnp.einsum('tv,td->vd', dlogits, h_act, preferred_element_type=jnp.float32)
            grad_scaled = grad_h * norm_vec
            grad_r = inv_rms * (grad_scaled - scaled_r * jnp.mean(grad_scaled * scaled_r, axis=-1, keepdims=True))
            grad_w = lax.psum(jnp.sum(grad_h * scaled_r, axis=0), 'dp')
            return loss_mean, grad_r.reshape(n_batch, n_seq, d_model), grad_emb, grad_w

        sharded = jax.shard_map(
            local_part, mesh=mesh,
            in_specs=(P('dp', None, None), P('dp', None, None), P('dp', None), P('tp', None), P(None)),
            out_specs=(P(), P('dp', None, None), P('tp', None), P(None)),
            check_vma=False)
        return sharded(hidden, residual, targets, embedding, norm_w)

    return program
```

time: 1960 us -> 536 us (0.27)
  waiting for transfers between devices: 1670 us -> 48.3 us
  matrix products: 126 us -> 276 us
  other arithmetic: 57.2 us -> 174 us
  local copies, waits for them, and re-layouts: 67.1 us -> 0.66 us
    psum x2 -> x1, waiting for transfers between devices: 1670 us -> 0.02 us  [local_part(): lax.psum(jnp.einsum('tv,vd->td', my_rows, emb_loc, preferred_element_type...]
    dot_general x1, matrix products: 43.1 us -> 121 us  [local_part(): jnp.einsum('td,vd->tv', h_act, emb_loc, preferred_element_type=jnp.float32)]
    dot_general x1, matrix products: 46 us -> 119 us  [local_part(): jnp.einsum('tv,td->vd', dlogits, h_act, preferred_element_type=jnp.float32)]
    convert_element_type x1, other arithmetic: 26.5 us -> 98.3 us  [local_part(): (jnp.where(is_target, prob_rows - 1.0, prob_rows) * inv_n).astype(jnp.bfl...]
    unnamed x5 -> x20, local copies, waits for them, and re-layouts: 67 us -> 0.6 us
    all_gather x0 -> x1, waiting for transfers between devices: none -> 48.2 us  [local_part(): scaled_all = lax.all_gather(scaled_r, 'dp', tiled=True)]
    reduce_sum x3 -> x4, other arithmetic: 25.1 us -> 66.1 us  [the longest x1 62.6 us: local_part(): part_sum = jnp.sum(jnp.exp(logits - part_max), axis=-1, keepdims=True)]
  transfers between devices with their start and end apart: 2 -> 2, of which waited for: 2 -> 1; matrix products, arithmetic and copies ran while one was open for 3% -> 23% of each run, Pallas kernels for 0% -> 0%
where the time goes in v1:
time: 536 us
  matrix products  276 us (51%)
  other arithmetic  174 us (32%)
  waiting for transfers between devices  48.3 us (9%)
  blocking collectives  20.9 us (4%)
  between operations  16 us (3%)
    dot_general x1, matrix products, local_part(): jnp.einsum('td,vd->tv', h_act, emb_loc, preferred_element_type=jnp.float32)  121 us
    dot_general x1, matrix products, local_part(): jnp.einsum('tv,td->vd', dlogits, h_act, preferred_element_type=jnp.float32)  119 us
    convert_element_type x1, other arithmetic, local_part(): (jnp.where(is_target, prob_rows - 1.0, prob_rows) * inv_n).astype(jnp.bfl...  98.3 us
    reduce_sum x1, other arithmetic, local_part(): part_sum = jnp.sum(jnp.exp(logits - part_max), axis=-1, keepdims=True)  62.6 us
    all_gather x1, waiting for transfers between devices, local_part(): scaled_all = lax.all_gather(scaled_r, 'dp', tiled=True)  48.2 us
    dot_general x1, matrix products, local_part(): jnp.einsum('tv,vd->td', my_rows, emb_loc, preferred_element_type=jnp.floa...  35.7 us
  transfers between devices with their start and end apart: 2, of which 1 were waited for; matrix products, arithmetic and copies ran while one was open for 23% of the time, Pallas kernels for 0%

profile of v1, /device:TPU:0, one launch (start us, length us, event | category | flops | bytes accessed | tf_op | source)
XLA Modules:
  0.0 535.6 jit_solution(14666612098915587725)
XLA Ops:
  7.2 0.0 all-gather.4.cloned.1.call-start
  7.2 2.2 fusion.4
  9.4 0.0 copy-start.7
  9.4 0.6 copy-done.7
  10.0 3.4 bitcast_multiply_fusion
  13.4 0.0 all-gather.4.cloned.1.call-update
  13.4 0.0 all-reduce.2.cloned.1.call-start
  13.5 9.8 %all-gather = s32[1,2048]{1,0:T(1,128)S(1)} all-gather(s32[1,512]{1,0:T(1,128)} %param.7), channel_id=2, replica_groups=mesh['tp'=2,'dp'=4] {'dp'}, dimensions={1}, use_global_device_ids=true | all-gather | bytes 10240 | tf_op jit(solution)/shard_map/all_gather | solution.py:21
  23.3 0.6 broadcast_subtract_fusion
  23.9 48.2 %all-gather.4.cloned.1.call-done = f32[2048,1024]{1,0:T(8,128)} async-done(((f32[512,1024]{1,0:T(8,128)}), f32[2048,1024]{1,0:T(8,128)}) %all-gather.4.cloned.1.call-update) | async-done | bytes 8388624 | tf_op jit(solution)/shard_map/all_gather | solution.py:20
  72.2 120.7 %fusion.9 = (f32[2048]{0:T(1024)S(1)}, f32[2048,25140]{0,1:T(8,128)}) fusion(bf16[25140,1024]{1,0:T(8,128)(2,1)} %param.8, f32[2048,1024]{1,0:T(8,128)} %all-gather.4.cloned.1.call-done, f32[1024]{0:T(1024)} %param.9), kind=kOutput, calls=%fused_computation.28 | convolution fusion | flops 105500483584 | bytes 265834496 | tf_op jit(solution)/shard_map/td,vd->tv/dot_general | solution.py:23
  192.8 0.0 copy-done.3
  192.8 62.6 %exponential_reduce_fusion = (f32[2048]{0:T(1024)S(1)}, f32[2048]{0:T(1024)S(1)}) fusion(f32[2048,25140]{0,1:T(8,128)} %get-tuple-element.11, f32[2048]{0:T(1024)S(1)} %get-tuple-element.10, s32[2048]{0:T(1024)S(1)} %bitcast.18), kind=kLoop, calls=%fused_computation.5 | loop fusion | flops 257429504 | bytes 205979648 | tf_op jit(solution)/shard_map/reduce_sum | solution.py:27
  255.5 4.8 all-gather.1
  260.3 0.1 reshape.57
  260.4 0.0 copy-start.1
  260.4 0.6 fusion.7
  261.0 98.3 %fusion.1 = bf16[2048,25140]{0,1:T(8,128)(2,1)} fusion(f32[2048,25140]{0,1:T(8,128)} %get-tuple-element.11, f32[2048]{0:T(1024)S(1)} %get-tuple-element.8, f32[2048]{0:T(1024)S(1)} %slice_reduce_fusion.1, s32[2048]{0:T(1024)S(1)} %bitcast.19), kind=kLoop, calls=%fused_computation.2 | loop fusion | flops 360407040 | bytes 308944896 | tf_op jit(solution)/shard_map/convert_element_type | solution.py:35
  359.3 0.0 copy-done.1
  359.3 0.0 copy-done.4
  359.3 0.0 copy-start.9
  359.4 35.7 %fusion.2 = f32[512,1024]{1,0:T(8,128)} fusion(bf16[25140,1024]{1,0:T(8,128)(2,1)} %param.8, bf16[2048,25140]{0,1:T(8,128)(2,1)} %fusion.1, s32[]{:T(128)S(6)} %select_n.13), kind=kOutput, calls=%fused_computation.6 | convolution fusion | flops 26361200640 | bytes 79339520 | tf_op jit(solution)/shard_map/tv,vd->td/dot_general | solution.py:37
  395.1 0.0 all-reduce.2.cloned.1.call-update
  395.1 0.0 copy-done.9
  395.1 0.0 copy-start
  395.2 119.3 %fusion.5 = f32[25140,1024]{1,0:T(8,128)} fusion(bf16[2048,25140]{0,1:T(8,128)(2,1)} %fusion.1, f32[2048,1024]{1,0:T(8,128)} %all-gather.4.cloned.1.call-done, f32[1024]{0:T(1024)S(1)} %copy-done.9), kind=kOutput, calls=%fused_computation.16 | convolution fusion | flops 105448996864 | bytes 214339584 | tf_op jit(solution)/shard_map/tv,td->vd/dot_general | solution.py:38
  514.5 0.6 subtract_reduce_fusion
  515.7 0.0 all-reduce.2.cloned.1.call-done
  515.8 0.0 copy-done
  515.8 2.2 multiply_reduce_fusion
  518.0 6.4 %psum.15 = f32[1024]{0:T(1024)} all-reduce(f32[1024]{0:T(1024)S(1)} %get-tuple-element.6), channel_id=1, replica_groups=mesh['tp'=2,'dp'=4] {'dp'}, use_global_device_ids=true, to_apply=%region_11.12 | all-reduce | flops 1024 | bytes 8192 | tf_op jit(solution)/shard_map/psum | solution.py:41
  524.3 3.3 multiply_bitcast_fusion
  (14 shorter events, 0.1 us)
Async XLA Ops:
  7.2 65.0 %all-gather.4.cloned.1.call-start = ((), (), s32[]{:S(2)}) async-start(), calls=%async_computation | async-start | bytes 10485760 | tf_op jit(solution)/shard_map/all_gather | solution.py:20
  9.4 0.6 copy-start.7
  13.4 502.3 %all-reduce.2.cloned.1.call-start = ((), (), s32[]{:S(2)}) async-start(), calls=%async_computation.1 | async-start | bytes 4194304 | tf_op jit(solution)/shard_map/psum | solution.py:37
  72.2 120.7 %copy-start.3 = (s32[1,2048]{1,0:T(1,128)S(1)}, s32[1,2048]{1,0:T(1,128)}, u32[]{:S(2)}) copy-start(s32[1,2048]{1,0:T(1,128)} %broadcast_subtract_fusion) | copy-start | bytes 24580
  260.4 99.0 %copy-start.1 = (f32[2048]{0:T(1024)}, f32[2048]{0:T(1024)S(1)}, u32[]{:S(2)}) copy-start(f32[2048]{0:T(1024)S(1)} %slice_reduce_fusion.1) | copy-start | bytes 24580
  261.0 98.3 %copy-start.4 = (f32[2048]{0:T(1024)}, f32[2048]{0:T(1024)S(1)}, u32[]{:S(2)}) copy-start(f32[2048]{0:T(1024)S(1)} %get-tuple-element.8) | copy-start | bytes 24580
  359.3 35.8 %copy-start.9 = (f32[1024]{0:T(1024)S(1)}, f32[1024]{0:T(1024)}, u32[]{:S(2)}) copy-start(f32[1024]{0:T(1024)} %param.9) | copy-start | bytes 12292
  395.1 119.3 %copy-start.2 = (f32[2048]{0:T(1024)S(1)}, f32[2048]{0:T(1024)}, u32[]{:S(2)}) copy-start(f32[2048]{0:T(1024)} %copy-done.1) | copy-start | bytes 24580
  395.1 119.3 %copy-start.5 = (f32[2048]{0:T(1024)S(1)}, f32[2048]{0:T(1024)}, u32[]{:S(2)}) copy-start(f32[2048]{0:T(1024)} %copy-done.4) | copy-start | bytes 24580
  395.1 119.3 %copy-start.6 = (f32[2048]{0:T(1024)S(1)}, f32[2048]{0:T(1024)}, u32[]{:S(2)}) copy-start(f32[2048]{0:T(1024)} %get-tuple-element.9) | copy-start | bytes 24580
  395.1 120.6 %copy-start = (f32[512,1024]{1,0:T(8,128)S(1)}, f32[512,1024]{1,0:T(8,128)}, u32[]{:S(2)}) copy-start(f32[512,1024]{1,0:T(8,128)} %bitcast_multiply_fusion) | copy-start | bytes 6291460
  395.2 129.2 %copy-start.8 = (f32[512]{0:T(512)S(1)}, f32[512]{0:T(512)}, u32[]{:S(2)}) copy-start(f32[512]{0:T(512)} %copy-done.7) | copy-start | bytes 6148
Sparse Core Ops, SparseCore 0:
  13.6 58.5 all-gather.3
  395.2 57.1 all-reduce.1

commit v2 on v0

v2 whole, which is shorter than its diff:
```python
import functools

import jax
import jax.numpy as jnp
from jax import lax
from jax.experimental import pallas as pl
from jax.experimental.pallas import tpu as pltpu
from jax.sharding import PartitionSpec as P

NORM_EPS = 1e-5
CH = 256
STEP = 7
PIECES = (8, 8, 8, 8, 8, 6, 3)
TAIL = 64
F32, BF16 = jnp.float32, jnp.bfloat16
NN = (((1,), (0,)), ((), ()))
NT = (((1,), (1,)), ((), ()))
TN = (((0,), (0,)), ((), ()))
VM = pl.BlockSpec(memory_space=pltpu.VMEM)
HB = pl.BlockSpec(memory_space=pl.ANY)


def dot(a, b, dims):
    return lax.dot_general(a, b, dims, preferred_element_type=F32)


def weights(logit, top, rate, hit, inv_n):
    return (jnp.exp(logit - top) * rate - jnp.where(hit, inv_n, 0.0)).astype(BF16)


def rows_of(n, width, base):
    return lax.broadcasted_iota(jnp.int32, (n, width), 0) + base


def stats_kernel(tail_rows, core_ref, emb_ref, tail_ref, ha_ref, hb_ref, tgt_ref, log_ref, logt_ref, stat_ref, top, total, hits):
    step, core = pl.program_id(0), core_ref[0]
    half = ha_ref.shape[0]

    @pl.when(step == 0)
    def _():
        top[...] = jnp.full_like(top, -jnp.inf)
        total[...] = jnp.zeros_like(total)
        hits[...] = jnp.zeros_like(hits)

    def fold(cols, logit, hit):
        split = logit.reshape(-1, 8, half)
        new = jnp.maximum(top[:, cols], jnp.max(split, axis=0))
        total[:, cols] = total[:, cols] * jnp.exp(top[:, cols] - new) + jnp.sum(jnp.exp(split - new[None]), axis=0)
        top[:, cols] = new
        hits[:, cols] += jnp.sum(jnp.where(hit, logit, 0.0).reshape(-1, 8, half), axis=0)

    for k in range(STEP):
        rows = pl.ds(k * CH, CH)
        for side, h_ref in ((0, ha_ref), (1, hb_ref)):
            cols = pl.ds(side * half, half)
            logit = dot(emb_ref[rows, :], h_ref[...], NT)
            log_ref[rows, cols] = logit
            want = tgt_ref[0:1, cols] - (step * STEP + k) * CH
            fold(cols, logit, rows_of(CH, half, 0) == want)

    @pl.when(step == pl.num_programs(0) - 1)
    def _():
        for side, h_ref in ((0, ha_ref), (1, hb_ref)):
            cols = pl.ds(side * half, half)
            ids = rows_of(TAIL, half, 0)
            live = jnp.logical_and(ids < tail_rows, core == 0)
            logit = jnp.where(live, dot(tail_ref[...], h_ref[...], NT), -jnp.inf)
            logt_ref[:, cols] = logit
            fold(cols, logit, jnp.logical_and(ids == tgt_ref[1:2, cols], live))
        peak = jnp.max(top[...], axis=0, keepdims=True)
        stat_ref[...] = jnp.zeros_like(stat_ref)
        stat_ref[0:1, :] = peak
        stat_ref[1:2, :] = jnp.sum(total[...] * jnp.exp(top[...] - peak), axis=0, keepdims=True)
        stat_ref[2:3, :] = jnp.sum(hits[...], axis=0, keepdims=True)


def dh_kernel(tail_rows, inv_n, core_ref, emb_ref, log_ref, tail_ref, logt_ref, row_ref, tgt_ref, da_ref, db_ref, g_ref, gt_ref):
    step, core = pl.program_id(0), core_ref[0]
    half = da_ref.shape[0]

    @pl.when(step == 0)
    def _():
        da_ref[...] = jnp.zeros_like(da_ref)
        db_ref[...] = jnp.zeros_like(db_ref)

    for k in range(STEP):
        rows = pl.ds(k * CH, CH)
        for side, d_ref in ((0, da_ref), (1, db_ref)):
            cols = pl.ds(side * half, half)
            want = tgt_ref[0:1, cols] - (step * STEP + k) * CH
            g_ref[rows, cols] = weights(log_ref[rows, cols], row_ref[0:1, cols], row_ref[1:2, cols], rows_of(CH, half, 0) == want, inv_n)
            d_ref[...] += dot(g_ref[rows, cols], emb_ref[rows, :], TN)

    @pl.when(step == pl.num_programs(0) - 1)
    def _():
        for side, d_ref in ((0, da_ref), (1, db_ref)):
            cols = pl.ds(side * half, half)
            ids = rows_of(TAIL, half, 0)
            live = jnp.logical_and(ids < tail_rows, core == 0)
            hit = jnp.logical_and(ids == tgt_ref[1:2, cols], live)
            gt_ref[:, cols] = weights(logt_ref[:, cols], row_ref[0:1, cols], row_ref[1:2, cols], hit, inv_n)
            d_ref[...] += dot(gt_ref[:, cols], tail_ref[...], TN)


def grad_kernel(first, count, late, inv_n, core_ref, emb_ref, log_ref, ha_ref, hb_ref, hc_ref, hd_ref, row_ref, rowx_ref, tgt_ref, tgtx_ref, *refs):
    per_core = sum(PIECES)
    refs = list(refs)
    if first:
        refs.pop(0)
    got_ref = refs.pop(0) if late else None
    out_ref, piece_ref, ga_ref, gx_ref, lx_ref, own_sem, got_sem = refs
    step, core = pl.program_id(0), core_ref[0]
    half = ha_ref.shape[0]
    rows = pl.ds(pl.multiple_of(step * CH, CH), CH)

    def own_copy(k):
        place = pl.multiple_of((core * per_core + first + k) * CH, CH)
        return pltpu.make_async_copy(piece_ref.at[pl.ds(pl.multiple_of(k * CH, CH), CH)], out_ref.at[pl.ds(place, CH)], own_sem)

    if late:
        back, size = late
        place = pl.multiple_of(((1 - core) * per_core + back) * CH, CH)
        got_copy = pltpu.make_async_copy(got_ref, out_ref.at[pl.ds(place, size * CH)], got_sem)

        @pl.when(step == 0)
        def _():
            got_copy.start()

    base = (first + step) * CH
    for side in (0, 1):
        cols = pl.ds(side * half, half)
        want = tgt_ref[0:1, cols] - base
        ga_ref[:, cols] = weights(log_ref[:, cols], row_ref[0:1, cols], row_ref[1:2, cols], rows_of(CH, half, 0) == want, inv_n)
    for side, h_ref in ((0, hc_ref), (1, hd_ref)):
        cols = pl.ds(side * half, half)
        lx_ref[:, cols] = dot(emb_ref[...], h_ref[...], NT)
    piece_ref[rows, :] = dot(ga_ref[:, pl.ds(0, half)], ha_ref[...], NN) + dot(ga_ref[:, pl.ds(half, half)], hb_ref[...], NN)
    for side in (0, 1):
        cols = pl.ds(side * half, half)
        want = tgtx_ref[0:1, cols] - base
        gx_ref[:, cols] = weights(lx_ref[:, cols], rowx_ref[0:1, cols], rowx_ref[1:2, cols], rows_of(CH, half, 0) == want, inv_n)
    piece_ref[rows, :] += dot(gx_ref[:, pl.ds(0, half)], hc_ref[...], NN) + dot(gx_ref[:, pl.ds(half, half)], hd_ref[...], NN)
    own_copy(step).start()

    @pl.when(step == count - 1)
    def _():
        def drain(k, _):
            own_copy(k).wait()
            return 0

        lax.fori_loop(0, count, drain, 0)
        if late:
            got_copy.wait()


def tail_kernel(inv_n, core_ref, tail_ref, ha_ref, hb_ref, hc_ref, hd_ref, row_ref, rowx_ref, tgt_ref, tgtx_ref, _, out_ref, g_ref):
    half = ha_ref.shape[0]
    grad = jnp.zeros(out_ref.shape, F32)
    ids = rows_of(TAIL, half, 0)
    for h_ref, r_ref, t_ref, side in ((ha_ref, row_ref, tgt_ref, 0), (hb_ref, row_ref, tgt_ref, 1), (hc_ref, rowx_ref, tgtx_ref, 0), (hd_ref, rowx_ref, tgtx_ref, 1)):
        cols = pl.ds(side * half, half)
        logit = dot(tail_ref[...], h_ref[...], NT)
        g_ref[...] = weights(logit, r_ref[0:1, cols], r_ref[1:2, cols], ids == t_ref[1:2, cols], inv_n)
        grad += dot(g_ref[...], h_ref[...], NN)
    out_ref[...] = grad


def last_kernel(late, core_ref, _, got_ref, out_ref, got_sem):
    back, size = late
    place = pl.multiple_of(((1 - core_ref[0]) * sum(PIECES) + back) * CH, CH)
    copy = pltpu.make_async_copy(got_ref, out_ref.at[pl.ds(place, size * CH)], got_sem)
    copy.start()
    copy.wait()


def cost(flops, moved):
    return pl.CostEstimate(flops=int(flops), bytes_accessed=int(moved), transcendentals=0)


def params(mib):
    return pltpu.CompilerParams(vmem_limit_bytes=mib << 20)


def solution(mesh):
    n_tp, n_dp = mesh.shape['tp'], mesh.shape['dp']

    def program(hidden, residual, targets, embedding, norm_w):
        inv_n = 1.0 / (hidden.shape[0] * hidden.shape[1])

        def local_part(hid_loc, res_loc, tgt_loc, emb_loc, norm_vec):
            n_batch, n_seq, d = hid_loc.shape
            half = n_batch * n_seq
            vocab_loc = emb_loc.shape[0]
            per_core = sum(PIECES)
            tail_rows = vocab_loc - 2 * per_core * CH
            my_tp, my_dp = lax.axis_index('tp'), lax.axis_index('dp')
            core = lax.rem(my_dp, 2)
            core_arg = core.reshape(1)
            swap = [(i, i ^ 1) for i in range(n_dp)]
            cross = [(i, i ^ 2) for i in range(n_dp)]
            flip = [(i, i ^ 1) for i in range(n_tp)]
            flip_swap = [(t * n_dp + i, (t ^ 1) * n_dp + (i ^ 1)) for t in range(n_tp) for i in range(n_dp)]

            resid = (res_loc + hid_loc.astype(F32)).reshape(half, d)
            inv_rms = lax.rsqrt(jnp.mean(resid * resid, axis=-1, keepdims=True) + NORM_EPS)
            scaled = resid * inv_rms
            tgt_own = tgt_loc.reshape(1, half)

            def act(n):
                return (n * norm_vec).astype(BF16)

            scaled_sib = lax.ppermute(scaled, 'dp', swap)
            tgt_sib = lax.ppermute(tgt_own, 'dp', swap)
            scaled_far = lax.ppermute(scaled, 'dp', cross)
            ha, hb = act(scaled), act(scaled_sib)

            def relative(both):
                shifted = both - my_tp * vocab_loc
                rel = jnp.concatenate([shifted - core * (per_core * CH), shifted - 2 * per_core * CH], axis=0)
                return jnp.pad(rel, ((0, 6), (0, 0)))

            tgt_raw = jnp.concatenate([tgt_own, tgt_sib], axis=1)
            tgt_near = relative(tgt_raw)
            tgt_far = relative(lax.ppermute(tgt_raw, 'dp', cross))
            emb_tail = jnp.pad(emb_loc[2 * per_core * CH:], ((0, TAIL - tail_rows), (0, 0)))

            steps, blk = per_core // STEP, STEP * CH
            flops_unit = 2.0 * CH * d * half
            smem = pltpu.SMEM
            logits, logits_tail, stat = pl.pallas_call(
                functools.partial(stats_kernel, tail_rows),
                grid_spec=pltpu.PrefetchScalarGridSpec(
                    num_scalar_prefetch=1, grid=(steps,),
                    in_specs=[pl.BlockSpec((blk, d), lambda i, c: (c[0] * steps + i, 0)), VM, VM, VM, VM],
                    out_specs=[pl.BlockSpec((blk, 2 * half), lambda i, c: (i, 0)), VM, VM],
                    scratch_shapes=[pltpu.VMEM((8, 2 * half), F32)] * 3),
                out_shape=[jax.ShapeDtypeStruct((per_core * CH, 2 * half), F32),
                           jax.ShapeDtypeStruct((TAIL, 2 * half), F32), jax.ShapeDtypeStruct((8, 2 * half), F32)],
                compiler_params=params(44),
                cost_estimate=cost(flops_unit * per_core * 2, per_core * CH * (2 * d + 8 * half)),
            )(core_arg, emb_loc, emb_tail, ha, hb, tgt_near)

            def turned(x):
                return jnp.concatenate([x[:, half:], x[:, :half]], axis=1)

            near = stat[0:3]
            sib = turned(lax.ppermute(near, 'dp', swap))
            over = lax.ppermute(near, 'tp', flip)
            over_sib = turned(lax.ppermute(near, ('tp', 'dp'), flip_swap))
            top = jnp.maximum(jnp.maximum(near[0], sib[0]), jnp.maximum(over[0], over_sib[0]))
            parts = [p[1] * jnp.exp(p[0] - top) for p in (near, sib, over, over_sib)]
            sum_exp = (parts[0] + parts[1]) + (parts[2] + parts[3])
            tgt_logit = (near[2] + sib[2]) + (over[2] + over_sib[2])
            token_loss = top + jnp.log(sum_exp) - tgt_logit
            row_near = jnp.pad(jnp.stack([top, inv_n / sum_exp]), ((0, 6), (0, 0)))
            row_near, scaled_far = lax.optimization_barrier((row_near, scaled_far))
            scaled_far_sib = lax.ppermute(scaled_far, 'dp', swap)
            row_far = lax.ppermute(row_near, 'dp', cross)
            loss_chip = jnp.sum(token_loss[:half]) + jnp.sum(token_loss[half:])
            loss_mean = (loss_chip + lax.ppermute(loss_chip.reshape(1), 'dp', cross)[0]) * inv_n

            dh_own, dh_sib = pl.pallas_call(
                functools.partial(dh_kernel, tail_rows, inv_n),
                grid_spec=pltpu.PrefetchScalarGridSpec(
                    num_scalar_prefetch=1, grid=(steps,),
                    in_specs=[pl.BlockSpec((blk, d), lambda i, c: (c[0] * steps + i, 0)),
                              pl.BlockSpec((blk, 2 * half), lambda i, c: (i, 0)), VM, VM, VM, VM],
                    out_specs=[VM, VM],
                    scratch_shapes=[pltpu.VMEM((blk, 2 * half), BF16), pltpu.VMEM((TAIL, 2 * half), BF16)]),
                out_shape=[jax.ShapeDtypeStruct((half, d), F32)] * 2,
                compiler_params=params(44),
                cost_estimate=cost(flops_unit * per_core * 2, per_core * CH * (2 * d + 8 * half)),
            )(core_arg, emb_loc, logits, emb_tail, logits_tail, row_near, tgt_near)

            row_near, row_far, scaled_far, scaled_far_sib, dh_own, dh_sib = lax.optimization_barrier(
                (row_near, row_far, scaled_far, scaled_far_sib, dh_own, dh_sib))
            hc, hd = act(scaled_far), act(scaled_far_sib)
            dh_chip = dh_own + lax.ppermute(dh_sib, 'dp', swap)
            grad_h = dh_chip + lax.ppermute(dh_chip, 'tp', flip)
            grad_scaled = grad_h * norm_vec
            grad_r = inv_rms * (grad_scaled - scaled * jnp.mean(grad_scaled * scaled, axis=-1, keepdims=True))
            grad_w = jnp.sum(grad_h * scaled, axis=0, keepdims=True)
            grad_w = grad_w + lax.ppermute(grad_w, 'dp', swap)
            grad_w = (grad_w + lax.ppermute(grad_w, 'dp', cross)).reshape(d)

            def piece_call(first, count, out, late, got):
                extra = ([] if out is None else [out]) + ([] if got is None else [got])
                kern = functools.partial(grad_kernel, first, count, late, inv_n)
                return pl.pallas_call(
                    kern,
                    grid_spec=pltpu.PrefetchScalarGridSpec(
                        num_scalar_prefetch=1, grid=(count,),
                        in_specs=[pl.BlockSpec((CH, d), lambda i, c: (c[0] * per_core + first + i, 0)),
                                  pl.BlockSpec((CH, 2 * half), lambda i, c: (first + i, 0))] + [VM] * 8
                        + ([] if out is None else [HB]) + ([] if got is None else [VM]),
                        out_specs=[HB, VM],
                        scratch_shapes=[pltpu.VMEM((CH, 2 * half), BF16), pltpu.VMEM((CH, 2 * half), BF16), pltpu.VMEM((CH, 2 * half), F32),
                                        pltpu.SemaphoreType.DMA, pltpu.SemaphoreType.DMA]),
                    out_shape=[jax.ShapeDtypeStruct((vocab_loc, d), F32), jax.ShapeDtypeStruct((count * CH, d), F32)],
                    input_output_aliases={} if out is None else {11: 0},
                    compiler_params=params(14),
                    cost_estimate=cost(flops_unit * count * 6, count * CH * (2 * d + 8 * half + 8 * d)),
                )(core_arg, emb_loc, logits, ha, hb, hc, hd, row_near, row_far, tgt_near, tgt_far, *extra)

            out, first, arrived = None, 0, []
            for k, count in enumerate(PIECES):
                late, got = arrived[k - 2] if k >= 2 else (None, None)
                out, piece = piece_call(first, count, out, late, got)
                arrived.append(((first, count), lax.ppermute(piece, 'dp', swap)))
                first += count

            out = pl.pallas_call(
                functools.partial(tail_kernel, inv_n),
                grid_spec=pltpu.PrefetchScalarGridSpec(
                    num_scalar_prefetch=1, grid=(1,), in_specs=[VM] * 9 + [HB],
                    out_specs=pl.BlockSpec((TAIL, d), lambda i, c: (2 * per_core * CH // TAIL, 0)),
                    scratch_shapes=[pltpu.VMEM((TAIL, half), BF16)]),
                out_shape=jax.ShapeDtypeStruct((vocab_loc, d), F32),
                input_output_aliases={10: 0},
                compiler_params=params(14),
                cost_estimate=cost(2.0 * TAIL * d * half * 8, 4 * TAIL * d),
            )(core_arg, emb_tail, ha, hb, hc, hd, row_near, row_far, tgt_near, tgt_far, out)
            for late, got in arrived[-2:]:
                out = pl.pallas_call(
                    functools.partial(last_kernel, late),
                    grid_spec=pltpu.PrefetchScalarGridSpec(
                        num_scalar_prefetch=1, grid=(1,), in_specs=[HB, VM], out_specs=HB, scratch_shapes=[pltpu.SemaphoreType.DMA]),
                    out_shape=jax.ShapeDtypeStruct((vocab_loc, d), F32),
                    input_output_aliases={1: 0},
                    compiler_params=params(14),
                    cost_estimate=cost(1e6, 4 * late[1] * CH * d),
                )(core_arg, out, got)
            return loss_mean, grad_r.reshape(n_batch, n_seq, d), out, grad_w

        sharded = jax.shard_map(
            local_part, mesh=mesh,
            in_specs=(P('dp', None, None), P('dp', None, None), P('dp', None), P('tp', None), P(None)),
            out_specs=(P(), P('dp', None, None), P('tp', None), P(None)),
            check_vma=False)
        return sharded(hidden, residual, targets, embedding, norm_w)

    return program
```

time: 1960 us -> 319 us (0.16)
  waiting for transfers between devices: 1670 us -> 58.1 us
  Pallas kernels: 0 us -> 224 us
  matrix products: 126 us -> 0 us
  local copies, waits for them, and re-layouts: 67.1 us -> 0.56 us
  other arithmetic: 57.2 us -> 18 us
    psum x2 -> x0, waiting for transfers between devices: 1670 us -> none  [the longest x1 1660 us: local_part(): lax.psum(jnp.einsum('tv,td->vd', dlogits, h_act, preferred_element_type=j...]
    pallas_call x0 -> x12, Pallas kernels: none -> 224 us  [the longest x7 132 us: piece_call(): pl.pallas_call(kern, grid_spec=pltpu.PrefetchScalarGridSpec(num_scalar_pr...]
    dot_general x3 -> x0, matrix products: 126 us -> none  [the longest x1 46 us: local_part(): jnp.einsum('tv,td->vd', dlogits, h_act, preferred_element_type=jnp.float32)]
    unnamed x5 -> x53, local copies, waits for them, and re-layouts: 67 us -> 0.51 us
    ppermute x0 -> x21, waiting for transfers between devices: none -> 58.1 us  [the longest x1 43.8 us: local_part(): grad_h = dh_chip + lax.ppermute(dh_chip, 'tp', flip)]
    convert_element_type x1 -> x2, other arithmetic: 26.5 us -> 3.54 us  [act(): return (n * norm_vec).astype(BF16)]
    reduce_sum x3 -> x2, other arithmetic: 25.1 us -> 5.15 us  [the longest x1 4.54 us: local_part(): grad_w = jnp.sum(grad_h * scaled, axis=0, keepdims=True)]
  transfers between devices with their start and end apart: 2 -> 21, of which waited for: 2 -> 8; matrix products, arithmetic and copies ran while one was open for 3% -> 3% of each run, Pallas kernels for 0% -> 63%
where the time goes in v2:
time: 319 us; the launch traced here: 318 us
  Pallas kernels  224 us (70%)
  waiting for transfers between devices  58.1 us (18%)
  other arithmetic  18 us (6%)
  starting transfers between devices  13.6 us (4%)
  between operations  4.13 us (1%)
    pallas_call x7, Pallas kernels, piece_call(): pl.pallas_call(kern, grid_spec=pltpu.PrefetchScalarGridSpec(num_scalar_pr...  132 us
    ppermute x1, waiting for transfers between devices, local_part(): grad_h = dh_chip + lax.ppermute(dh_chip, 'tp', flip)  43.8 us
    pallas_call x1, Pallas kernels, local_part(): pl.pallas_call(functools.partial(stats_kernel, tail_rows), grid_spec=pltp...  43.3 us
    pallas_call x1, Pallas kernels, local_part(): pl.pallas_call(functools.partial(dh_kernel, tail_rows, inv_n), grid_spec=...  37.1 us
    pallas_call x2, Pallas kernels, local_part(): pl.pallas_call(functools.partial(last_kernel, late), grid_spec=pltpu.Pref...  9.06 us
  transfers between devices with their start and end apart: 21, of which 8 were waited for; matrix products, arithmetic and copies ran while one was open for 3% of the time, Pallas kernels for 63%

profile of v2, /device:TPU:0, one launch (start us, length us, event | category | flops | bytes accessed | tf_op | source)
XLA Modules:
  0.0 318.5 jit_solution(4216731428413840160)
XLA Ops:
  0.7 2.4 fusion
  3.4 1.7 multiply_convert_fusion.3
  5.2 0.9 collective-permute-start
  6.0 2.5 collective-permute-start.6
  8.8 1.0 collective-permute-done.1
  9.9 1.8 multiply_convert_fusion.2.hb_ref
  11.7 43.3 %shard_map.84 = (f32[12544,1024]{1,0:T(8,128)}, f32[64,1024]{1,0:T(8,128)S(1)}, f32[8,1024]{1,0:T(8,128)S(1)}) custom-call(s32[1]{0:T(128)} %bitcast.core_ref, bf16[25140,1024]{1,0:T(8,128)(2,1)} %emb_ref.17, bf16[64,1024]{1,0:T(8,128)(2,1)S(1)} %pad.15.tail_ref, bf16[512,1024]{1,0:T(8,128)(2,1)S(1)} %get-tuple-element.68.ha_ref, ...), custom_call_target="tpu_custom_call" | custom-call | flops 26306674688 | bytes 77070336 | tf_op jit(solution)/shard_map/pallas_call | solution.py:230
  55.0 2.6 collective-permute-start.4
  58.0 1.1 collective-permute-done.4
  59.1 2.3 collective-permute-done.3
  61.4 0.6 maximum_maximum_fusion
  62.0 0.6 add_divide_fusion
  62.6 1.5 collective-permute-start.7
  64.2 37.1 %shard_map.85 = (f32[512,1024]{1,0:T(8,128)S(1)}, f32[512,1024]{1,0:T(8,128)S(1)}) custom-call(s32[1]{0:T(128)} %bitcast.core_ref, bf16[25140,1024]{1,0:T(8,128)(2,1)} %emb_ref.17, f32[12544,1024]{1,0:T(8,128)} %get-tuple-element.34.log_ref, bf16[64,1024]{1,0:T(8,128)(2,1)S(1)} %pad.15.tail_ref, f32[64,1024]{1,0:T(8,128)S(1)} %get-tuple-element.35.logt_ref, ...), custom_call_target="tpu_custom_call" | custom-call | flops 26306674688 | bytes 77070336 | tf_op jit(solution)/shard_map/pallas_call | solution.py:262
  101.8 3.8 %collective-permute-done.9 = f32[512,1024]{1,0:T(8,128)S(1)} collective-permute-done((f32[512,1024]{1,0:T(8,128)S(1)}, f32[512,1024]{1,0:T(8,128)S(1)}, u32[]{:S(2)}, u32[]{:S(2)}) %collective-permute-start.9) | collective-permute-done | bytes 2097184 | tf_op jit(solution)/shard_map/ppermute | solution.py:278
  106.8 3.3 %collective-permute-done.11 = s32[1,1024]{1,0:T(1,128)S(1)} collective-permute-done((s32[1,1024]{1,0:T(1,128)S(1)}, s32[1,1024]{1,0:T(1,128)S(1)}, u32[]{:S(2)}, u32[]{:S(2)}) %collective-permute-start.11) | collective-permute-done | bytes 4128 | tf_op jit(solution)/shard_map/ppermute | solution.py:224
  110.2 43.8 %collective-permute-done.10 = f32[512,1024]{1,0:T(8,128)S(1)} collective-permute-done((f32[512,1024]{1,0:T(8,128)S(1)}, f32[512,1024]{1,0:T(8,128)S(1)}, u32[]{:S(2)}, u32[]{:S(2)}) %collective-permute-start.10) | collective-permute-done | bytes 2097184 | tf_op jit(solution)/shard_map/ppermute | solution.py:279
  153.9 4.5 %multiply_reduce_fusion = (f32[1024]{0:T(1024)}, f32[512]{0:T(512)}, bf16[512,1024]{1,0:T(8,128)(2,1)S(1)}, bf16[512,1024]{1,0:T(8,128)(2,1)S(1)}) fusion(f32[512,1024]{1,0:T(8,128)} %get-tuple-element.69, f32[512,1024]{1,0:T(8,128)S(1)} %add.101, f32[512,1024]{1,0:T(8,128)S(1)} %collective-permute-done.10, f32[1024]{0:T(1024)S(1)} %copy-done.8, ...), kind=kLoop, calls=%fused_computation.3 | loop fusion | flops 5241344 | bytes 12593152 | tf_op jit(solution)/shard_map/reduce_sum | solution.py:282
  158.5 18.6 %shard_map.86 = (f32[25140,1024]{1,0:T(8,128)}, f32[2048,1024]{1,0:T(8,128)S(1)}) custom-call(s32[1]{0:T(128)} %bitcast.core_ref, bf16[25140,1024]{1,0:T(8,128)(2,1)} %emb_ref.17, f32[12544,1024]{1,0:T(8,128)} %get-tuple-element.34.log_ref, bf16[512,1024]{1,0:T(8,128)(2,1)S(1)} %get-tuple-element.68.ha_ref, ...), custom_call_target="tpu_custom_call" | custom-call | flops 12884901888 | bytes 29360128 | tf_op jit(solution)/shard_map/pallas_call | solution.py:289
  177.1 18.3 %shard_map.87 = (f32[25140,1024]{1,0:T(8,128)}, f32[2048,1024]{1,0:T(8,128)S(1)}) custom-call(s32[1]{0:T(128)} %bitcast.core_ref, bf16[25140,1024]{1,0:T(8,128)(2,1)} %emb_ref.17, f32[12544,1024]{1,0:T(8,128)} %get-tuple-element.34.log_ref, bf16[512,1024]{1,0:T(8,128)(2,1)S(1)} %get-tuple-element.68.ha_ref, ...), custom_call_target="tpu_custom_call", output_to_operand_aliasing={{0}: (11, {})} | custom-call | flops 12884901888 | bytes 29360128 | tf_op jit(solution)/shard_map/pallas_call | solution.py:289
  195.9 22.2 %shard_map.88 = (f32[25140,1024]{1,0:T(8,128)}, f32[2048,1024]{1,0:T(8,128)}) custom-call(s32[1]{0:T(128)} %bitcast.core_ref, bf16[25140,1024]{1,0:T(8,128)(2,1)} %emb_ref.17, f32[12544,1024]{1,0:T(8,128)} %get-tuple-element.34.log_ref, bf16[512,1024]{1,0:T(8,128)(2,1)S(1)} %get-tuple-element.68.ha_ref, ...), custom_call_target="tpu_custom_call", output_to_operand_aliasing={{0}: (11, {})} | custom-call | flops 12884901888 | bytes 29360128 | tf_op jit(solution)/shard_map/pallas_call | solution.py:289
  218.2 22.1 %shard_map.89 = (f32[25140,1024]{1,0:T(8,128)}, f32[2048,1024]{1,0:T(8,128)}) custom-call(s32[1]{0:T(128)} %bitcast.core_ref, bf16[25140,1024]{1,0:T(8,128)(2,1)} %emb_ref.17, f32[12544,1024]{1,0:T(8,128)} %get-tuple-element.34.log_ref, bf16[512,1024]{1,0:T(8,128)(2,1)S(1)} %get-tuple-element.68.ha_ref, ...), custom_call_target="tpu_custom_call", output_to_operand_aliasing={{0}: (11, {})} | custom-call | flops 12884901888 | bytes 29360128 | tf_op jit(solution)/shard_map/pallas_call | solution.py:289
  240.7 22.1 %shard_map.90 = (f32[25140,1024]{1,0:T(8,128)}, f32[2048,1024]{1,0:T(8,128)}) custom-call(s32[1]{0:T(128)} %bitcast.core_ref, bf16[25140,1024]{1,0:T(8,128)(2,1)} %emb_ref.17, f32[12544,1024]{1,0:T(8,128)} %get-tuple-element.34.log_ref, bf16[512,1024]{1,0:T(8,128)(2,1)S(1)} %get-tuple-element.68.ha_ref, ...), custom_call_target="tpu_custom_call", output_to_operand_aliasing={{0}: (11, {})} | custom-call | flops 12884901888 | bytes 29360128 | tf_op jit(solution)/shard_map/pallas_call | solution.py:289
  262.9 17.6 %shard_map.91 = (f32[25140,1024]{1,0:T(8,128)}, f32[1536,1024]{1,0:T(8,128)}) custom-call(s32[1]{0:T(128)} %bitcast.core_ref, bf16[25140,1024]{1,0:T(8,128)(2,1)} %emb_ref.17, f32[12544,1024]{1,0:T(8,128)} %get-tuple-element.34.log_ref, bf16[512,1024]{1,0:T(8,128)(2,1)S(1)} %get-tuple-element.68.ha_ref, ...), custom_call_target="tpu_custom_call", output_to_operand_aliasing={{0}: (11, {})} | custom-call | flops 9663676416 | bytes 22020096 | tf_op jit(solution)/shard_map/pallas_call | solution.py:289
  281.0 10.6 %shard_map.92 = (f32[25140,1024]{1,0:T(8,128)}, f32[768,1024]{1,0:T(8,128)}) custom-call(s32[1]{0:T(128)} %bitcast.core_ref, bf16[25140,1024]{1,0:T(8,128)(2,1)} %emb_ref.17, f32[12544,1024]{1,0:T(8,128)} %get-tuple-element.34.log_ref, bf16[512,1024]{1,0:T(8,128)(2,1)S(1)} %get-tuple-element.68.ha_ref, ...), custom_call_target="tpu_custom_call", output_to_operand_aliasing={{0}: (11, {})} | custom-call | flops 4831838208 | bytes 11010048 | tf_op jit(solution)/shard_map/pallas_call | solution.py:289
  293.9 1.9 collective-permute-start.5
  295.8 1.7 collective-permute-done.5
  298.2 1.1 collective-permute-done.19
  299.9 4.6 %multiply_bitcast_fusion = f32[1,512,1024]{2,1,0:T(8,128)} fusion(f32[512,1024]{1,0:T(8,128)} %get-tuple-element.69, f32[512]{0:T(512)S(1)} %broadcast_multiply_fusion, f32[1024]{0:T(1024)S(1)} %copy-done.9, f32[512]{0:T(512)S(1)} %copy-done.15, f32[512,1024]{1,0:T(8,128)} %copy-done.4, f32[512,1024]{1,0:T(8,128)} %copy-done.6), kind=kLoop, calls=%fused_computation.6 | loop fusion | flops 2621440 | bytes 8396800 | tf_op jit(solution)/shard_map/reshape | solution.py:333
  305.1 3.1 shard_map.93._
  308.3 5.5 %shard_map.94._ = f32[25140,1024]{1,0:T(8,128)} custom-call(s32[1]{0:T(128)} %bitcast.core_ref, f32[25140,1024]{1,0:T(8,128)} %shard_map.93._, f32[1536,1024]{1,0:T(8,128)} %collective-permute-done.17.got_ref), custom_call_target="tpu_custom_call", output_to_operand_aliasing={{}: (1, {})} | custom-call | flops 1000000 | bytes 6291456 | tf_op jit(solution)/shard_map/pallas_call | solution.py:324
  313.8 3.6 %shard_map.95 = f32[25140,1024]{1,0:T(8,128)} custom-call(s32[1]{0:T(128)} %bitcast.core_ref, f32[25140,1024]{1,0:T(8,128)} %shard_map.94._, f32[768,1024]{1,0:T(8,128)} %collective-permute-done.18.got_ref), custom_call_target="tpu_custom_call", output_to_operand_aliasing={{}: (1, {})} | custom-call | flops 1000000 | bytes 3145728 | tf_op jit(solution)/shard_map/pallas_call | solution.py:324
  (103 shorter events, 6.5 us)
Async XLA Ops:
  5.2 4.7 %collective-permute-start = (f32[512,1024]{1,0:T(8,128)}, f32[512,1024]{1,0:T(8,128)}, u32[]{:S(2)}, u32[]{:S(2)}) collective-permute-start(f32[512,1024]{1,0:T(8,128)} %get-tuple-element.69), channel_id=1, source_target_pairs={{0,1},{1,0},{2,3},{3,2},{4,5},{5,4},{6,7},{7,6}} | collective-permute-start | bytes 6291464 | tf_op jit(solution)/shard_map/ppermute | solution.py:212
  6.0 56.6 %collective-permute-start.6 = (f32[512,1024]{1,0:T(8,128)}, f32[512,1024]{1,0:T(8,128)}, u32[]{:S(2)}, u32[]{:S(2)}) collective-permute-start(f32[512,1024]{1,0:T(8,128)} %get-tuple-element.69), channel_id=1, source_target_pairs={{0,2},{1,3},{2,0},{3,1},{4,6},{5,7},{6,4},{7,5}} | collective-permute-start | bytes 6291464 | tf_op jit(solution)/shard_map/ppermute | solution.py:214
  8.5 1.3 collective-permute-start.1
  8.7 55.4 %copy-start.2 = (bf16[64,1024]{1,0:T(8,128)(2,1)}, bf16[64,1024]{1,0:T(8,128)(2,1)S(1)}, u32[]{:S(2)}) copy-start(bf16[64,1024]{1,0:T(8,128)(2,1)S(1)} %pad.15.tail_ref) | copy-start | bytes 393220
  55.0 4.1 %collective-permute-start.4 = (f32[3,1024]{1,0:T(4,128)S(1)}, f32[3,1024]{1,0:T(4,128)S(1)}, u32[]{:S(2)}, u32[]{:S(2)}) collective-permute-start(f32[3,1024]{1,0:T(4,128)S(1)} %slice.69), channel_id=1, source_target_pairs={{0,5},{1,4},{2,7},{3,6},{4,1},{5,0},{6,3},{7,2}} | collective-permute-start | bytes 36872 | tf_op jit(solution)/shard_map/ppermute | solution.py:249
  57.6 3.7 %collective-permute-start.3 = (f32[3,1024]{1,0:T(4,128)S(1)}, f32[3,1024]{1,0:T(4,128)S(1)}, u32[]{:S(2)}, u32[]{:S(2)}) collective-permute-start(f32[3,1024]{1,0:T(4,128)S(1)} %slice.69), channel_id=1, source_target_pairs={{0,4},{4,0},{1,5},{5,1},{2,6},{6,2},{3,7},{7,3}} | collective-permute-start | bytes 36872 | tf_op jit(solution)/shard_map/ppermute | solution.py:248
  57.9 1.2 collective-permute-start.2
  62.6 38.6 %collective-permute-start.7 = (f32[8,1024]{1,0:T(8,128)S(1)}, f32[8,1024]{1,0:T(8,128)S(1)}, u32[]{:S(2)}, u32[]{:S(2)}) collective-permute-start(f32[8,1024]{1,0:T(8,128)S(1)} %select_maximum_fusion.row_ref), channel_id=1, source_target_pairs={{0,2},{1,3},{2,0},{3,1},{4,6},{5,7},{6,4},{7,5}} | collective-permute-start | bytes 98312 | tf_op jit(solution)/shard_map/ppermute | solution.py:258
  64.1 37.1 %collective-permute-start.8 = (f32[512,1024]{1,0:T(8,128)}, f32[512,1024]{1,0:T(8,128)S(1)}, u32[]{:S(2)}, u32[]{:S(2)}) collective-permute-start(f32[512,1024]{1,0:T(8,128)} %collective-permute-done.6), channel_id=1, source_target_pairs={{0,1},{1,0},{2,3},{3,2},{4,5},{5,4},{6,7},{7,6}} | collective-permute-start | bytes 6291464 | tf_op jit(solution)/shard_map/ppermute | solution.py:257
  101.3 4.3 %collective-permute-start.9 = (f32[512,1024]{1,0:T(8,128)S(1)}, f32[512,1024]{1,0:T(8,128)S(1)}, u32[]{:S(2)}, u32[]{:S(2)}) collective-permute-start(f32[512,1024]{1,0:T(8,128)S(1)} %get-tuple-element.39), channel_id=1, source_target_pairs={{0,1},{1,0},{2,3},{3,2},{4,5},{5,4},{6,7},{7,6}} | collective-permute-start | bytes 6291464 | tf_op jit(solution)/shard_map/ppermute | solution.py:278
  106.0 52.5 %copy-start.4 = (f32[512,1024]{1,0:T(8,128)}, f32[512,1024]{1,0:T(8,128)S(1)}, u32[]{:S(2)}) copy-start(f32[512,1024]{1,0:T(8,128)S(1)} %add.101) | copy-start | bytes 6291460
  106.0 47.9 %collective-permute-start.10 = (f32[512,1024]{1,0:T(8,128)S(1)}, f32[512,1024]{1,0:T(8,128)S(1)}, u32[]{:S(2)}, u32[]{:S(2)}) collective-permute-start(f32[512,1024]{1,0:T(8,128)S(1)} %add.101), channel_id=1, source_target_pairs={{0,4},{4,0},{1,5},{5,1},{2,6},{6,2},{3,7},{7,3}} | collective-permute-start | bytes 6291464 | tf_op jit(solution)/shard_map/ppermute | solution.py:279
  106.5 3.6 %collective-permute-start.11 = (s32[1,1024]{1,0:T(1,128)S(1)}, s32[1,1024]{1,0:T(1,128)S(1)}, u32[]{:S(2)}, u32[]{:S(2)}) collective-permute-start(s32[1,1024]{1,0:T(1,128)S(1)} %constant_dynamic-update-slice_fusion), channel_id=1, source_target_pairs={{0,2},{1,3},{2,0},{3,1},{4,6},{5,7},{6,4},{7,5}} | collective-permute-start | bytes 12296 | tf_op jit(solution)/shard_map/ppermute | solution.py:224
  158.5 122.4 %copy-start = (bf16[512,1024]{1,0:T(8,128)(2,1)}, bf16[512,1024]{1,0:T(8,128)(2,1)S(1)}, u32[]{:S(2)}) copy-start(bf16[512,1024]{1,0:T(8,128)(2,1)S(1)} %get-tuple-element.82.hc_ref) | copy-start | bytes 3145732
  177.1 18.8 %collective-permute-start.12 = (f32[2048,1024]{1,0:T(8,128)S(1)}, f32[2048,1024]{1,0:T(8,128)S(1)}, u32[]{:S(2)}, u32[]{:S(2)}) collective-permute-start(f32[2048,1024]{1,0:T(8,128)S(1)} %get-tuple-element.46), channel_id=1, source_target_pairs={{0,1},{1,0},{2,3},{3,2},{4,5},{5,4},{6,7},{7,6}} | collective-permute-start | bytes 25165832 | tf_op jit(solution)/shard_map/ppermute | solution.py:309
  195.4 22.8 %collective-permute-start.13 = (f32[2048,1024]{1,0:T(8,128)S(1)}, f32[2048,1024]{1,0:T(8,128)S(1)}, u32[]{:S(2)}, u32[]{:S(2)}) collective-permute-start(f32[2048,1024]{1,0:T(8,128)S(1)} %get-tuple-element.48), channel_id=1, source_target_pairs={{0,1},{1,0},{2,3},{3,2},{4,5},{5,4},{6,7},{7,6}} | collective-permute-start | bytes 25165832 | tf_op jit(solution)/shard_map/ppermute | solution.py:309
  218.1 22.6 %collective-permute-start.14 = (f32[2048,1024]{1,0:T(8,128)}, f32[2048,1024]{1,0:T(8,128)S(1)}, u32[]{:S(2)}, u32[]{:S(2)}) collective-permute-start(f32[2048,1024]{1,0:T(8,128)} %get-tuple-element.50), channel_id=1, source_target_pairs={{0,1},{1,0},{2,3},{3,2},{4,5},{5,4},{6,7},{7,6}} | collective-permute-start | bytes 25165832 | tf_op jit(solution)/shard_map/ppermute | solution.py:309
  240.3 22.7 %collective-permute-start.15 = (f32[2048,1024]{1,0:T(8,128)}, f32[2048,1024]{1,0:T(8,128)S(1)}, u32[]{:S(2)}, u32[]{:S(2)}) collective-permute-start(f32[2048,1024]{1,0:T(8,128)} %get-tuple-element.52), channel_id=1, source_target_pairs={{0,1},{1,0},{2,3},{3,2},{4,5},{5,4},{6,7},{7,6}} | collective-permute-start | bytes 25165832 | tf_op jit(solution)/shard_map/ppermute | solution.py:309
  262.9 18.0 %collective-permute-start.16 = (f32[2048,1024]{1,0:T(8,128)}, f32[2048,1024]{1,0:T(8,128)S(1)}, u32[]{:S(2)}, u32[]{:S(2)}) collective-permute-start(f32[2048,1024]{1,0:T(8,128)} %get-tuple-element.54), channel_id=1, source_target_pairs={{0,1},{1,0},{2,3},{3,2},{4,5},{5,4},{6,7},{7,6}} | collective-permute-start | bytes 25165832 | tf_op jit(solution)/shard_map/ppermute | solution.py:309
  280.6 27.7 %collective-permute-start.17 = (f32[1536,1024]{1,0:T(8,128)}, f32[1536,1024]{1,0:T(8,128)}, u32[]{:S(2)}, u32[]{:S(2)}) collective-permute-start(f32[1536,1024]{1,0:T(8,128)} %get-tuple-element.56), channel_id=1, source_target_pairs={{0,1},{1,0},{2,3},{3,2},{4,5},{5,4},{6,7},{7,6}} | collective-permute-start | bytes 18874376 | tf_op jit(solution)/shard_map/ppermute | solution.py:309
  280.9 11.1 %copy-start.11 = (f32[1,1024]{1,0:T(1,128)S(1)}, f32[1,1024]{1,0:T(1,128)}, u32[]{:S(2)}) copy-start(f32[1,1024]{1,0:T(1,128)} %copy-done.10) | copy-start | bytes 12292
  280.9 11.1 %copy-start.13 = (f32[1,1024]{1,0:T(1,128)S(1)}, f32[1,1024]{1,0:T(1,128)}, u32[]{:S(2)}) copy-start(f32[1,1024]{1,0:T(1,128)} %copy-done.12) | copy-start | bytes 12292
  280.9 11.1 %copy-start.17 = (f32[1,1024]{1,0:T(1,128)S(1)}, f32[1,1024]{1,0:T(1,128)}, u32[]{:S(2)}) copy-start(f32[1,1024]{1,0:T(1,128)} %get-tuple-element.71) | copy-start | bytes 12292
  280.9 11.0 %copy-start.18 = (f32[1,1024]{1,0:T(1,128)S(1)}, f32[1,1024]{1,0:T(1,128)}, u32[]{:S(2)}) copy-start(f32[1,1024]{1,0:T(1,128)} %get-tuple-element.72) | copy-start | bytes 12292
  280.9 17.2 %copy-start.16 = (f32[1024]{0:T(1024)S(1)}, f32[1024]{0:T(1024)}, u32[]{:S(2)}) copy-start(f32[1024]{0:T(1024)} %get-tuple-element.58) | copy-start | bytes 12292
  281.0 17.2 %copy-start.24 = (f32[512]{0:T(512)S(1)}, f32[512]{0:T(512)}, u32[]{:S(2)}) copy-start(f32[512]{0:T(512)} %get-tuple-element.59) | copy-start | bytes 6148
  281.0 19.0 %copy-start.9 = (f32[1024]{0:T(1024)S(1)}, f32[1024]{0:T(1024)}, u32[]{:S(2)}) copy-start(f32[1024]{0:T(1024)} %param.9) | copy-start | bytes 12292
  281.0 19.0 %copy-start.15 = (f32[512]{0:T(512)S(1)}, f32[512]{0:T(512)}, u32[]{:S(2)}) copy-start(f32[512]{0:T(512)} %copy-done.14) | copy-start | bytes 6148
  291.6 22.1 %collective-permute-start.18 = (f32[768,1024]{1,0:T(8,128)}, f32[768,1024]{1,0:T(8,128)}, u32[]{:S(2)}, u32[]{:S(2)}) collective-permute-start(f32[768,1024]{1,0:T(8,128)} %get-tuple-element.57), channel_id=1, source_target_pairs={{0,1},{1,0},{2,3},{3,2},{4,5},{5,4},{6,7},{7,6}} | collective-permute-start | bytes 9437192 | tf_op jit(solution)/shard_map/ppermute | solution.py:309
  293.9 3.6 %collective-permute-start.5 = (f32[1]{0:T(128)}, f32[1]{0:T(128)}, u32[]{:S(2)}, u32[]{:S(2)}) collective-permute-start(f32[1]{0:T(128)} %bitcast.11), channel_id=1, source_target_pairs={{0,2},{1,3},{2,0},{3,1},{4,6},{5,7},{6,4},{7,5}} | collective-permute-start | bytes 20 | tf_op jit(solution)/shard_map/ppermute | solution.py:260
  298.2 1.2 collective-permute-start.19
  299.4 5.2 %collective-permute-start.20 = (f32[1,1024]{1,0:T(1,128)S(1)}, f32[1,1024]{1,0:T(1,128)S(1)}, u32[]{:S(2)}, u32[]{:S(2)}) collective-permute-start(f32[1,1024]{1,0:T(1,128)S(1)} %add.103), channel_id=1, source_target_pairs={{0,2},{1,3},{2,0},{3,1},{4,6},{5,7},{6,4},{7,5}} | collective-permute-start | bytes 12296 | tf_op jit(solution)/shard_map/ppermute | solution.py:284
  (16 other events, 92.8 us)

commit v3 on v2

--- a/solution.py
+++ b/solution.py
@@ -7,10 +7,11 @@
 from jax.experimental.pallas import tpu as pltpu
 from jax.sharding import PartitionSpec as P
 
+
 NORM_EPS = 1e-5
 CH = 256
 STEP = 7
-PIECES = (8, 8, 8, 8, 8, 6, 3)
+PIECES = (5, 5, 5, 5, 5, 5, 5, 5, 4, 3, 2)
 TAIL = 64
 F32, BF16 = jnp.float32, jnp.bfloat16
 NN = (((1,), (0,)), ((), ()))
@@ -74,12 +75,13 @@
         stat_ref[2:3, :] = jnp.sum(hits[...], axis=0, keepdims=True)
 
 
-def dh_kernel(tail_rows, inv_n, core_ref, emb_ref, log_ref, tail_ref, logt_ref, row_ref, tgt_ref, da_ref, db_ref, g_ref, gt_ref):
+def dh_kernel(tail_rows, inv_n, core_ref, emb_ref, log_ref, tail_ref, logt_ref, row_ref, tgt_ref, da_ref, db_ref, loss_ref, g_ref, gt_ref):
     step, core = pl.program_id(0), core_ref[0]
     half = da_ref.shape[0]
 
     @pl.when(step == 0)
     def _():
+        loss_ref[...] = jnp.full(loss_ref.shape, jnp.sum(row_ref[2:3, pl.ds(0, half)]) + jnp.sum(row_ref[2:3, pl.ds(half, half)]))
         da_ref[...] = jnp.zeros_like(da_ref)
         db_ref[...] = jnp.zeros_like(db_ref)
 
@@ -102,55 +104,77 @@
             d_ref[...] += dot(gt_ref[:, cols], tail_ref[...], TN)
 
 
-def grad_kernel(first, count, late, inv_n, core_ref, emb_ref, log_ref, ha_ref, hb_ref, hc_ref, hd_ref, row_ref, rowx_ref, tgt_ref, tgtx_ref, *refs):
+def rows_at(core, first, count):
+    return pl.ds(pl.multiple_of((core * sum(PIECES) + first) * CH, CH), count * CH)
+
+
+def grad_kernel(first, count, prev, late, inv_n, core_ref, emb_ref, log_ref, ha_ref, hb_ref, hc_ref, hd_ref, row_ref, rowx_ref, tgt_ref, tgtx_ref, mark_ref, *refs):
     per_core = sum(PIECES)
     refs = list(refs)
-    if first:
-        refs.pop(0)
+    if prev:
+        refs = refs[3:]
+    own_ref = refs.pop(0) if prev else None
     got_ref = refs.pop(0) if late else None
-    out_ref, piece_ref, ga_ref, gx_ref, lx_ref, own_sem, got_sem = refs
-    step, core = pl.program_id(0), core_ref[0]
+    out_ref, emb_buf, log_buf, piece_ref, token_ref, ga_ref, gx_ref, lx_ref, emb_sem, log_sem, own_sem, got_sem = refs
+    core = core_ref[0]
     half = ha_ref.shape[0]
-    rows = pl.ds(pl.multiple_of(step * CH, CH), CH)
-
-    def own_copy(k):
-        place = pl.multiple_of((core * per_core + first + k) * CH, CH)
-        return pltpu.make_async_copy(piece_ref.at[pl.ds(pl.multiple_of(k * CH, CH), CH)], out_ref.at[pl.ds(place, CH)], own_sem)
-
+    token_ref[...] = mark_ref[...]
+
+    def fetch(k):
+        slot = lax.rem(k, 2)
+        mine = pl.ds(pl.multiple_of(k * CH, CH), CH)
+        return (pltpu.make_async_copy(emb_ref.at[rows_at(core, k, 1)], emb_buf.at[slot], emb_sem),
+                pltpu.make_async_copy(log_ref.at[mine], log_buf.at[slot], log_sem))
+
+    writes = []
+    if prev:
+        writes.append(pltpu.make_async_copy(own_ref, out_ref.at[rows_at(core, *prev)], own_sem))
     if late:
-        back, size = late
-        place = pl.multiple_of(((1 - core) * per_core + back) * CH, CH)
-        got_copy = pltpu.make_async_copy(got_ref, out_ref.at[pl.ds(place, size * CH)], got_sem)
-
-        @pl.when(step == 0)
+        writes.append(pltpu.make_async_copy(got_ref, out_ref.at[rows_at(1 - core, *late)], got_sem))
+    if not prev:
+        for copy in fetch(jnp.int32(first)):
+            copy.start()
+        for copy in fetch(jnp.int32(first)):
+            copy.wait()
+    for copy in writes:
+        copy.start()
+
+    def step(i, carry):
+        k = first + i
+        slot = lax.rem(k, 2)
+        rows = pl.ds(pl.multiple_of(i * CH, CH), CH)
+        more = k + 1 < per_core
+
+        @pl.when(more)
         def _():
-            got_copy.start()
-
-    base = (first + step) * CH
-    for side in (0, 1):
-        cols = pl.ds(side * half, half)
-        want = tgt_ref[0:1, cols] - base
-        ga_ref[:, cols] = weights(log_ref[:, cols], row_ref[0:1, cols], row_ref[1:2, cols], rows_of(CH, half, 0) == want, inv_n)
-    for side, h_ref in ((0, hc_ref), (1, hd_ref)):
-        cols = pl.ds(side * half, half)
-        lx_ref[:, cols] = dot(emb_ref[...], h_ref[...], NT)
-    piece_ref[rows, :] = dot(ga_ref[:, pl.ds(0, half)], ha_ref[...], NN) + dot(ga_ref[:, pl.ds(half, half)], hb_ref[...], NN)
-    for side in (0, 1):
-        cols = pl.ds(side * half, half)
-        want = tgtx_ref[0:1, cols] - base
-        gx_ref[:, cols] = weights(lx_ref[:, cols], rowx_ref[0:1, cols], rowx_ref[1:2, cols], rows_of(CH, half, 0) == want, inv_n)
-    piece_ref[rows, :] += dot(gx_ref[:, pl.ds(0, half)], hc_ref[...], NN) + dot(gx_ref[:, pl.ds(half, half)], hd_ref[...], NN)
-    own_copy(step).start()
-
-    @pl.when(step == count - 1)
-    def _():
-        def drain(k, _):
-            own_copy(k).wait()
-            return 0
-
-        lax.fori_loop(0, count, drain, 0)
-        if late:
-            got_copy.wait()
+            for copy in fetch(k + 1):
+                copy.start()
+
+        base = k * CH
+        for side in (0, 1):
+            cols = pl.ds(side * half, half)
+            want = tgt_ref[0:1, cols] - base
+            ga_ref[:, cols] = weights(log_buf[slot, :, cols], row_ref[0:1, cols], row_ref[1:2, cols], rows_of(CH, half, 0) == want, inv_n)
+        for side, h_ref in ((0, hc_ref), (1, hd_ref)):
+            cols = pl.ds(side * half, half)
+            lx_ref[:, cols] = dot(emb_buf[slot], h_ref[...], NT)
+        piece_ref[rows, :] = dot(ga_ref[:, pl.ds(0, half)], ha_ref[...], NN) + dot(ga_ref[:, pl.ds(half, half)], hb_ref[...], NN)
+        for side in (0, 1):
+            cols = pl.ds(side * half, half)
+            want = tgtx_ref[0:1, cols] - base
+            gx_ref[:, cols] = weights(lx_ref[:, cols], rowx_ref[0:1, cols], rowx_ref[1:2, cols], rows_of(CH, half, 0) == want, inv_n)
+        piece_ref[rows, :] += dot(gx_ref[:, pl.ds(0, half)], hc_ref[...], NN) + dot(gx_ref[:, pl.ds(half, half)], hd_ref[...], NN)
+
+        @pl.when(more)
+        def _():
+            for copy in fetch(k + 1):
+                copy.wait()
+
+        return carry
+
+    lax.fori_loop(0, count, step, 0)
+    for copy in writes:
+        copy.wait()
 
 
 def tail_kernel(inv_n, core_ref, tail_ref, ha_ref, hb_ref, hc_ref, hd_ref, row_ref, rowx_ref, tgt_ref, tgtx_ref, _, out_ref, g_ref):
@@ -165,12 +189,16 @@
     out_ref[...] = grad
 
 
-def last_kernel(late, core_ref, _, got_ref, out_ref, got_sem):
-    back, size = late
-    place = pl.multiple_of(((1 - core_ref[0]) * sum(PIECES) + back) * CH, CH)
-    copy = pltpu.make_async_copy(got_ref, out_ref.at[pl.ds(place, size * CH)], got_sem)
-    copy.start()
-    copy.wait()
+def last_kernel(places, core_ref, _, *refs):
+    srcs, out_ref, sems = refs[:len(places)], refs[len(places)], refs[len(places) + 1:]
+    copies = []
+    for src, sem, (other, place) in zip(srcs, sems, places):
+        side = 1 - core_ref[0] if other else core_ref[0]
+        copies.append(pltpu.make_async_copy(src, out_ref.at[rows_at(side, *place)], sem))
+    for copy in copies:
+        copy.start()
+    for copy in copies:
+        copy.wait()
 
 
 def cost(flops, moved):
@@ -221,12 +249,11 @@
 
             tgt_raw = jnp.concatenate([tgt_own, tgt_sib], axis=1)
             tgt_near = relative(tgt_raw)
-            tgt_far = relative(lax.ppermute(tgt_raw, 'dp', cross))
+            tgt_raw_far = lax.ppermute(tgt_raw, 'dp', cross)
             emb_tail = jnp.pad(emb_loc[2 * per_core * CH:], ((0, TAIL - tail_rows), (0, 0)))
 
             steps, blk = per_core // STEP, STEP * CH
             flops_unit = 2.0 * CH * d * half
-            smem = pltpu.SMEM
             logits, logits_tail, stat = pl.pallas_call(
                 functools.partial(stats_kernel, tail_rows),
                 grid_spec=pltpu.PrefetchScalarGridSpec(
@@ -236,7 +263,7 @@
                     scratch_shapes=[pltpu.VMEM((8, 2 * half), F32)] * 3),
                 out_shape=[jax.ShapeDtypeStruct((per_core * CH, 2 * half), F32),
                            jax.ShapeDtypeStruct((TAIL, 2 * half), F32), jax.ShapeDtypeStruct((8, 2 * half), F32)],
-                compiler_params=params(44),
+                compiler_params=params(27),
                 cost_estimate=cost(flops_unit * per_core * 2, per_core * CH * (2 * d + 8 * half)),
             )(core_arg, emb_loc, emb_tail, ha, hb, tgt_near)
 
@@ -252,62 +279,75 @@
             sum_exp = (parts[0] + parts[1]) + (parts[2] + parts[3])
             tgt_logit = (near[2] + sib[2]) + (over[2] + over_sib[2])
             token_loss = top + jnp.log(sum_exp) - tgt_logit
-            row_near = jnp.pad(jnp.stack([top, inv_n / sum_exp]), ((0, 6), (0, 0)))
-            row_near, scaled_far = lax.optimization_barrier((row_near, scaled_far))
+            row_near = jnp.pad(jnp.stack([top, inv_n / sum_exp, token_loss]), ((0, 5), (0, 0)))
+            row_near, scaled_far, tgt_raw_far = lax.optimization_barrier((row_near, scaled_far, tgt_raw_far))
+            tgt_far = relative(tgt_raw_far)
             scaled_far_sib = lax.ppermute(scaled_far, 'dp', swap)
             row_far = lax.ppermute(row_near, 'dp', cross)
-            loss_chip = jnp.sum(token_loss[:half]) + jnp.sum(token_loss[half:])
-            loss_mean = (loss_chip + lax.ppermute(loss_chip.reshape(1), 'dp', cross)[0]) * inv_n
-
-            dh_own, dh_sib = pl.pallas_call(
+
+            dh_own, dh_sib, loss_chip = pl.pallas_call(
                 functools.partial(dh_kernel, tail_rows, inv_n),
                 grid_spec=pltpu.PrefetchScalarGridSpec(
                     num_scalar_prefetch=1, grid=(steps,),
                     in_specs=[pl.BlockSpec((blk, d), lambda i, c: (c[0] * steps + i, 0)),
                               pl.BlockSpec((blk, 2 * half), lambda i, c: (i, 0)), VM, VM, VM, VM],
-                    out_specs=[VM, VM],
+                    out_specs=[VM, VM, VM],
                     scratch_shapes=[pltpu.VMEM((blk, 2 * half), BF16), pltpu.VMEM((TAIL, 2 * half), BF16)]),
-                out_shape=[jax.ShapeDtypeStruct((half, d), F32)] * 2,
-                compiler_params=params(44),
+                out_shape=[jax.ShapeDtypeStruct((half, d), F32)] * 2 + [jax.ShapeDtypeStruct((8, 128), F32)],
+                compiler_params=params(31),
                 cost_estimate=cost(flops_unit * per_core * 2, per_core * CH * (2 * d + 8 * half)),
             )(core_arg, emb_loc, logits, emb_tail, logits_tail, row_near, tgt_near)
 
-            row_near, row_far, scaled_far, scaled_far_sib, dh_own, dh_sib = lax.optimization_barrier(
-                (row_near, row_far, scaled_far, scaled_far_sib, dh_own, dh_sib))
+            tie = lax.optimization_barrier
+            row_near, row_far, scaled_far, scaled_far_sib, dh_own, dh_sib, tgt_far = tie(
+                (row_near, row_far, scaled_far, scaled_far_sib, dh_own, dh_sib, tgt_far))
             hc, hd = act(scaled_far), act(scaled_far_sib)
-            dh_chip = dh_own + lax.ppermute(dh_sib, 'dp', swap)
-            grad_h = dh_chip + lax.ppermute(dh_chip, 'tp', flip)
-            grad_scaled = grad_h * norm_vec
-            grad_r = inv_rms * (grad_scaled - scaled * jnp.mean(grad_scaled * scaled, axis=-1, keepdims=True))
-            grad_w = jnp.sum(grad_h * scaled, axis=0, keepdims=True)
-            grad_w = grad_w + lax.ppermute(grad_w, 'dp', swap)
-            grad_w = (grad_w + lax.ppermute(grad_w, 'dp', cross)).reshape(d)
-
-            def piece_call(first, count, out, late, got):
-                extra = ([] if out is None else [out]) + ([] if got is None else [got])
-                kern = functools.partial(grad_kernel, first, count, late, inv_n)
+            dh_got = lax.ppermute(dh_sib, 'dp', swap)
+            loss_far = lax.ppermute(loss_chip, 'dp', cross)
+
+            def piece_call(first, count, mark, out, bufs, prev, own, late, got):
+                extra = ([] if out is None else [out, *bufs, own]) + ([] if got is None else [got])
+                specs = ([] if out is None else [HB, VM, VM, VM]) + ([] if got is None else [VM])
                 return pl.pallas_call(
-                    kern,
-                    grid_spec=pltpu.PrefetchScalarGridSpec(
-                        num_scalar_prefetch=1, grid=(count,),
-                        in_specs=[pl.BlockSpec((CH, d), lambda i, c: (c[0] * per_core + first + i, 0)),
-                                  pl.BlockSpec((CH, 2 * half), lambda i, c: (first + i, 0))] + [VM] * 8
-                        + ([] if out is None else [HB]) + ([] if got is None else [VM]),
-                        out_specs=[HB, VM],
-                        scratch_shapes=[pltpu.VMEM((CH, 2 * half), BF16), pltpu.VMEM((CH, 2 * half), BF16), pltpu.VMEM((CH, 2 * half), F32),
-                                        pltpu.SemaphoreType.DMA, pltpu.SemaphoreType.DMA]),
-                    out_shape=[jax.ShapeDtypeStruct((vocab_loc, d), F32), jax.ShapeDtypeStruct((count * CH, d), F32)],
-                    input_output_aliases={} if out is None else {11: 0},
-                    compiler_params=params(14),
+                    functools.partial(grad_kernel, first, count, prev, late, inv_n),
+                    in_specs=[pl.BlockSpec(memory_space=pltpu.SMEM), HB, HB] + [VM] * 9 + specs,
+                    out_specs=[HB, VM, VM, VM, VM],
+                    scratch_shapes=[pltpu.VMEM((CH, 2 * half), BF16), pltpu.VMEM((CH, 2 * half), BF16), pltpu.VMEM((CH, 2 * half), F32)]
+                    + [pltpu.SemaphoreType.DMA] * 4,
+                    out_shape=[jax.ShapeDtypeStruct((vocab_loc, d), F32), jax.ShapeDtypeStruct((2, CH, d), BF16),
+                               jax.ShapeDtypeStruct((2, CH, 2 * half), F32), pltpu.VMEM((count * CH, d), F32),
+                               jax.ShapeDtypeStruct((8, 128), F32)],
+                    input_output_aliases={} if out is None else {12: 0, 13: 1, 14: 2},
+                    compiler_params=params(10),
                     cost_estimate=cost(flops_unit * count * 6, count * CH * (2 * d + 8 * half + 8 * d)),
-                )(core_arg, emb_loc, logits, ha, hb, hc, hd, row_near, row_far, tgt_near, tgt_far, *extra)
-
-            out, first, arrived = None, 0, []
+                )(core_arg, emb_loc, logits, ha, hb, hc, hd, row_near, row_far, tgt_near, tgt_far, mark, *extra)
+
+            out, bufs, first, own, prev, arrived = None, (), 0, None, None, []
+            mark = jnp.zeros((8, 128), F32)
             for k, count in enumerate(PIECES):
                 late, got = arrived[k - 2] if k >= 2 else (None, None)
-                out, piece = piece_call(first, count, out, late, got)
-                arrived.append(((first, count), lax.ppermute(piece, 'dp', swap)))
+                out, *bufs, piece, mark = piece_call(first, count, mark, out, bufs, prev, own, late, got)
+                own, prev = piece, (first, count)
+                arrived.append((prev, lax.ppermute(piece, 'dp', swap)))
                 first += count
+                if k == 0:
+                    dh_got, loss_far, mark = tie((dh_got, loss_far, mark))
+                    dh_chip, mark = tie((dh_own + dh_got, mark))
+                    dh_far = lax.ppermute(dh_chip, 'tp', flip)
+                if k == 4:
+                    dh_far, mark = tie((dh_far, mark))
+                    grad_h = dh_chip + dh_far
+                    grad_scaled = grad_h * norm_vec
+                    grad_r = inv_rms * (grad_scaled - scaled * jnp.mean(grad_scaled * scaled, axis=-1, keepdims=True))
+                    grad_w = jnp.sum(grad_h * scaled, axis=0, keepdims=True)
+                    grad_r, grad_w, mark = tie((grad_r, grad_w, mark))
+                    grad_w_got = lax.ppermute(grad_w, 'dp', swap)
+                if k == 5:
+                    grad_w_got, mark = tie((grad_w_got, mark))
+                    grad_w, mark = tie((grad_w + grad_w_got, mark))
+                    grad_w_got = lax.ppermute(grad_w, 'dp', cross)
+            loss_mean = ((loss_chip + loss_far) * inv_n)[0, 0]
+            grad_w = (grad_w + grad_w_got).reshape(d)
 
             out = pl.pallas_call(
                 functools.partial(tail_kernel, inv_n),
@@ -320,16 +360,16 @@
                 compiler_params=params(14),
                 cost_estimate=cost(2.0 * TAIL * d * half * 8, 4 * TAIL * d),
             )(core_arg, emb_tail, ha, hb, hc, hd, row_near, row_far, tgt_near, tgt_far, out)
-            for late, got in arrived[-2:]:
+            for parts in ([(False, prev, own), (True, *arrived[-2])], [(True, *arrived[-1])]):
                 out = pl.pallas_call(
-                    functools.partial(last_kernel, late),
-                    grid_spec=pltpu.PrefetchScalarGridSpec(
-                        num_scalar_prefetch=1, grid=(1,), in_specs=[HB, VM], out_specs=HB, scratch_shapes=[pltpu.SemaphoreType.DMA]),
+                    functools.partial(last_kernel, [p[:2] for p in parts]),
+                    in_specs=[pl.BlockSpec(memory_space=pltpu.SMEM), HB] + [VM] * len(parts), out_specs=HB,
+                    scratch_shapes=[pltpu.SemaphoreType.DMA] * len(parts),
                     out_shape=jax.ShapeDtypeStruct((vocab_loc, d), F32),
                     input_output_aliases={1: 0},
-                    compiler_params=params(14),
-                    cost_estimate=cost(1e6, 4 * late[1] * CH * d),
-                )(core_arg, out, got)
+                    compiler_params=params(8),
+                    cost_estimate=cost(1e6, sum(4 * p[1][1] * CH * d for p in parts)),
+                )(core_arg, out, *[p[2] for p in parts])
             return loss_mean, grad_r.reshape(n_batch, n_seq, d), out, grad_w
 
         sharded = jax.shard_map(

time: 319 us -> 290 us (0.909)
  Pallas kernels: 224 us -> 201 us
  other arithmetic: 18 us -> 12.3 us
    pallas_call x9 -> x13, Pallas kernels: 141 us -> 117 us  [the longest x11 114 us: piece_call(): pl.pallas_call(functools.partial(grad_kernel, first, count, prev, late, i...]
    reshape x1 -> x0, other arithmetic: 4.6 us -> none  [local_part(): return (loss_mean, grad_r.reshape(n_batch, n_seq, d), out, grad_w)]
    reduce_sum x1, other arithmetic: 4.54 us -> 0.69 us  [local_part(): grad_w = jnp.sum(grad_h * scaled, axis=0, keepdims=True)]
    ppermute x13 -> x17, starting transfers between devices: 5.5 us -> 9.06 us  [the longest x1 2.61 us: local_part(): tgt_raw_far = lax.ppermute(tgt_raw, 'dp', cross)]
    ppermute x13 -> x17, waiting for transfers between devices: 53.7 us -> 54.2 us  [the longest x1 34.8 us: local_part(): dh_far = lax.ppermute(dh_chip, 'tp', flip)]
  transfers between devices with their start and end apart: 21 -> 25, of which waited for: 8 -> 8; matrix products, arithmetic and copies ran while one was open for 3% -> 3% of each run, Pallas kernels for 63% -> 65%
where the time goes in v3:
time: 290 us; the launch traced here: 289 us
  Pallas kernels  201 us (69%)
  waiting for transfers between devices  58.6 us (20%)
  starting transfers between devices  15.3 us (5%)
  other arithmetic  12.3 us (4%)
    pallas_call x11, Pallas kernels, piece_call(): pl.pallas_call(functools.partial(grad_kernel, first, count, prev, late, i...  114 us
    pallas_call x1, Pallas kernels, local_part(): pl.pallas_call(functools.partial(stats_kernel, tail_rows), grid_spec=pltp...  43.6 us
    pallas_call x1, Pallas kernels, local_part(): pl.pallas_call(functools.partial(dh_kernel, tail_rows, inv_n), grid_spec=...  36.6 us
    ppermute x1, waiting for transfers between devices, local_part(): dh_far = lax.ppermute(dh_chip, 'tp', flip)  34.8 us
    ppermute x1, waiting for transfers between devices, local_part(): grad_w_got = lax.ppermute(grad_w, 'dp', swap)  8.15 us
    ppermute x1, waiting for transfers between devices, local_part(): dh_got = lax.ppermute(dh_sib, 'dp', swap)  7.53 us
  transfers between devices with their start and end apart: 25, of which 8 were waited for; matrix products, arithmetic and copies ran while one was open for 3% of the time, Pallas kernels for 65%

profile of v3, /device:TPU:0, one launch (start us, length us, event | category | flops | bytes accessed | tf_op | source)
XLA Modules:
  0.0 289.4 jit_solution(1354748097458459403)
XLA Ops:
  0.7 2.4 fusion
  4.9 2.5 collective-permute-start.5
  8.9 1.8 multiply_convert_fusion.2.hb_ref
  10.7 43.6 %shard_map.84 = (f32[12544,1024]{1,0:T(8,128)}, f32[64,1024]{1,0:T(8,128)S(1)}, f32[8,1024]{1,0:T(8,128)S(1)}) custom-call(s32[1]{0:T(128)} %bitcast.core_ref, bf16[25140,1024]{1,0:T(8,128)(2,1)} %emb_ref.25, bf16[64,1024]{1,0:T(8,128)(2,1)S(1)} %pad.15.tail_ref, bf16[512,1024]{1,0:T(8,128)(2,1)S(1)} %get-tuple-element.173.ha_ref, ...), custom_call_target="tpu_custom_call" | custom-call | flops 26306674688 | bytes 77070336 | tf_op jit(solution)/shard_map/pallas_call | solution.py:257
  54.7 2.6 collective-permute-start.6
  59.0 1.4 collective-permute-done.4
  60.5 1.8 collective-permute-done.3
  63.0 36.6 %shard_map.85 = (f32[512,1024]{1,0:T(8,128)S(1)}, f32[512,1024]{1,0:T(8,128)S(1)}, f32[8,128]{1,0:T(8,128)S(1)}) custom-call(s32[1]{0:T(128)} %bitcast.core_ref, bf16[25140,1024]{1,0:T(8,128)(2,1)} %emb_ref.25, f32[12544,1024]{1,0:T(8,128)} %get-tuple-element.86.log_ref, bf16[64,1024]{1,0:T(8,128)(2,1)S(1)} %pad.15.tail_ref, ...), custom_call_target="tpu_custom_call" | custom-call | flops 26306674688 | bytes 77070336 | tf_op jit(solution)/shard_map/pallas_call | solution.py:288
  99.7 2.1 multiply_convert_fusion
  101.9 11.6 %shard_map.86 = (f32[25140,1024]{1,0:T(8,128)}, bf16[2,256,1024]{2,1,0:T(8,128)(2,1)S(1)}, f32[2,256,1024]{2,1,0:T(8,128)S(1)}, f32[1280,1024]{1,0:T(8,128)S(1)}, f32[8,128]{1,0:T(8,128)S(1)}) custom-call(s32[1]{0:T(128)} %bitcast.core_ref, bf16[25140,1024]{1,0:T(8,128)(2,1)} %emb_ref.25, f32[12544,1024]{1,0:T(8,128)} %get-tuple-element.86.log_ref, ...), custom_call_target="tpu_custom_call" | custom-call | flops 8053063680 | bytes 18350080 | tf_op jit(solution)/shard_map/pallas_call | solution.py:311
  114.0 1.5 collective-permute-start.10
  115.5 2.1 collective-permute-done.10
  117.6 7.5 %collective-permute-done.9 = f32[512,1024]{1,0:T(8,128)S(1)} collective-permute-done((f32[512,1024]{1,0:T(8,128)S(1)}, f32[512,1024]{1,0:T(8,128)S(1)}, u32[]{:S(2)}, u32[]{:S(2)}) %collective-permute-start.9) | collective-permute-done | bytes 2097184 | tf_op jit(solution)/shard_map/ppermute | solution.py:305
  125.1 1.7 add.89
  126.9 10.7 %shard_map.87 = (f32[25140,1024]{1,0:T(8,128)}, bf16[2,256,1024]{2,1,0:T(8,128)(2,1)S(1)}, f32[2,256,1024]{2,1,0:T(8,128)S(1)}, f32[1280,1024]{1,0:T(8,128)S(1)}, f32[8,128]{1,0:T(8,128)S(1)}) custom-call(s32[1]{0:T(128)} %bitcast.core_ref, bf16[25140,1024]{1,0:T(8,128)(2,1)} %emb_ref.25, ...), custom_call_target="tpu_custom_call", output_to_operand_aliasing={{0}: (12, {}), {1}: (13, {}), {2}: (14, {})} | custom-call | flops 8053063680 | bytes 18350080 | tf_op jit(solution)/shard_map/pallas_call | solution.py:311
  137.8 11.2 %shard_map.88 = (f32[25140,1024]{1,0:T(8,128)}, bf16[2,256,1024]{2,1,0:T(8,128)(2,1)S(1)}, f32[2,256,1024]{2,1,0:T(8,128)S(1)}, f32[1280,1024]{1,0:T(8,128)S(1)}, f32[8,128]{1,0:T(8,128)S(1)}) custom-call(s32[1]{0:T(128)} %bitcast.core_ref, bf16[25140,1024]{1,0:T(8,128)(2,1)} %emb_ref.25, ...), custom_call_target="tpu_custom_call", output_to_operand_aliasing={{0}: (12, {}), {1}: (13, {}), {2}: (14, {})} | custom-call | flops 8053063680 | bytes 18350080 | tf_op jit(solution)/shard_map/pallas_call | solution.py:311
  149.4 12.2 %shard_map.89 = (f32[25140,1024]{1,0:T(8,128)}, bf16[2,256,1024]{2,1,0:T(8,128)(2,1)S(1)}, f32[2,256,1024]{2,1,0:T(8,128)S(1)}, f32[1280,1024]{1,0:T(8,128)S(1)}, f32[8,128]{1,0:T(8,128)S(1)}) custom-call(s32[1]{0:T(128)} %bitcast.core_ref, bf16[25140,1024]{1,0:T(8,128)(2,1)} %emb_ref.25, ...), custom_call_target="tpu_custom_call", output_to_operand_aliasing={{0}: (12, {}), {1}: (13, {}), {2}: (14, {})} | custom-call | flops 8053063680 | bytes 18350080 | tf_op jit(solution)/shard_map/pallas_call | solution.py:311
  162.2 12.7 %shard_map.90 = (f32[25140,1024]{1,0:T(8,128)}, bf16[2,256,1024]{2,1,0:T(8,128)(2,1)S(1)}, f32[2,256,1024]{2,1,0:T(8,128)S(1)}, f32[1280,1024]{1,0:T(8,128)S(1)}, f32[8,128]{1,0:T(8,128)S(1)}) custom-call(s32[1]{0:T(128)} %bitcast.core_ref, bf16[25140,1024]{1,0:T(8,128)(2,1)} %emb_ref.25, ...), custom_call_target="tpu_custom_call", output_to_operand_aliasing={{0}: (12, {}), {1}: (13, {}), {2}: (14, {})} | custom-call | flops 8053063680 | bytes 18350080 | tf_op jit(solution)/shard_map/pallas_call | solution.py:311
  174.9 34.8 %collective-permute-done.11 = f32[512,1024]{1,0:T(8,128)S(1)} collective-permute-done((f32[512,1024]{1,0:T(8,128)S(1)}, f32[512,1024]{1,0:T(8,128)S(1)}, u32[]{:S(2)}, u32[]{:S(2)}) %collective-permute-start.11) | collective-permute-done | bytes 2097184 | tf_op jit(solution)/shard_map/ppermute | solution.py:336
  210.4 1.8 subtract_multiply_fusion
  212.2 11.2 %shard_map.91 = (f32[25140,1024]{1,0:T(8,128)}, bf16[2,256,1024]{2,1,0:T(8,128)(2,1)S(1)}, f32[2,256,1024]{2,1,0:T(8,128)S(1)}, f32[1280,1024]{1,0:T(8,128)S(1)}, f32[8,128]{1,0:T(8,128)S(1)}) custom-call(s32[1]{0:T(128)} %bitcast.core_ref, bf16[25140,1024]{1,0:T(8,128)(2,1)} %emb_ref.25, ...), custom_call_target="tpu_custom_call", output_to_operand_aliasing={{0}: (12, {}), {1}: (13, {}), {2}: (14, {})} | custom-call | flops 8053063680 | bytes 18350080 | tf_op jit(solution)/shard_map/pallas_call | solution.py:311
  224.0 8.2 %collective-permute-done.15 = f32[1,1024]{1,0:T(1,128)S(1)} collective-permute-done((f32[1,1024]{1,0:T(1,128)S(1)}, f32[1,1024]{1,0:T(1,128)S(1)}, u32[]{:S(2)}, u32[]{:S(2)}) %collective-permute-start.15) | collective-permute-done | bytes 4128 | tf_op jit(solution)/shard_map/ppermute | solution.py:344
  232.7 11.2 %shard_map.92 = (f32[25140,1024]{1,0:T(8,128)}, bf16[2,256,1024]{2,1,0:T(8,128)(2,1)S(1)}, f32[2,256,1024]{2,1,0:T(8,128)S(1)}, f32[1280,1024]{1,0:T(8,128)S(1)}, f32[8,128]{1,0:T(8,128)S(1)}) custom-call(s32[1]{0:T(128)} %bitcast.core_ref, bf16[25140,1024]{1,0:T(8,128)(2,1)} %emb_ref.25, ...), custom_call_target="tpu_custom_call", output_to_operand_aliasing={{0}: (12, {}), {1}: (13, {}), {2}: (14, {})} | custom-call | flops 8053063680 | bytes 18350080 | tf_op jit(solution)/shard_map/pallas_call | solution.py:311
  244.1 11.2 %shard_map.93 = (f32[25140,1024]{1,0:T(8,128)}, bf16[2,256,1024]{2,1,0:T(8,128)(2,1)S(1)}, f32[2,256,1024]{2,1,0:T(8,128)S(1)}, f32[1280,1024]{1,0:T(8,128)S(1)}, f32[8,128]{1,0:T(8,128)S(1)}) custom-call(s32[1]{0:T(128)} %bitcast.core_ref, bf16[25140,1024]{1,0:T(8,128)(2,1)} %emb_ref.25, ...), custom_call_target="tpu_custom_call", output_to_operand_aliasing={{0}: (12, {}), {1}: (13, {}), {2}: (14, {})} | custom-call | flops 8053063680 | bytes 18350080 | tf_op jit(solution)/shard_map/pallas_call | solution.py:311
  255.7 9.2 %shard_map.94 = (f32[25140,1024]{1,0:T(8,128)}, bf16[2,256,1024]{2,1,0:T(8,128)(2,1)S(1)}, f32[2,256,1024]{2,1,0:T(8,128)S(1)}, f32[1024,1024]{1,0:T(8,128)S(1)}, f32[8,128]{1,0:T(8,128)S(1)}) custom-call(s32[1]{0:T(128)} %bitcast.core_ref, bf16[25140,1024]{1,0:T(8,128)(2,1)} %emb_ref.25, ...), custom_call_target="tpu_custom_call", output_to_operand_aliasing={{0}: (12, {}), {1}: (13, {}), {2}: (14, {})} | custom-call | flops 6442450944 | bytes 14680064 | tf_op jit(solution)/shard_map/pallas_call | solution.py:311
  265.1 7.1 %shard_map.95 = (f32[25140,1024]{1,0:T(8,128)}, bf16[2,256,1024]{2,1,0:T(8,128)(2,1)S(1)}, f32[2,256,1024]{2,1,0:T(8,128)S(1)}, f32[768,1024]{1,0:T(8,128)S(1)}, f32[8,128]{1,0:T(8,128)S(1)}) custom-call(s32[1]{0:T(128)} %bitcast.core_ref, bf16[25140,1024]{1,0:T(8,128)(2,1)} %emb_ref.25, ...), custom_call_target="tpu_custom_call", output_to_operand_aliasing={{0}: (12, {}), {1}: (13, {}), {2}: (14, {})} | custom-call | flops 4831838208 | bytes 11010048 | tf_op jit(solution)/shard_map/pallas_call | solution.py:311
  272.7 5.4 %shard_map.96 = (f32[25140,1024]{1,0:T(8,128)}, bf16[2,256,1024]{2,1,0:T(8,128)(2,1)S(1)}, f32[2,256,1024]{2,1,0:T(8,128)S(1)}, f32[512,1024]{1,0:T(8,128)S(1)}, f32[8,128]{1,0:T(8,128)}) custom-call(s32[1]{0:T(128)} %bitcast.core_ref, bf16[25140,1024]{1,0:T(8,128)(2,1)} %emb_ref.25, ...), custom_call_target="tpu_custom_call", output_to_operand_aliasing={{0}: (12, {}), {1}: (13, {}), {2}: (14, {})} | custom-call | flops 3221225472 | bytes 7340032 | tf_op jit(solution)/shard_map/pallas_call | solution.py:311
  278.2 1.5 collective-permute-start.24
  280.2 1.6 collective-permute-done.24
  282.4 3.1 %shard_map.97._ = f32[25140,1024]{1,0:T(8,128)} custom-call(s32[1]{0:T(128)} %bitcast.core_ref, bf16[64,1024]{1,0:T(8,128)(2,1)S(1)} %copy-done.1, bf16[512,1024]{1,0:T(8,128)(2,1)S(1)} %get-tuple-element.173.ha_ref, bf16[512,1024]{1,0:T(8,128)(2,1)S(1)} %multiply_convert_fusion.2.hb_ref, ...), custom_call_target="tpu_custom_call", output_to_operand_aliasing={{}: (10, {})} | custom-call | flops 536870912 | bytes 262144 | tf_op jit(solution)/shard_map/pallas_call | solution.py:352
  285.5 2.4 shard_map.98._
  287.9 1.3 shard_map.99
  (99 shorter events, 12.2 us)
Async XLA Ops:
  4.0 50.3 %copy-start.4 = (f32[512,1024]{1,0:T(8,128)}, f32[512,1024]{1,0:T(8,128)S(1)}, u32[]{:S(2)}) copy-start(f32[512,1024]{1,0:T(8,128)S(1)} %get-tuple-element.174) | copy-start | bytes 6291460
  4.0 4.8 %collective-permute-start = (f32[512,1024]{1,0:T(8,128)S(1)}, f32[512,1024]{1,0:T(8,128)}, u32[]{:S(2)}, u32[]{:S(2)}) collective-permute-start(f32[512,1024]{1,0:T(8,128)S(1)} %get-tuple-element.174), channel_id=1, source_target_pairs={{0,1},{1,0},{2,3},{3,2},{4,5},{5,4},{6,7},{7,6}} | collective-permute-start | bytes 6291464 | tf_op jit(solution)/shard_map/ppermute | solution.py:240
  4.9 57.5 %collective-permute-start.5 = (f32[512,1024]{1,0:T(8,128)S(1)}, f32[512,1024]{1,0:T(8,128)}, u32[]{:S(2)}, u32[]{:S(2)}) collective-permute-start(f32[512,1024]{1,0:T(8,128)S(1)} %get-tuple-element.174), channel_id=1, source_target_pairs={{0,2},{1,3},{2,0},{3,1},{4,6},{5,7},{6,4},{7,5}} | collective-permute-start | bytes 6291464 | tf_op jit(solution)/shard_map/ppermute | solution.py:242
  7.4 1.4 collective-permute-start.1
  7.6 55.4 %copy-start = (bf16[64,1024]{1,0:T(8,128)(2,1)}, bf16[64,1024]{1,0:T(8,128)(2,1)S(1)}, u32[]{:S(2)}) copy-start(bf16[64,1024]{1,0:T(8,128)(2,1)S(1)} %pad.15.tail_ref) | copy-start | bytes 393220
  54.3 4.7 %collective-permute-start.2 = (f32[3,1024]{1,0:T(4,128)S(1)}, f32[3,1024]{1,0:T(4,128)S(1)}, u32[]{:S(2)}, u32[]{:S(2)}) collective-permute-start(f32[3,1024]{1,0:T(4,128)S(1)} %slice.66), channel_id=1, source_target_pairs={{0,1},{1,0},{2,3},{3,2},{4,5},{5,4},{6,7},{7,6}} | collective-permute-start | bytes 36872 | tf_op jit(solution)/shard_map/ppermute | solution.py:274
  54.7 7.7 %collective-permute-start.6 = (s32[1,1024]{1,0:T(1,128)S(1)}, s32[1,1024]{1,0:T(1,128)S(1)}, u32[]{:S(2)}, u32[]{:S(2)}) collective-permute-start(s32[1,1024]{1,0:T(1,128)S(1)} %constant_dynamic-update-slice_fusion), channel_id=1, source_target_pairs={{0,2},{1,3},{2,0},{3,1},{4,6},{5,7},{6,4},{7,5}} | collective-permute-start | bytes 12296 | tf_op jit(solution)/shard_map/ppermute | solution.py:252
  57.3 3.2 %collective-permute-start.4 = (f32[3,1024]{1,0:T(4,128)S(1)}, f32[3,1024]{1,0:T(4,128)S(1)}, u32[]{:S(2)}, u32[]{:S(2)}) collective-permute-start(f32[3,1024]{1,0:T(4,128)S(1)} %slice.66), channel_id=1, source_target_pairs={{0,5},{1,4},{2,7},{3,6},{4,1},{5,0},{6,3},{7,2}} | collective-permute-start | bytes 36872 | tf_op jit(solution)/shard_map/ppermute | solution.py:276
  58.5 3.7 %collective-permute-start.3 = (f32[3,1024]{1,0:T(4,128)S(1)}, f32[3,1024]{1,0:T(4,128)S(1)}, u32[]{:S(2)}, u32[]{:S(2)}) collective-permute-start(f32[3,1024]{1,0:T(4,128)S(1)} %slice.66), channel_id=1, source_target_pairs={{0,4},{4,0},{1,5},{5,1},{2,6},{6,2},{3,7},{7,3}} | collective-permute-start | bytes 36872 | tf_op jit(solution)/shard_map/ppermute | solution.py:275
  62.4 37.3 %collective-permute-start.8 = (f32[512,1024]{1,0:T(8,128)}, f32[512,1024]{1,0:T(8,128)S(1)}, u32[]{:S(2)}, u32[]{:S(2)}) collective-permute-start(f32[512,1024]{1,0:T(8,128)} %collective-permute-done.5), channel_id=1, source_target_pairs={{0,1},{1,0},{2,3},{3,2},{4,5},{5,4},{6,7},{7,6}} | collective-permute-start | bytes 6291464 | tf_op jit(solution)/shard_map/ppermute | solution.py:285
  62.4 37.2 %collective-permute-start.7 = (f32[8,1024]{1,0:T(8,128)S(1)}, f32[8,1024]{1,0:T(8,128)S(1)}, u32[]{:S(2)}, u32[]{:S(2)}) collective-permute-start(f32[8,1024]{1,0:T(8,128)S(1)} %select_maximum_fusion.row_ref), channel_id=1, source_target_pairs={{0,2},{1,3},{2,0},{3,1},{4,6},{5,7},{6,4},{7,5}} | collective-permute-start | bytes 98312 | tf_op jit(solution)/shard_map/ppermute | solution.py:286
  99.6 14.4 %copy-start.2 = (f32[8,128]{1,0:T(8,128)}, f32[8,128]{1,0:T(8,128)S(1)}, u32[]{:S(2)}) copy-start(f32[8,128]{1,0:T(8,128)S(1)} %get-tuple-element.90) | copy-start | bytes 12292
  113.5 24.4 %collective-permute-start.12 = (f32[1280,1024]{1,0:T(8,128)S(1)}, f32[1280,1024]{1,0:T(8,128)S(1)}, u32[]{:S(2)}, u32[]{:S(2)}) collective-permute-start(f32[1280,1024]{1,0:T(8,128)S(1)} %get-tuple-element.111.refs_3_), channel_id=1, source_target_pairs={{0,1},{1,0},{2,3},{3,2},{4,5},{5,4},{6,7},{7,6}} | collective-permute-start | bytes 15728648 | tf_op jit(solution)/shard_map/ppermute | solution.py:331
  113.7 11.5 %collective-permute-start.9 = (f32[512,1024]{1,0:T(8,128)S(1)}, f32[512,1024]{1,0:T(8,128)S(1)}, u32[]{:S(2)}, u32[]{:S(2)}) collective-permute-start(f32[512,1024]{1,0:T(8,128)S(1)} %get-tuple-element.95), channel_id=1, source_target_pairs={{0,1},{1,0},{2,3},{3,2},{4,5},{5,4},{6,7},{7,6}} | collective-permute-start | bytes 6291464 | tf_op jit(solution)/shard_map/ppermute | solution.py:305
  114.0 3.6 %collective-permute-start.10 = (f32[8,128]{1,0:T(8,128)S(1)}, f32[8,128]{1,0:T(8,128)S(1)}, u32[]{:S(2)}, u32[]{:S(2)}) collective-permute-start(f32[8,128]{1,0:T(8,128)S(1)} %get-tuple-element.90), channel_id=1, source_target_pairs={{0,2},{1,3},{2,0},{3,1},{4,6},{5,7},{6,4},{7,5}} | collective-permute-start | bytes 12296 | tf_op jit(solution)/shard_map/ppermute | solution.py:306
  137.6 11.8 %collective-permute-start.13 = (f32[1280,1024]{1,0:T(8,128)S(1)}, f32[1280,1024]{1,0:T(8,128)S(1)}, u32[]{:S(2)}, u32[]{:S(2)}) collective-permute-start(f32[1280,1024]{1,0:T(8,128)S(1)} %get-tuple-element.116.refs_3_), channel_id=1, source_target_pairs={{0,1},{1,0},{2,3},{3,2},{4,5},{5,4},{6,7},{7,6}} | collective-permute-start | bytes 15728648 | tf_op jit(solution)/shard_map/ppermute | solution.py:331
  149.0 13.2 %collective-permute-start.14 = (f32[1280,1024]{1,0:T(8,128)S(1)}, f32[1280,1024]{1,0:T(8,128)S(1)}, u32[]{:S(2)}, u32[]{:S(2)}) collective-permute-start(f32[1280,1024]{1,0:T(8,128)S(1)} %get-tuple-element.121.refs_3_), channel_id=1, source_target_pairs={{0,1},{1,0},{2,3},{3,2},{4,5},{5,4},{6,7},{7,6}} | collective-permute-start | bytes 15728648 | tf_op jit(solution)/shard_map/ppermute | solution.py:331
  149.4 12.5 %copy-start.6 = (f32[512,1024]{1,0:T(8,128)S(1)}, f32[512,1024]{1,0:T(8,128)}, u32[]{:S(2)}) copy-start(f32[512,1024]{1,0:T(8,128)} %add.89) | copy-start | bytes 6291460
  161.6 50.6 %collective-permute-start.16 = (f32[1280,1024]{1,0:T(8,128)S(1)}, f32[1280,1024]{1,0:T(8,128)S(1)}, u32[]{:S(2)}, u32[]{:S(2)}) collective-permute-start(f32[1280,1024]{1,0:T(8,128)S(1)} %get-tuple-element.126.refs_3_), channel_id=1, source_target_pairs={{0,1},{1,0},{2,3},{3,2},{4,5},{5,4},{6,7},{7,6}} | collective-permute-start | bytes 15728648 | tf_op jit(solution)/shard_map/ppermute | solution.py:331
  161.9 47.8 %collective-permute-start.11 = (f32[512,1024]{1,0:T(8,128)S(1)}, f32[512,1024]{1,0:T(8,128)S(1)}, u32[]{:S(2)}, u32[]{:S(2)}) collective-permute-start(f32[512,1024]{1,0:T(8,128)S(1)} %copy-done.6), channel_id=1, source_target_pairs={{0,4},{4,0},{1,5},{5,1},{2,6},{6,2},{3,7},{7,3}} | collective-permute-start | bytes 6291464 | tf_op jit(solution)/shard_map/ppermute | solution.py:336
  162.2 47.5 %copy-start.5 = (f32[512,1024]{1,0:T(8,128)S(1)}, f32[512,1024]{1,0:T(8,128)}, u32[]{:S(2)}) copy-start(f32[512,1024]{1,0:T(8,128)} %copy-done.4) | copy-start | bytes 6291460
  162.2 47.5 %copy-start.10 = (f32[1024]{0:T(1024)S(1)}, f32[1024]{0:T(1024)}, u32[]{:S(2)}) copy-start(f32[1024]{0:T(1024)} %param.9) | copy-start | bytes 12292
  174.9 57.9 %collective-permute-start.17 = (f32[1280,1024]{1,0:T(8,128)S(1)}, f32[1280,1024]{1,0:T(8,128)S(1)}, u32[]{:S(2)}, u32[]{:S(2)}) collective-permute-start(f32[1280,1024]{1,0:T(8,128)S(1)} %get-tuple-element.136.refs_3_), channel_id=1, source_target_pairs={{0,1},{1,0},{2,3},{3,2},{4,5},{5,4},{6,7},{7,6}} | collective-permute-start | bytes 15728648 | tf_op jit(solution)/shard_map/ppermute | solution.py:331
  223.4 20.7 %collective-permute-start.18 = (f32[1280,1024]{1,0:T(8,128)S(1)}, f32[1280,1024]{1,0:T(8,128)S(1)}, u32[]{:S(2)}, u32[]{:S(2)}) collective-permute-start(f32[1280,1024]{1,0:T(8,128)S(1)} %get-tuple-element.144.refs_3_), channel_id=1, source_target_pairs={{0,1},{1,0},{2,3},{3,2},{4,5},{5,4},{6,7},{7,6}} | collective-permute-start | bytes 15728648 | tf_op jit(solution)/shard_map/ppermute | solution.py:331
  223.5 8.7 %collective-permute-start.15 = (f32[1,1024]{1,0:T(1,128)S(1)}, f32[1,1024]{1,0:T(1,128)S(1)}, u32[]{:S(2)}, u32[]{:S(2)}) collective-permute-start(f32[1,1024]{1,0:T(1,128)S(1)} %bitcast.12), channel_id=1, source_target_pairs={{0,1},{1,0},{2,3},{3,2},{4,5},{5,4},{6,7},{7,6}} | collective-permute-start | bytes 12296 | tf_op jit(solution)/shard_map/ppermute | solution.py:344
  244.0 11.8 %collective-permute-start.19 = (f32[1280,1024]{1,0:T(8,128)S(1)}, f32[1280,1024]{1,0:T(8,128)S(1)}, u32[]{:S(2)}, u32[]{:S(2)}) collective-permute-start(f32[1280,1024]{1,0:T(8,128)S(1)} %get-tuple-element.149.refs_3_), channel_id=1, source_target_pairs={{0,1},{1,0},{2,3},{3,2},{4,5},{5,4},{6,7},{7,6}} | collective-permute-start | bytes 15728648 | tf_op jit(solution)/shard_map/ppermute | solution.py:331
  255.4 9.8 %collective-permute-start.20 = (f32[1280,1024]{1,0:T(8,128)S(1)}, f32[1280,1024]{1,0:T(8,128)S(1)}, u32[]{:S(2)}, u32[]{:S(2)}) collective-permute-start(f32[1280,1024]{1,0:T(8,128)S(1)} %get-tuple-element.154.refs_3_), channel_id=1, source_target_pairs={{0,1},{1,0},{2,3},{3,2},{4,5},{5,4},{6,7},{7,6}} | collective-permute-start | bytes 15728648 | tf_op jit(solution)/shard_map/ppermute | solution.py:331
  265.0 7.7 %collective-permute-start.21 = (f32[1024,1024]{1,0:T(8,128)S(1)}, f32[1024,1024]{1,0:T(8,128)S(1)}, u32[]{:S(2)}, u32[]{:S(2)}) collective-permute-start(f32[1024,1024]{1,0:T(8,128)S(1)} %get-tuple-element.159.refs_3_), channel_id=1, source_target_pairs={{0,1},{1,0},{2,3},{3,2},{4,5},{5,4},{6,7},{7,6}} | collective-permute-start | bytes 12582920 | tf_op jit(solution)/shard_map/ppermute | solution.py:331
  272.3 13.3 %collective-permute-start.22 = (f32[768,1024]{1,0:T(8,128)S(1)}, f32[768,1024]{1,0:T(8,128)S(1)}, u32[]{:S(2)}, u32[]{:S(2)}) collective-permute-start(f32[768,1024]{1,0:T(8,128)S(1)} %get-tuple-element.164.refs_3_), channel_id=1, source_target_pairs={{0,1},{1,0},{2,3},{3,2},{4,5},{5,4},{6,7},{7,6}} | collective-permute-start | bytes 9437192 | tf_op jit(solution)/shard_map/ppermute | solution.py:331
  272.7 9.8 %copy-start.1 = (bf16[64,1024]{1,0:T(8,128)(2,1)S(1)}, bf16[64,1024]{1,0:T(8,128)(2,1)}, u32[]{:S(2)}) copy-start(bf16[64,1024]{1,0:T(8,128)(2,1)} %copy-done) | copy-start | bytes 393220
  278.0 9.9 %collective-permute-start.23 = (f32[512,1024]{1,0:T(8,128)S(1)}, f32[512,1024]{1,0:T(8,128)S(1)}, u32[]{:S(2)}, u32[]{:S(2)}) collective-permute-start(f32[512,1024]{1,0:T(8,128)S(1)} %get-tuple-element.166.refs_0_), channel_id=1, source_target_pairs={{0,1},{1,0},{2,3},{3,2},{4,5},{5,4},{6,7},{7,6}} | collective-permute-start | bytes 6291464 | tf_op jit(solution)/shard_map/ppermute | solution.py:331
  278.2 3.6 %collective-permute-start.24 = (f32[1,1024]{1,0:T(1,128)S(1)}, f32[1,1024]{1,0:T(1,128)S(1)}, u32[]{:S(2)}, u32[]{:S(2)}) collective-permute-start(f32[1,1024]{1,0:T(1,128)S(1)} %copy-done.13), channel_id=1, source_target_pairs={{0,2},{1,3},{2,0},{3,1},{4,6},{5,7},{6,4},{7,5}} | collective-permute-start | bytes 12296 | tf_op jit(solution)/shard_map/ppermute | solution.py:348
  (11 other events, 46.2 us)

commit v4 on v3

v4 whole, which is shorter than its diff:
```python
import functools

import jax
import jax.numpy as jnp
from jax import lax
from jax.experimental import pallas as pl
from jax.experimental.pallas import tpu as pltpu
from jax.sharding import PartitionSpec as P


NORM_EPS = 1e-5
CH = 256
STEP = 7
GROUPS = (1, 2, 2, 2)
PIECES = (6, 6, 6, 5, 5, 5, 5, 5, 4, 2)
ADD_AT, FINISH_AT = 1, 5
TAIL = 64
F32, BF16 = jnp.float32, jnp.bfloat16
NN = (((1,), (0,)), ((), ()))
NT = (((1,), (1,)), ((), ()))
TN = (((0,), (0,)), ((), ()))
VM = pl.BlockSpec(memory_space=pltpu.VMEM)
HB = pl.BlockSpec(memory_space=pl.ANY)


def dot(a, b, dims):
    return lax.dot_general(a, b, dims, preferred_element_type=F32)


LOG2E = 1.4426950408889634


def weights(logit, shift, hit, inv_n):
    return (jnp.exp2(logit * LOG2E + shift) - jnp.where(hit, inv_n, 0.0)).astype(BF16)


def rows_of(n, width, base):
    return lax.broadcasted_iota(jnp.int32, (n, width), 0) + base


def norm_kernel(hid_ref, res_ref, norm_ref, scaled_ref, act_ref, inv_ref):
    resid = res_ref[...] + hid_ref[...].astype(F32)
    inv = lax.rsqrt(jnp.mean(resid * resid, axis=-1, keepdims=True) + NORM_EPS)
    scaled = resid * inv
    scaled_ref[...] = scaled
    act_ref[...] = (scaled * norm_ref[...]).astype(BF16)
    inv_ref[...] = jnp.broadcast_to(inv, inv_ref.shape)


def stats_kernel(tail_rows, core_ref, emb_ref, tail_ref, ha_ref, sib_ref, norm_ref, tgt_ref, log_ref, logt_ref, stat_ref, hb_ref, top, total, hits):
    step, core = pl.program_id(0), core_ref[0]
    half = ha_ref.shape[0]

    @pl.when(step == 0)
    def _():
        top[...] = jnp.full_like(top, -jnp.inf)
        total[...] = jnp.zeros_like(total)
        hits[...] = jnp.zeros_like(hits)
        hb_ref[...] = (sib_ref[...] * norm_ref[...]).astype(BF16)

    def fold(cols, logit, hit):
        split = logit.reshape(-1, 8, half)
        new = jnp.maximum(top[:, cols], jnp.max(split, axis=0))
        total[:, cols] = total[:, cols] * jnp.exp(top[:, cols] - new) + jnp.sum(jnp.exp(split - new[None]), axis=0)
        top[:, cols] = new
        hits[:, cols] += jnp.sum(jnp.where(hit, logit, 0.0).reshape(-1, 8, half), axis=0)

    for k in range(STEP):
        rows = pl.ds(k * CH, CH)
        for side, h_ref in ((0, ha_ref), (1, hb_ref)):
            cols = pl.ds(side * half, half)
            logit = dot(emb_ref[rows, :], h_ref[...], NT)
            log_ref[rows, cols] = logit
            want = tgt_ref[0:1, cols] - (core_ref[1] + (step * STEP + k) * CH)
            fold(cols, logit, rows_of(CH, half, 0) == want)

    @pl.when(step == pl.num_programs(0) - 1)
    def _():
        for side, h_ref in ((0, ha_ref), (1, hb_ref)):
            cols = pl.ds(side * half, half)
            ids = rows_of(TAIL, half, 0)
            live = jnp.logical_and(ids < tail_rows, core == 0)
            logit = jnp.where(live, dot(tail_ref[...], h_ref[...], NT), -jnp.inf)
            logt_ref[:, cols] = logit
            fold(cols, logit, jnp.logical_and(ids + core_ref[2] == tgt_ref[0:1, cols], live))
        peak = jnp.max(top[...], axis=0, keepdims=True)
        stat_ref[...] = jnp.zeros_like(stat_ref)
        stat_ref[0:1, :] = peak
        stat_ref[1:2, :] = jnp.sum(total[...] * jnp.exp(top[...] - peak), axis=0, keepdims=True)
        stat_ref[2:3, :] = jnp.sum(hits[...], axis=0, keepdims=True)


def dh_kernel(tail_rows, inv_n, core_ref, emb_ref, log_ref, tail_ref, logt_ref, row_ref, tgt_ref, da_ref, db_ref, loss_ref, g_ref, gt_ref):
    step, core = pl.program_id(0), core_ref[0]
    half = da_ref.shape[0]

    @pl.when(step == 0)
    def _():
        loss_ref[...] = jnp.full(loss_ref.shape, jnp.sum(row_ref[1:2, pl.ds(0, half)]) + jnp.sum(row_ref[1:2, pl.ds(half, half)]))
        da_ref[...] = jnp.zeros_like(da_ref)
        db_ref[...] = jnp.zeros_like(db_ref)

    k = 0
    for group in GROUPS:
        for side, d_ref in ((0, da_ref), (1, db_ref)):
            cols = pl.ds(side * half, half)
            for i in range(k, k + group):
                rows = pl.ds(i * CH, CH)
                want = tgt_ref[0:1, cols] - (core_ref[1] + (step * STEP + i) * CH)
                g_ref[rows, cols] = weights(log_ref[rows, cols], row_ref[0:1, cols], rows_of(CH, half, 0) == want, inv_n)
            rows = pl.ds(k * CH, group * CH)
            d_ref[...] += dot(g_ref[rows, cols], emb_ref[rows, :], TN)
        k += group

    @pl.when(step == pl.num_programs(0) - 1)
    def _():
        for side, d_ref in ((0, da_ref), (1, db_ref)):
            cols = pl.ds(side * half, half)
            ids = rows_of(TAIL, half, 0)
            live = jnp.logical_and(ids < tail_rows, core == 0)
            hit = jnp.logical_and(ids + core_ref[2] == tgt_ref[0:1, cols], live)
            gt_ref[:, cols] = weights(logt_ref[:, cols], row_ref[0:1, cols], hit, inv_n)
            d_ref[...] += dot(gt_ref[:, cols], tail_ref[...], TN)


JOBS = {None: (0, 0), 'act': (3, 2), 'add': (2, 1)}


def finish_kernel(norm_ref, inv_ref, scaled_ref, near_ref, far_ref, grad_ref, sum_ref, total_ref):
    @pl.when(pl.program_id(0) == 0)
    def _():
        total_ref[...] = jnp.zeros_like(total_ref)

    grad_h, scaled = near_ref[...] + far_ref[...], scaled_ref[...]
    total_ref[...] += jnp.sum((grad_h * scaled).reshape(-1, 8, scaled.shape[1]), axis=0)
    grad_scaled = grad_h * norm_ref[...]
    mean = jnp.mean(grad_scaled * scaled, axis=-1, keepdims=True)
    grad_ref[...] = inv_ref[:, 0:1] * (grad_scaled - scaled * mean)
    sum_ref[...] = jnp.sum(total_ref[...], axis=0, keepdims=True)


def rows_at(core, first, count):
    return pl.ds(pl.multiple_of((core * sum(PIECES) + first) * CH, CH), count * CH)


def grad_kernel(job, first, count, prev, late, inv_n, core_ref, emb_ref, log_ref, ha_ref, hb_ref, hc_ref, hd_ref, row_ref, rowx_ref, mark_ref, *refs):
    per_core = sum(PIECES)
    refs = list(refs)
    if prev:
        refs = refs[3:]
    own_ref = refs.pop(0) if prev else None
    got_ref = refs.pop(0) if late else None
    jobs_in = [refs.pop(0) for _ in range(JOBS[job][0])]
    jobs_out = [refs.pop(5) for _ in range(JOBS[job][1])]
    out_ref, emb_buf, log_buf, piece_ref, token_ref, ga_ref, gx_ref, lx_ref, emb_sem, log_sem, own_sem, got_sem = refs
    core = core_ref[0]
    half = ha_ref.shape[0]
    token_ref[...] = mark_ref[...]

    def fetch(k):
        slot = lax.rem(k, 2)
        mine = pl.ds(pl.multiple_of(k * CH, CH), CH)
        return (pltpu.make_async_copy(emb_ref.at[rows_at(core, k, 1)], emb_buf.at[slot], emb_sem),
                pltpu.make_async_copy(log_ref.at[mine], log_buf.at[slot], log_sem))

    writes = []
    if prev:
        writes.append(pltpu.make_async_copy(own_ref, out_ref.at[rows_at(core, *prev)], own_sem))
    if late:
        writes.append(pltpu.make_async_copy(got_ref, out_ref.at[rows_at(1 - core, *late)], got_sem))
    if not prev:
        for copy in fetch(jnp.int32(first)):
            copy.start()
        for copy in fetch(jnp.int32(first)):
            copy.wait()
    for copy in writes:
        copy.start()
    if job == 'act':
        norm_ref, *src = jobs_in
        for src_ref, dst_ref in zip(src, jobs_out):
            dst_ref[...] = (src_ref[...] * norm_ref[...]).astype(BF16)
        hc_ref, hd_ref = jobs_out
    if job == 'add':
        jobs_out[0][...] = jobs_in[0][...] + jobs_in[1][...]

    def step(i, carry):
        k = first + i
        slot = lax.rem(k, 2)
        rows = pl.ds(pl.multiple_of(i * CH, CH), CH)
        more = k + 1 < per_core

        @pl.when(more)
        def _():
            for copy in fetch(k + 1):
                copy.start()

        base = core_ref[1] + k * CH
        for side in (0, 1):
            cols = pl.ds(side * half, half)
            want = row_ref[2:3, cols].astype(jnp.int32) - base
            ga_ref[:, cols] = weights(log_buf[slot, :, cols], row_ref[0:1, cols], rows_of(CH, half, 0) == want, inv_n)
        for side, h_ref in ((0, hc_ref), (1, hd_ref)):
            cols = pl.ds(side * half, half)
            lx_ref[:, cols] = dot(emb_buf[slot], h_ref[...], NT)
        piece_ref[rows, :] = dot(ga_ref[:, pl.ds(0, half)], ha_ref[...], NN) + dot(ga_ref[:, pl.ds(half, half)], hb_ref[...], NN)
        for side in (0, 1):
            cols = pl.ds(side * half, half)
            want = rowx_ref[2:3, cols].astype(jnp.int32) - base
            gx_ref[:, cols] = weights(lx_ref[:, cols], rowx_ref[0:1, cols], rows_of(CH, half, 0) == want, inv_n)
        piece_ref[rows, :] += dot(gx_ref[:, pl.ds(0, half)], hc_ref[...], NN) + dot(gx_ref[:, pl.ds(half, half)], hd_ref[...], NN)

        @pl.when(more)
        def _():
            for copy in fetch(k + 1):
                copy.wait()

        return carry

    lax.fori_loop(0, count, step, 0)
    for copy in writes:
        copy.wait()


def tail_kernel(inv_n, core_ref, tail_ref, ha_ref, hb_ref, hc_ref, hd_ref, row_ref, rowx_ref, _, out_ref, g_ref):
    half = ha_ref.shape[0]
    grad = jnp.zeros(out_ref.shape, F32)
    ids = rows_of(TAIL, half, 0)
    for h_ref, r_ref, side in ((ha_ref, row_ref, 0), (hb_ref, row_ref, 1), (hc_ref, rowx_ref, 0), (hd_ref, rowx_ref, 1)):
        cols = pl.ds(side * half, half)
        logit = dot(tail_ref[...], h_ref[...], NT)
        g_ref[...] = weights(logit, r_ref[0:1, cols], ids + core_ref[2] == r_ref[2:3, cols].astype(jnp.int32), inv_n)
        grad += dot(g_ref[...], h_ref[...], NN)
    out_ref[...] = grad


def last_kernel(places, core_ref, _, *refs):
    srcs, out_ref, sems = refs[:len(places)], refs[len(places)], refs[len(places) + 1:]
    copies = []
    for src, sem, (other, place) in zip(srcs, sems, places):
        side = 1 - core_ref[0] if other else core_ref[0]
        copies.append(pltpu.make_async_copy(src, out_ref.at[rows_at(side, *place)], sem))
    for copy in copies:
        copy.start()
    for copy in copies:
        copy.wait()


def cost(flops, moved):
    return pl.CostEstimate(flops=int(flops), bytes_accessed=int(moved), transcendentals=0)


def params(mib):
    return pltpu.CompilerParams(vmem_limit_bytes=mib << 20)


def swapped(value, axis, perm):
    return lax.ppermute(value, axis, perm)


def solution(mesh):
    n_tp, n_dp = mesh.shape['tp'], mesh.shape['dp']

    def program(hidden, residual, targets, embedding, norm_w):
        inv_n = 1.0 / (hidden.shape[0] * hidden.shape[1])

        def local_part(hid_loc, res_loc, tgt_loc, emb_loc, norm_vec):
            n_batch, n_seq, d = hid_loc.shape
            half = n_batch * n_seq
            vocab_loc = emb_loc.shape[0]
            per_core = sum(PIECES)
            tail_rows = vocab_loc - 2 * per_core * CH
            my_tp, my_dp = lax.axis_index('tp'), lax.axis_index('dp')
            core = lax.rem(my_dp, 2)
            start = my_tp * vocab_loc
            core_arg = jnp.stack([core, start + core * (per_core * CH), start + 2 * per_core * CH])
            swap = [(i, i ^ 1) for i in range(n_dp)]
            cross = [(i, i ^ 2) for i in range(n_dp)]
            cross_swap = [(i, i ^ 3) for i in range(n_dp)]
            flip = [(i, i ^ 1) for i in range(n_tp)]
            flip_swap = [(t * n_dp + i, (t ^ 1) * n_dp + (i ^ 1)) for t in range(n_tp) for i in range(n_dp)]

            norm_row = norm_vec.reshape(1, d)
            tgt_own = tgt_loc.reshape(1, half)
            rows = half // 4
            scaled, ha, inv_rms = pl.pallas_call(
                norm_kernel,
                grid=(4,),
                in_specs=[pl.BlockSpec((rows, d), lambda i: (i, 0)), pl.BlockSpec((rows, d), lambda i: (i, 0)), VM],
                out_specs=[pl.BlockSpec((rows, d), lambda i: (i, 0)), pl.BlockSpec((rows, d), lambda i: (i, 0)), pl.BlockSpec((rows, 128), lambda i: (i, 0))],
                out_shape=[jax.ShapeDtypeStruct((half, d), F32), jax.ShapeDtypeStruct((half, d), BF16), jax.ShapeDtypeStruct((half, 128), F32)],
                compiler_params=params(14),
                cost_estimate=cost(1e7, half * d * 12),
            )(hid_loc.reshape(half, d), res_loc.reshape(half, d), norm_row)
            scaled_sib = lax.ppermute(scaled, 'dp', swap)
            tgt_sib = lax.ppermute(tgt_own, 'dp', swap)
            scaled_far = swapped(scaled, 'dp', cross)
            tgt_near = jnp.concatenate([tgt_own, tgt_sib], axis=1)
            emb_tail = jnp.pad(emb_loc[2 * per_core * CH:], ((0, TAIL - tail_rows), (0, 0)))

            steps, blk = per_core // STEP, STEP * CH
            flops_unit = 2.0 * CH * d * half
            logits, logits_tail, stat, hb = pl.pallas_call(
                functools.partial(stats_kernel, tail_rows),
                grid_spec=pltpu.PrefetchScalarGridSpec(
                    num_scalar_prefetch=1, grid=(steps,),
                    in_specs=[pl.BlockSpec((blk, d), lambda i, c: (c[0] * steps + i, 0)), VM, VM, VM, VM, VM],
                    out_specs=[pl.BlockSpec((blk, 2 * half), lambda i, c: (i, 0)), VM, VM, VM],
                    scratch_shapes=[pltpu.VMEM((8, 2 * half), F32)] * 3),
                out_shape=[jax.ShapeDtypeStruct((per_core * CH, 2 * half), F32),
                           jax.ShapeDtypeStruct((TAIL, 2 * half), F32), jax.ShapeDtypeStruct((8, 2 * half), F32), jax.ShapeDtypeStruct((half, d), BF16)],
                compiler_params=params(30),
                cost_estimate=cost(flops_unit * per_core * 2, per_core * CH * (2 * d + 8 * half)),
            )(core_arg, emb_loc, emb_tail, ha, scaled_sib, norm_row, tgt_near)

            def turned(x):
                return jnp.concatenate([x[:, half:], x[:, :half]], axis=1)

            near = stat[0:3]
            sib = turned(lax.ppermute(near, 'dp', swap))
            over = lax.ppermute(near, 'tp', flip)
            over_sib = turned(lax.ppermute(near, ('tp', 'dp'), flip_swap))
            top = jnp.maximum(jnp.maximum(near[0], sib[0]), jnp.maximum(over[0], over_sib[0]))
            parts = [p[1] * jnp.exp(p[0] - top) for p in (near, sib, over, over_sib)]
            sum_exp = (parts[0] + parts[1]) + (parts[2] + parts[3])
            tgt_logit = (near[2] + sib[2]) + (over[2] + over_sib[2])
            token_loss = top + jnp.log(sum_exp) - tgt_logit
            row_near = jnp.pad(jnp.stack([jnp.log2(inv_n / sum_exp) - top * LOG2E, token_loss, tgt_near[0].astype(F32)]), ((0, 5), (0, 0)))
            row_near, scaled_far = lax.optimization_barrier((row_near, scaled_far))
            scaled_far_sib = swapped(scaled_far, 'dp', swap)
            row_far = swapped(row_near, 'dp', cross)

            dh_own, dh_sib, loss_chip = pl.pallas_call(
                functools.partial(dh_kernel, tail_rows, inv_n),
                grid_spec=pltpu.PrefetchScalarGridSpec(
                    num_scalar_prefetch=1, grid=(steps,),
                    in_specs=[pl.BlockSpec((blk, d), lambda i, c: (c[0] * steps + i, 0)),
                              pl.BlockSpec((blk, 2 * half), lambda i, c: (i, 0)), VM, VM, VM, VM],
                    out_specs=[VM, VM, VM],
                    scratch_shapes=[pltpu.VMEM((blk, 2 * half), BF16), pltpu.VMEM((TAIL, 2 * half), BF16)]),
                out_shape=[jax.ShapeDtypeStruct((half, d), F32)] * 2 + [jax.ShapeDtypeStruct((8, 128), F32)],
                compiler_params=params(31),
                cost_estimate=cost(flops_unit * per_core * 2, per_core * CH * (2 * d + 8 * half)),
            )(core_arg, emb_loc, logits, emb_tail, logits_tail, row_near, tgt_near)

            tie = lax.optimization_barrier
            row_near, row_far, scaled_far, scaled_far_sib, dh_own, dh_sib = tie(
                (row_near, row_far, scaled_far, scaled_far_sib, dh_own, dh_sib))
            dh_got = swapped(dh_sib, 'dp', swap)
            loss_far = swapped(loss_chip, 'dp', cross)

            def piece_call(first, count, mark, out, bufs, prev, own, late, got, far, job, job_args, job_outs):
                extra = ([] if out is None else [out, *bufs, own]) + ([] if got is None else [got]) + job_args
                specs = ([] if out is None else [HB, VM, VM, VM]) + ([] if got is None else [VM]) + [VM] * len(job_args)
                return pl.pallas_call(
                    functools.partial(grad_kernel, job, first, count, prev, late, inv_n),
                    in_specs=[pl.BlockSpec(memory_space=pltpu.SMEM), HB, HB] + [VM] * 7 + specs,
                    out_specs=[HB] + [VM] * (4 + len(job_outs)),
                    scratch_shapes=[pltpu.VMEM((CH, 2 * half), BF16), pltpu.VMEM((CH, 2 * half), BF16), pltpu.VMEM((CH, 2 * half), F32)]
                    + [pltpu.SemaphoreType.DMA] * 4,
                    out_shape=[jax.ShapeDtypeStruct((vocab_loc, d), F32), jax.ShapeDtypeStruct((2, CH, d), BF16),
                               jax.ShapeDtypeStruct((2, CH, 2 * half), F32), pltpu.VMEM((count * CH, d), F32),
                               jax.ShapeDtypeStruct((8, 128), F32)] + job_outs,
                    input_output_aliases={} if out is None else {10: 0, 11: 1, 12: 2},
                    compiler_params=params(8 if job is None else 10),
                    cost_estimate=cost(flops_unit * count * 6, count * CH * (2 * d + 8 * half + 8 * d)),
                )(core_arg, emb_loc, logits, ha, hb, *far, row_near, row_far, mark, *extra)

            out, bufs, first, own, prev, arrived = None, (), 0, None, None, []
            mark = jnp.zeros((8, 128), F32)
            far = (ha, hb)
            for k, count in enumerate(PIECES):
                late, got = arrived[k - 2] if k >= 2 else (None, None)
                job, job_args, job_outs = None, [], []
                if k == 0:
                    job, job_args = 'act', [norm_row, scaled_far, scaled_far_sib]
                    job_outs = [jax.ShapeDtypeStruct((half, d), BF16)] * 2
                if k == ADD_AT:
                    dh_got, mark = tie((dh_got, mark))
                    job, job_args, job_outs = 'add', [dh_own, dh_got], [jax.ShapeDtypeStruct((half, d), F32)]
                out, emb_buf, log_buf, piece, mark, *made = piece_call(
                    first, count, mark, out, bufs, prev, own, late, got, far, job, job_args, job_outs)
                bufs = (emb_buf, log_buf)
                own, prev = piece, (first, count)
                arrived.append((prev, lax.ppermute(piece, 'dp', swap)))
                first += count
                if k == 0:
                    far = made
                if k == ADD_AT:
                    loss_far, mark = tie((loss_far, mark))
                    dh_chip, mark = tie((made[0], mark))
                    dh_far = swapped(dh_chip, 'tp', flip)
                if k == FINISH_AT:
                    dh_far, mark = tie((dh_far, mark))
                    blk_rows = pl.BlockSpec((half // 4, d), lambda i: (i, 0))
                    grad_r, grad_w = pl.pallas_call(
                        finish_kernel,
                        grid=(4,),
                        in_specs=[VM, pl.BlockSpec((half // 4, 128), lambda i: (i, 0)), blk_rows, blk_rows, blk_rows],
                        out_specs=[blk_rows, VM],
                        scratch_shapes=[pltpu.VMEM((8, d), F32)],
                        out_shape=[jax.ShapeDtypeStruct((half, d), F32), jax.ShapeDtypeStruct((1, d), F32)],
                        compiler_params=params(8),
                        cost_estimate=cost(1e7, half * d * 16),
                    )(norm_row, inv_rms, scaled, dh_chip, dh_far)
                    grad_w, mark = tie((grad_w, mark))
                    gw = [swapped(grad_w, 'dp', swap), swapped(grad_w, 'dp', cross), swapped(grad_w, 'dp', cross_swap)]
            loss_mean = ((loss_chip + loss_far) * inv_n)[0, 0]
            grad_w = ((grad_w + gw[0]) + (gw[1] + gw[2])).reshape(d)
            hc, hd = far

            out = pl.pallas_call(
                functools.partial(tail_kernel, inv_n),
                grid_spec=pltpu.PrefetchScalarGridSpec(
                    num_scalar_prefetch=1, grid=(1,), in_specs=[VM] * 7 + [HB],
                    out_specs=pl.BlockSpec((TAIL, d), lambda i, c: (2 * per_core * CH // TAIL, 0)),
                    scratch_shapes=[pltpu.VMEM((TAIL, half), BF16)]),
                out_shape=jax.ShapeDtypeStruct((vocab_loc, d), F32),
                input_output_aliases={8: 0},
                compiler_params=params(14),
                cost_estimate=cost(2.0 * TAIL * d * half * 8, 4 * TAIL * d),
            )(core_arg, emb_tail, ha, hb, hc, hd, row_near, row_far, out)
            for parts in ([(False, prev, own), (True, *arrived[-2])], [(True, *arrived[-1])]):
                out = pl.pallas_call(
                    functools.partial(last_kernel, [p[:2] for p in parts]),
                    in_specs=[pl.BlockSpec(memory_space=pltpu.SMEM), HB] + [VM] * len(parts), out_specs=HB,
                    scratch_shapes=[pltpu.SemaphoreType.DMA] * len(parts),
                    out_shape=jax.ShapeDtypeStruct((vocab_loc, d), F32),
                    input_output_aliases={1: 0},
                    compiler_params=params(8),
                    cost_estimate=cost(1e6, sum(4 * p[1][1] * CH * d for p in parts)),
                )(core_arg, out, *[p[2] for p in parts])
            return loss_mean, grad_r.reshape(n_batch, n_seq, d), out, grad_w

        sharded = jax.shard_map(
            local_part, mesh=mesh,
            in_specs=(P('dp', None, None), P('dp', None, None), P('dp', None), P('tp', None), P(None)),
            out_specs=(P(), P('dp', None, None), P('tp', None), P(None)),
            check_vma=False)
        return sharded(hidden, residual, targets, embedding, norm_w)

    return program
```

time: 290 us -> 300 us (1.034)
  other arithmetic: 12.3 us -> 0.8 us
  waiting for transfers between devices: 58.6 us -> 68.1 us
  Pallas kernels: 201 us -> 208 us
  local copies, waits for them, and re-layouts: 1.25 us -> 6.94 us
    ppermute x9, waiting for transfers between devices: 54.2 us -> 64.3 us  [swapped(): return lax.ppermute(value, axis, perm)]
    unnamed x35 -> x25, local copies, waits for them, and re-layouts: 0.69 us -> 5.48 us
    pallas_call x11 -> x12, Pallas kernels: 114 us -> 118 us  [the longest x10 115 us: piece_call(): pl.pallas_call(functools.partial(grad_kernel, job, first, count, prev, la...]
    convert_element_type x3 -> x1, other arithmetic: 4.35 us -> 0.01 us  [local_part(): tgt_near[0].astype(F32)]
    reduce_sum x2 -> x0, other arithmetic: 3.04 us -> none  [the longest x1 2.35 us: local_part(): jnp.mean(resid * resid, axis=-1, keepdims=True) + NORM_EPS]
  transfers between devices with their start and end apart: 25 -> 24, of which waited for: 8 -> 6; matrix products, arithmetic and copies ran while one was open for 3% -> 1% of each run, Pallas kernels for 65% -> 64%
where the time goes in v4:
time: 300 us; the launch traced here: 299 us
  Pallas kernels  208 us (69%)
  waiting for transfers between devices  68.1 us (23%)
  starting transfers between devices  13.5 us (4%)
  local copies, waits for them, and re-layouts  6.94 us (2%)
    pallas_call x10, Pallas kernels, piece_call(): pl.pallas_call(functools.partial(grad_kernel, job, first, count, prev, la...  115 us
    ppermute x9, waiting for transfers between devices, swapped(): return lax.ppermute(value, axis, perm)  64.3 us
    pallas_call x1, Pallas kernels, local_part(): pl.pallas_call(functools.partial(stats_kernel, tail_rows), grid_spec=pltp...  45.6 us
    pallas_call x1, Pallas kernels, local_part(): pl.pallas_call(functools.partial(dh_kernel, tail_rows, inv_n), grid_spec=...  35.7 us
    ppermute x9, starting transfers between devices, swapped(): return lax.ppermute(value, axis, perm)  7.25 us
  transfers between devices with their start and end apart: 24, of which 6 were waited for; matrix products, arithmetic and copies ran while one was open for 1% of the time, Pallas kernels for 64%

profile of v4, /device:TPU:0, one launch (start us, length us, event | category | flops | bytes accessed | tf_op | source)
XLA Modules:
  0.0 298.8 jit_solution(10999556426534469556)
XLA Ops:
  0.6 1.6 copy-done
  2.2 1.2 copy-done.3
  3.5 0.7 copy-done.4
  4.1 0.7 shard_map.84
  4.9 0.9 collective-permute-start
  5.7 2.5 collective-permute-start.5
  9.2 0.9 slice.64
  10.8 45.6 %shard_map.85 = (f32[12544,1024]{1,0:T(8,128)}, f32[64,1024]{1,0:T(8,128)S(1)}, f32[8,1024]{1,0:T(8,128)S(1)}, bf16[512,1024]{1,0:T(8,128)(2,1)S(1)}) custom-call(s32[3]{0:T(128)S(1)} %pad_add_fusion.core_ref, bf16[25140,1024]{1,0:T(8,128)(2,1)} %emb_ref.23, bf16[64,1024]{1,0:T(8,128)(2,1)S(1)} %pad.8.tail_ref, ...), custom_call_target="tpu_custom_call" | custom-call | flops 26306674688 | bytes 77070336 | tf_op jit(solution)/shard_map/pallas_call | solution.py:302
  56.8 2.2 collective-permute-start.4
  59.0 1.4 collective-permute-done.4
  60.4 2.3 collective-permute-done.3
  62.9 1.5 collective-permute-start.7
  64.4 35.7 %shard_map.86 = (f32[512,1024]{1,0:T(8,128)S(1)}, f32[512,1024]{1,0:T(8,128)S(1)}, f32[8,128]{1,0:T(8,128)S(1)}) custom-call(s32[3]{0:T(128)S(1)} %pad_add_fusion.core_ref, bf16[25140,1024]{1,0:T(8,128)(2,1)} %emb_ref.23, f32[12544,1024]{1,0:T(8,128)} %get-tuple-element.86.log_ref, bf16[64,1024]{1,0:T(8,128)(2,1)S(1)} %pad.8.tail_ref, ...), custom_call_target="tpu_custom_call" | custom-call | flops 26306674688 | bytes 77070336 | tf_op jit(solution)/shard_map/pallas_call | solution.py:332
  100.2 15.2 %shard_map.87 = (f32[25140,1024]{1,0:T(8,128)}, bf16[2,256,1024]{2,1,0:T(8,128)(2,1)S(1)}, f32[2,256,1024]{2,1,0:T(8,128)S(1)}, f32[1536,1024]{1,0:T(8,128)S(1)}...) custom-call(s32[3]{0:T(128)S(1)} %pad_add_fusion.core_ref, ...), custom_call_target="tpu_custom_call" | custom-call | flops 9663676416 | bytes 22020096 | tf_op jit(solution)/shard_map/pallas_call | solution.py:354
  115.9 12.6 %collective-permute-done.9.refs_5_ = f32[512,1024]{1,0:T(8,128)S(1)} collective-permute-done((f32[512,1024]{1,0:T(8,128)S(1)}, f32[512,1024]{1,0:T(8,128)S(1)}, u32[]{:S(2)}, u32[]{:S(2)}) %collective-permute-start.9) | collective-permute-done | bytes 2097184 | tf_op jit(solution)/shard_map/ppermute | solution.py:257
  128.5 13.2 %shard_map.88 = (f32[25140,1024]{1,0:T(8,128)}, bf16[2,256,1024]{2,1,0:T(8,128)(2,1)S(1)}, f32[2,256,1024]{2,1,0:T(8,128)S(1)}, f32[1536,1024]{1,0:T(8,128)S(1)}...) custom-call(s32[3]{0:T(128)S(1)} %pad_add_fusion.core_ref, ...), custom_call_target="tpu_custom_call", output_to_operand_aliasing={{0}: (10, {}), {1}: (11, {}), {2}: (12, {})} | custom-call | flops 9663676416 | bytes 22020096 | tf_op jit(solution)/shard_map/pallas_call | solution.py:354
  142.5 3.1 %collective-permute-done.6 = f32[8,128]{1,0:T(8,128)S(1)} collective-permute-done((f32[8,128]{1,0:T(8,128)S(1)}, f32[8,128]{1,0:T(8,128)S(1)}, u32[]{:S(2)}, u32[]{:S(2)}) %collective-permute-start.6) | collective-permute-done | bytes 4128 | tf_op jit(solution)/shard_map/ppermute | solution.py:257
  146.2 13.5 %shard_map.89 = (f32[25140,1024]{1,0:T(8,128)}, bf16[2,256,1024]{2,1,0:T(8,128)(2,1)S(1)}, f32[2,256,1024]{2,1,0:T(8,128)S(1)}, f32[1536,1024]{1,0:T(8,128)S(1)}, f32[8,128]{1,0:T(8,128)S(1)}) custom-call(s32[3]{0:T(128)S(1)} %pad_add_fusion.core_ref, bf16[25140,1024]{1,0:T(8,128)(2,1)} %emb_ref.23, ...), custom_call_target="tpu_custom_call", output_to_operand_aliasing={{0}: (10, {}), {1}: (11, {}), {2}: (12, {})} | custom-call | flops 9663676416 | bytes 22020096 | tf_op jit(solution)/shard_map/pallas_call | solution.py:354
  159.7 11.5 %shard_map.90 = (f32[25140,1024]{1,0:T(8,128)}, bf16[2,256,1024]{2,1,0:T(8,128)(2,1)S(1)}, f32[2,256,1024]{2,1,0:T(8,128)S(1)}, f32[1280,1024]{1,0:T(8,128)S(1)}, f32[8,128]{1,0:T(8,128)S(1)}) custom-call(s32[3]{0:T(128)S(1)} %pad_add_fusion.core_ref, bf16[25140,1024]{1,0:T(8,128)(2,1)} %emb_ref.23, ...), custom_call_target="tpu_custom_call", output_to_operand_aliasing={{0}: (10, {}), {1}: (11, {}), {2}: (12, {})} | custom-call | flops 8053063680 | bytes 18350080 | tf_op jit(solution)/shard_map/pallas_call | solution.py:354
  171.8 11.5 %shard_map.91 = (f32[25140,1024]{1,0:T(8,128)}, bf16[2,256,1024]{2,1,0:T(8,128)(2,1)S(1)}, f32[2,256,1024]{2,1,0:T(8,128)S(1)}, f32[1280,1024]{1,0:T(8,128)S(1)}, f32[8,128]{1,0:T(8,128)S(1)}) custom-call(s32[3]{0:T(128)S(1)} %pad_add_fusion.core_ref, bf16[25140,1024]{1,0:T(8,128)(2,1)} %emb_ref.23, ...), custom_call_target="tpu_custom_call", output_to_operand_aliasing={{0}: (10, {}), {1}: (11, {}), {2}: (12, {})} | custom-call | flops 8053063680 | bytes 18350080 | tf_op jit(solution)/shard_map/pallas_call | solution.py:354
  183.3 11.8 %shard_map.92 = (f32[25140,1024]{1,0:T(8,128)}, bf16[2,256,1024]{2,1,0:T(8,128)(2,1)S(1)}, f32[2,256,1024]{2,1,0:T(8,128)S(1)}, f32[1280,1024]{1,0:T(8,128)S(1)}, f32[8,128]{1,0:T(8,128)S(1)}) custom-call(s32[3]{0:T(128)S(1)} %pad_add_fusion.core_ref, bf16[25140,1024]{1,0:T(8,128)(2,1)} %emb_ref.23, ...), custom_call_target="tpu_custom_call", output_to_operand_aliasing={{0}: (10, {}), {1}: (11, {}), {2}: (12, {})} | custom-call | flops 8053063680 | bytes 18350080 | tf_op jit(solution)/shard_map/pallas_call | solution.py:354
  196.2 47.1 %collective-permute-done.10.far_ref = f32[512,1024]{1,0:T(8,128)S(1)} collective-permute-done((f32[512,1024]{1,0:T(8,128)S(1)}, f32[512,1024]{1,0:T(8,128)S(1)}, u32[]{:S(2)}, u32[]{:S(2)}) %collective-permute-start.10) | collective-permute-done | bytes 2097184 | tf_op jit(solution)/shard_map/ppermute | solution.py:257
  243.2 2.4 shard_map.93
  245.7 11.5 %shard_map.94 = (f32[25140,1024]{1,0:T(8,128)}, bf16[2,256,1024]{2,1,0:T(8,128)(2,1)S(1)}, f32[2,256,1024]{2,1,0:T(8,128)S(1)}, f32[1280,1024]{1,0:T(8,128)S(1)}, f32[8,128]{1,0:T(8,128)S(1)}) custom-call(s32[3]{0:T(128)S(1)} %pad_add_fusion.core_ref, bf16[25140,1024]{1,0:T(8,128)(2,1)} %emb_ref.23, ...), custom_call_target="tpu_custom_call", output_to_operand_aliasing={{0}: (10, {}), {1}: (11, {}), {2}: (12, {})} | custom-call | flops 8053063680 | bytes 18350080 | tf_op jit(solution)/shard_map/pallas_call | solution.py:354
  257.2 11.8 %shard_map.95 = (f32[25140,1024]{1,0:T(8,128)}, bf16[2,256,1024]{2,1,0:T(8,128)(2,1)S(1)}, f32[2,256,1024]{2,1,0:T(8,128)S(1)}, f32[1280,1024]{1,0:T(8,128)S(1)}, f32[8,128]{1,0:T(8,128)S(1)}) custom-call(s32[3]{0:T(128)S(1)} %pad_add_fusion.core_ref, bf16[25140,1024]{1,0:T(8,128)(2,1)} %emb_ref.23, ...), custom_call_target="tpu_custom_call", output_to_operand_aliasing={{0}: (10, {}), {1}: (11, {}), {2}: (12, {})} | custom-call | flops 8053063680 | bytes 18350080 | tf_op jit(solution)/shard_map/pallas_call | solution.py:354
  269.5 9.5 %shard_map.96 = (f32[25140,1024]{1,0:T(8,128)}, bf16[2,256,1024]{2,1,0:T(8,128)(2,1)S(1)}, f32[2,256,1024]{2,1,0:T(8,128)S(1)}, f32[1024,1024]{1,0:T(8,128)S(1)}, f32[8,128]{1,0:T(8,128)S(1)}) custom-call(s32[3]{0:T(128)S(1)} %pad_add_fusion.core_ref, bf16[25140,1024]{1,0:T(8,128)(2,1)} %emb_ref.23, ...), custom_call_target="tpu_custom_call", output_to_operand_aliasing={{0}: (10, {}), {1}: (11, {}), {2}: (12, {})} | custom-call | flops 6442450944 | bytes 14680064 | tf_op jit(solution)/shard_map/pallas_call | solution.py:354
  279.1 5.7 %shard_map.97 = (f32[25140,1024]{1,0:T(8,128)}, bf16[2,256,1024]{2,1,0:T(8,128)(2,1)S(1)}, f32[2,256,1024]{2,1,0:T(8,128)S(1)}, f32[512,1024]{1,0:T(8,128)S(1)}, f32[8,128]{1,0:T(8,128)}) custom-call(s32[3]{0:T(128)S(1)} %pad_add_fusion.core_ref, bf16[25140,1024]{1,0:T(8,128)(2,1)} %emb_ref.23, ...), custom_call_target="tpu_custom_call", output_to_operand_aliasing={{0}: (10, {}), {1}: (11, {}), {2}: (12, {})} | custom-call | flops 3221225472 | bytes 7340032 | tf_op jit(solution)/shard_map/pallas_call | solution.py:354
  285.9 1.3 collective-permute-start.23
  287.7 1.5 collective-permute-done.21
  289.8 3.6 %shard_map.98._ = f32[25140,1024]{1,0:T(8,128)} custom-call(s32[3]{0:T(128)S(1)} %pad_add_fusion.core_ref, bf16[64,1024]{1,0:T(8,128)(2,1)S(1)} %pad.8.tail_ref, bf16[512,1024]{1,0:T(8,128)(2,1)S(1)} %get-tuple-element.84.ha_ref.hc_ref, bf16[512,1024]{1,0:T(8,128)(2,1)S(1)} %get-tuple-element.91.hb_ref.hd_ref, ...), custom_call_target="tpu_custom_call", output_to_operand_aliasing={{}: (8, {})} | custom-call | flops 536870912 | bytes 262144 | tf_op jit(solution)/shard_map/pallas_call | solution.py:411
  293.5 3.3 %shard_map.99._ = f32[25140,1024]{1,0:T(8,128)} custom-call(s32[3]{0:T(128)S(1)} %pad_add_fusion.core_ref, f32[25140,1024]{1,0:T(8,128)} %shard_map.98._, f32[512,1024]{1,0:T(8,128)S(1)} %get-tuple-element.162.refs_0_, f32[1024,1024]{1,0:T(8,128)S(1)} %collective-permute-done.19.refs_1_), custom_call_target="tpu_custom_call", output_to_operand_aliasing={{}: (1, {})} | custom-call | flops 1000000 | bytes 6291456 | tf_op jit(solution)/shard_map/pallas_call | solution.py:423
  296.8 1.9 shard_map.100
  (73 shorter events, 8.5 us)
Async XLA Ops:
  0.6 1.6 copy-start
  4.8 51.6 %copy-start.1 = (f32[512,1024]{1,0:T(8,128)}, f32[512,1024]{1,0:T(8,128)S(1)}, u32[]{:S(2)}) copy-start(f32[512,1024]{1,0:T(8,128)S(1)} %get-tuple-element.85.scaled_ref) | copy-start | bytes 6291460
  4.9 5.3 %collective-permute-start = (f32[512,1024]{1,0:T(8,128)S(1)}, f32[512,1024]{1,0:T(8,128)}, u32[]{:S(2)}, u32[]{:S(2)}) collective-permute-start(f32[512,1024]{1,0:T(8,128)S(1)} %get-tuple-element.85.scaled_ref), channel_id=1, source_target_pairs={{0,1},{1,0},{2,3},{3,2},{4,5},{5,4},{6,7},{7,6}} | collective-permute-start | bytes 6291464 | tf_op jit(solution)/shard_map/ppermute | solution.py:294
  5.7 57.1 %collective-permute-start.5 = (f32[512,1024]{1,0:T(8,128)S(1)}, f32[512,1024]{1,0:T(8,128)}, u32[]{:S(2)}, u32[]{:S(2)}) collective-permute-start(f32[512,1024]{1,0:T(8,128)S(1)} %get-tuple-element.85.scaled_ref), channel_id=1, source_target_pairs={{0,2},{1,3},{2,0},{3,1},{4,6},{5,7},{6,4},{7,5}} | collective-permute-start | bytes 6291464 | tf_op jit(solution)/shard_map/ppermute | solution.py:257
  8.2 1.9 collective-permute-start.1
  56.4 2.6 collective-permute-start.2
  56.8 3.6 %collective-permute-start.4 = (f32[3,1024]{1,0:T(4,128)S(1)}, f32[3,1024]{1,0:T(4,128)S(1)}, u32[]{:S(2)}, u32[]{:S(2)}) collective-permute-start(f32[3,1024]{1,0:T(4,128)S(1)} %slice.67), channel_id=1, source_target_pairs={{0,5},{1,4},{2,7},{3,6},{4,1},{5,0},{6,3},{7,2}} | collective-permute-start | bytes 36872 | tf_op jit(solution)/shard_map/ppermute | solution.py:321
  59.0 3.7 %collective-permute-start.3 = (f32[3,1024]{1,0:T(4,128)S(1)}, f32[3,1024]{1,0:T(4,128)S(1)}, u32[]{:S(2)}, u32[]{:S(2)}) collective-permute-start(f32[3,1024]{1,0:T(4,128)S(1)} %slice.67), channel_id=1, source_target_pairs={{0,4},{4,0},{1,5},{5,1},{2,6},{6,2},{3,7},{7,3}} | collective-permute-start | bytes 36872 | tf_op jit(solution)/shard_map/ppermute | solution.py:320
  62.8 37.3 %collective-permute-start.8 = (f32[512,1024]{1,0:T(8,128)}, f32[512,1024]{1,0:T(8,128)S(1)}, u32[]{:S(2)}, u32[]{:S(2)}) collective-permute-start(f32[512,1024]{1,0:T(8,128)} %collective-permute-done.5.refs_1_), channel_id=1, source_target_pairs={{0,1},{1,0},{2,3},{3,2},{4,5},{5,4},{6,7},{7,6}} | collective-permute-start | bytes 6291464 | tf_op jit(solution)/shard_map/ppermute | solution.py:257
  62.9 37.3 %collective-permute-start.7 = (f32[8,1024]{1,0:T(8,128)S(1)}, f32[8,1024]{1,0:T(8,128)S(1)}, u32[]{:S(2)}, u32[]{:S(2)}) collective-permute-start(f32[8,1024]{1,0:T(8,128)S(1)} %select_maximum_fusion.row_ref), channel_id=1, source_target_pairs={{0,2},{1,3},{2,0},{3,1},{4,6},{5,7},{6,4},{7,5}} | collective-permute-start | bytes 98312 | tf_op jit(solution)/shard_map/ppermute | solution.py:257
  64.4 35.8 %copy-start.6 = (f32[1024]{0:T(1024)S(1)}, f32[1024]{0:T(1024)}, u32[]{:S(2)}) copy-start(f32[1024]{0:T(1024)} %param.9) | copy-start | bytes 12292
  100.1 41.9 %copy-start.8 = (f32[8,128]{1,0:T(8,128)}, f32[8,128]{1,0:T(8,128)S(1)}, u32[]{:S(2)}) copy-start(f32[8,128]{1,0:T(8,128)S(1)} %get-tuple-element.90) | copy-start | bytes 12292
  115.4 30.2 %collective-permute-start.11 = (f32[1536,1024]{1,0:T(8,128)S(1)}, f32[1536,1024]{1,0:T(8,128)S(1)}, u32[]{:S(2)}, u32[]{:S(2)}) collective-permute-start(f32[1536,1024]{1,0:T(8,128)S(1)} %get-tuple-element.107.refs_3_), channel_id=1, source_target_pairs={{0,1},{1,0},{2,3},{3,2},{4,5},{5,4},{6,7},{7,6}} | collective-permute-start | bytes 18874376 | tf_op jit(solution)/shard_map/ppermute | solution.py:384
  115.6 13.0 %collective-permute-start.9 = (f32[512,1024]{1,0:T(8,128)S(1)}, f32[512,1024]{1,0:T(8,128)S(1)}, u32[]{:S(2)}, u32[]{:S(2)}) collective-permute-start(f32[512,1024]{1,0:T(8,128)S(1)} %get-tuple-element.101), channel_id=1, source_target_pairs={{0,1},{1,0},{2,3},{3,2},{4,5},{5,4},{6,7},{7,6}} | collective-permute-start | bytes 6291464 | tf_op jit(solution)/shard_map/ppermute | solution.py:257
  141.8 17.9 %collective-permute-start.12 = (f32[1536,1024]{1,0:T(8,128)S(1)}, f32[1536,1024]{1,0:T(8,128)S(1)}, u32[]{:S(2)}, u32[]{:S(2)}) collective-permute-start(f32[1536,1024]{1,0:T(8,128)S(1)} %get-tuple-element.120.refs_3_), channel_id=1, source_target_pairs={{0,1},{1,0},{2,3},{3,2},{4,5},{5,4},{6,7},{7,6}} | collective-permute-start | bytes 18874376 | tf_op jit(solution)/shard_map/ppermute | solution.py:384
  142.0 3.6 %collective-permute-start.6 = (f32[8,128]{1,0:T(8,128)S(1)}, f32[8,128]{1,0:T(8,128)S(1)}, u32[]{:S(2)}, u32[]{:S(2)}) collective-permute-start(f32[8,128]{1,0:T(8,128)S(1)} %get-tuple-element.90), channel_id=1, source_target_pairs={{0,2},{1,3},{2,0},{3,1},{4,6},{5,7},{6,4},{7,5}} | collective-permute-start | bytes 12296 | tf_op jit(solution)/shard_map/ppermute | solution.py:257
  159.7 12.1 %collective-permute-start.13 = (f32[1536,1024]{1,0:T(8,128)S(1)}, f32[1536,1024]{1,0:T(8,128)S(1)}, u32[]{:S(2)}, u32[]{:S(2)}) collective-permute-start(f32[1536,1024]{1,0:T(8,128)S(1)} %get-tuple-element.125.refs_3_), channel_id=1, source_target_pairs={{0,1},{1,0},{2,3},{3,2},{4,5},{5,4},{6,7},{7,6}} | collective-permute-start | bytes 18874376 | tf_op jit(solution)/shard_map/ppermute | solution.py:384
  171.3 12.1 %collective-permute-start.14 = (f32[1280,1024]{1,0:T(8,128)S(1)}, f32[1280,1024]{1,0:T(8,128)S(1)}, u32[]{:S(2)}, u32[]{:S(2)}) collective-permute-start(f32[1280,1024]{1,0:T(8,128)S(1)} %get-tuple-element.130.refs_3_), channel_id=1, source_target_pairs={{0,1},{1,0},{2,3},{3,2},{4,5},{5,4},{6,7},{7,6}} | collective-permute-start | bytes 15728648 | tf_op jit(solution)/shard_map/ppermute | solution.py:384
  183.3 62.4 %collective-permute-start.15 = (f32[1280,1024]{1,0:T(8,128)S(1)}, f32[1280,1024]{1,0:T(8,128)S(1)}, u32[]{:S(2)}, u32[]{:S(2)}) collective-permute-start(f32[1280,1024]{1,0:T(8,128)S(1)} %get-tuple-element.135.refs_3_), channel_id=1, source_target_pairs={{0,1},{1,0},{2,3},{3,2},{4,5},{5,4},{6,7},{7,6}} | collective-permute-start | bytes 15728648 | tf_op jit(solution)/shard_map/ppermute | solution.py:384
  183.3 59.9 %copy-start.2 = (f32[512,1024]{1,0:T(8,128)S(1)}, f32[512,1024]{1,0:T(8,128)}, u32[]{:S(2)}) copy-start(f32[512,1024]{1,0:T(8,128)} %copy-done.1) | copy-start | bytes 6291460
  183.3 59.9 %copy-start.7 = (f32[1024]{0:T(1024)S(1)}, f32[1024]{0:T(1024)}, u32[]{:S(2)}) copy-start(f32[1024]{0:T(1024)} %param.9) | copy-start | bytes 12292
  195.1 62.1 %collective-permute-start.16 = (f32[1280,1024]{1,0:T(8,128)S(1)}, f32[1280,1024]{1,0:T(8,128)S(1)}, u32[]{:S(2)}, u32[]{:S(2)}) collective-permute-start(f32[1280,1024]{1,0:T(8,128)S(1)} %get-tuple-element.145.refs_3_), channel_id=1, source_target_pairs={{0,1},{1,0},{2,3},{3,2},{4,5},{5,4},{6,7},{7,6}} | collective-permute-start | bytes 15728648 | tf_op jit(solution)/shard_map/ppermute | solution.py:384
  195.7 47.6 %collective-permute-start.10 = (f32[512,1024]{1,0:T(8,128)S(1)}, f32[512,1024]{1,0:T(8,128)S(1)}, u32[]{:S(2)}, u32[]{:S(2)}) collective-permute-start(f32[512,1024]{1,0:T(8,128)S(1)} %get-tuple-element.115.near_ref), channel_id=1, source_target_pairs={{0,4},{4,0},{1,5},{5,1},{2,6},{6,2},{3,7},{7,3}} | collective-permute-start | bytes 6291464 | tf_op jit(solution)/shard_map/ppermute | solution.py:257
  257.2 12.3 %collective-permute-start.17 = (f32[1280,1024]{1,0:T(8,128)S(1)}, f32[1280,1024]{1,0:T(8,128)S(1)}, u32[]{:S(2)}, u32[]{:S(2)}) collective-permute-start(f32[1280,1024]{1,0:T(8,128)S(1)} %get-tuple-element.150.refs_3_), channel_id=1, source_target_pairs={{0,1},{1,0},{2,3},{3,2},{4,5},{5,4},{6,7},{7,6}} | collective-permute-start | bytes 15728648 | tf_op jit(solution)/shard_map/ppermute | solution.py:384
  269.0 10.1 %collective-permute-start.18 = (f32[1280,1024]{1,0:T(8,128)S(1)}, f32[1280,1024]{1,0:T(8,128)S(1)}, u32[]{:S(2)}, u32[]{:S(2)}) collective-permute-start(f32[1280,1024]{1,0:T(8,128)S(1)} %get-tuple-element.155.refs_3_), channel_id=1, source_target_pairs={{0,1},{1,0},{2,3},{3,2},{4,5},{5,4},{6,7},{7,6}} | collective-permute-start | bytes 15728648 | tf_op jit(solution)/shard_map/ppermute | solution.py:384
  279.0 14.4 %collective-permute-start.19 = (f32[1024,1024]{1,0:T(8,128)S(1)}, f32[1024,1024]{1,0:T(8,128)S(1)}, u32[]{:S(2)}, u32[]{:S(2)}) collective-permute-start(f32[1024,1024]{1,0:T(8,128)S(1)} %get-tuple-element.160.refs_3_), channel_id=1, source_target_pairs={{0,1},{1,0},{2,3},{3,2},{4,5},{5,4},{6,7},{7,6}} | collective-permute-start | bytes 12582920 | tf_op jit(solution)/shard_map/ppermute | solution.py:384
  279.1 8.1 %copy-start.9 = (f32[8,128]{1,0:T(8,128)S(1)}, f32[8,128]{1,0:T(8,128)}, u32[]{:S(2)}) copy-start(f32[8,128]{1,0:T(8,128)} %copy-done.8) | copy-start | bytes 12292
  279.1 8.1 %copy-start.11 = (f32[8,128]{1,0:T(8,128)S(1)}, f32[8,128]{1,0:T(8,128)}, u32[]{:S(2)}) copy-start(f32[8,128]{1,0:T(8,128)} %copy-done.10) | copy-start | bytes 12292
  284.8 11.9 %collective-permute-start.20 = (f32[512,1024]{1,0:T(8,128)S(1)}, f32[512,1024]{1,0:T(8,128)S(1)}, u32[]{:S(2)}, u32[]{:S(2)}) collective-permute-start(f32[512,1024]{1,0:T(8,128)S(1)} %get-tuple-element.162.refs_0_), channel_id=1, source_target_pairs={{0,1},{1,0},{2,3},{3,2},{4,5},{5,4},{6,7},{7,6}} | collective-permute-start | bytes 6291464 | tf_op jit(solution)/shard_map/ppermute | solution.py:384
  285.3 3.9 %collective-permute-start.21 = (f32[1,1024]{1,0:T(1,128)S(1)}, f32[1,1024]{1,0:T(1,128)S(1)}, u32[]{:S(2)}, u32[]{:S(2)}) collective-permute-start(f32[1,1024]{1,0:T(1,128)S(1)} %get-tuple-element.163), channel_id=1, source_target_pairs={{0,1},{1,0},{2,3},{3,2},{4,5},{5,4},{6,7},{7,6}} | collective-permute-start | bytes 12296 | tf_op jit(solution)/shard_map/ppermute | solution.py:257
  285.3 3.9 %collective-permute-start.22 = (f32[1,1024]{1,0:T(1,128)S(1)}, f32[1,1024]{1,0:T(1,128)S(1)}, u32[]{:S(2)}, u32[]{:S(2)}) collective-permute-start(f32[1,1024]{1,0:T(1,128)S(1)} %get-tuple-element.163), channel_id=1, source_target_pairs={{0,2},{1,3},{2,0},{3,1},{4,6},{5,7},{6,4},{7,5}} | collective-permute-start | bytes 12296 | tf_op jit(solution)/shard_map/ppermute | solution.py:257
  285.9 3.3 %collective-permute-start.23 = (f32[1,1024]{1,0:T(1,128)S(1)}, f32[1,1024]{1,0:T(1,128)S(1)}, u32[]{:S(2)}, u32[]{:S(2)}) collective-permute-start(f32[1,1024]{1,0:T(1,128)S(1)} %get-tuple-element.163), channel_id=1, source_target_pairs={{0,3},{1,2},{2,1},{3,0},{4,7},{5,6},{6,5},{7,4}} | collective-permute-start | bytes 12296 | tf_op jit(solution)/shard_map/ppermute | solution.py:257
  (4 other events, 3.2 us)

commit v5 on v4

--- a/solution.py
+++ b/solution.py
@@ -34,6 +34,11 @@
     return (jnp.exp2(logit * LOG2E + shift) - jnp.where(hit, inv_n, 0.0)).astype(BF16)
 
 
+def seat(vocab_loc):
+    core, start, span = lax.rem(lax.axis_index('dp'), 2), lax.axis_index('tp') * vocab_loc, sum(PIECES) * CH
+    return core, start + core * span, start + 2 * span
+
+
 def rows_of(n, width, base):
     return lax.broadcasted_iota(jnp.int32, (n, width), 0) + base
 
@@ -48,7 +53,8 @@
 
 
 def stats_kernel(tail_rows, core_ref, emb_ref, tail_ref, ha_ref, sib_ref, norm_ref, tgt_ref, log_ref, logt_ref, stat_ref, hb_ref, top, total, hits):
-    step, core = pl.program_id(0), core_ref[0]
+    step = pl.program_id(0)
+    core, base, tail_base = seat(2 * sum(PIECES) * CH + tail_rows)
     half = ha_ref.shape[0]
 
     @pl.when(step == 0)
@@ -71,7 +77,7 @@
             cols = pl.ds(side * half, half)
             logit = dot(emb_ref[rows, :], h_ref[...], NT)
             log_ref[rows, cols] = logit
-            want = tgt_ref[0:1, cols] - (core_ref[1] + (step * STEP + k) * CH)
+            want = tgt_ref[0:1, cols] - (base + (step * STEP + k) * CH)
             fold(cols, logit, rows_of(CH, half, 0) == want)
 
     @pl.when(step == pl.num_programs(0) - 1)
@@ -82,7 +88,7 @@
             live = jnp.logical_and(ids < tail_rows, core == 0)
             logit = jnp.where(live, dot(tail_ref[...], h_ref[...], NT), -jnp.inf)
             logt_ref[:, cols] = logit
-            fold(cols, logit, jnp.logical_and(ids + core_ref[2] == tgt_ref[0:1, cols], live))
+            fold(cols, logit, jnp.logical_and(ids + tail_base == tgt_ref[0:1, cols], live))
         peak = jnp.max(top[...], axis=0, keepdims=True)
         stat_ref[...] = jnp.zeros_like(stat_ref)
         stat_ref[0:1, :] = peak
@@ -91,7 +97,8 @@
 
 
 def dh_kernel(tail_rows, inv_n, core_ref, emb_ref, log_ref, tail_ref, logt_ref, row_ref, tgt_ref, da_ref, db_ref, loss_ref, g_ref, gt_ref):
-    step, core = pl.program_id(0), core_ref[0]
+    step = pl.program_id(0)
+    core, base, tail_base = seat(2 * sum(PIECES) * CH + tail_rows)
     half = da_ref.shape[0]
 
     @pl.when(step == 0)
@@ -106,7 +113,7 @@
             cols = pl.ds(side * half, half)
             for i in range(k, k + group):
                 rows = pl.ds(i * CH, CH)
-                want = tgt_ref[0:1, cols] - (core_ref[1] + (step * STEP + i) * CH)
+                want = tgt_ref[0:1, cols] - (base + (step * STEP + i) * CH)
                 g_ref[rows, cols] = weights(log_ref[rows, cols], row_ref[0:1, cols], rows_of(CH, half, 0) == want, inv_n)
             rows = pl.ds(k * CH, group * CH)
             d_ref[...] += dot(g_ref[rows, cols], emb_ref[rows, :], TN)
@@ -118,7 +125,7 @@
             cols = pl.ds(side * half, half)
             ids = rows_of(TAIL, half, 0)
             live = jnp.logical_and(ids < tail_rows, core == 0)
-            hit = jnp.logical_and(ids + core_ref[2] == tgt_ref[0:1, cols], live)
+            hit = jnp.logical_and(ids + tail_base == tgt_ref[0:1, cols], live)
             gt_ref[:, cols] = weights(logt_ref[:, cols], row_ref[0:1, cols], hit, inv_n)
             d_ref[...] += dot(gt_ref[:, cols], tail_ref[...], TN)
 
@@ -126,7 +133,7 @@
 JOBS = {None: (0, 0), 'act': (3, 2), 'add': (2, 1)}
 
 
-def finish_kernel(norm_ref, inv_ref, scaled_ref, near_ref, far_ref, grad_ref, sum_ref, total_ref):
+def finish_kernel(norm_ref, inv_ref, loss_ref, scaled_ref, near_ref, far_ref, grad_ref, sum_ref, total_ref):
     @pl.when(pl.program_id(0) == 0)
     def _():
         total_ref[...] = jnp.zeros_like(total_ref)
@@ -136,14 +143,16 @@
     grad_scaled = grad_h * norm_ref[...]
     mean = jnp.mean(grad_scaled * scaled, axis=-1, keepdims=True)
     grad_ref[...] = inv_ref[:, 0:1] * (grad_scaled - scaled * mean)
-    sum_ref[...] = jnp.sum(total_ref[...], axis=0, keepdims=True)
+    sum_ref[0:1, :] = jnp.sum(total_ref[...], axis=0, keepdims=True)
+    sum_ref[1:2, :] = jnp.zeros((1, sum_ref.shape[1]), F32)
+    sum_ref[1:2, 0:128] = loss_ref[0:1, :]
 
 
 def rows_at(core, first, count):
     return pl.ds(pl.multiple_of((core * sum(PIECES) + first) * CH, CH), count * CH)
 
 
-def grad_kernel(job, first, count, prev, late, inv_n, core_ref, emb_ref, log_ref, ha_ref, hb_ref, hc_ref, hd_ref, row_ref, rowx_ref, mark_ref, *refs):
+def grad_kernel(job, first, count, prev, late, inv_n, emb_ref, log_ref, ha_ref, hb_ref, hc_ref, hd_ref, row_ref, rowx_ref, mark_ref, *refs):
     per_core = sum(PIECES)
     refs = list(refs)
     if prev:
@@ -153,7 +162,7 @@
     jobs_in = [refs.pop(0) for _ in range(JOBS[job][0])]
     jobs_out = [refs.pop(5) for _ in range(JOBS[job][1])]
     out_ref, emb_buf, log_buf, piece_ref, token_ref, ga_ref, gx_ref, lx_ref, emb_sem, log_sem, own_sem, got_sem = refs
-    core = core_ref[0]
+    core, start, _ = seat(out_ref.shape[0])
     half = ha_ref.shape[0]
     token_ref[...] = mark_ref[...]
 
@@ -194,7 +203,7 @@
             for copy in fetch(k + 1):
                 copy.start()
 
-        base = core_ref[1] + k * CH
+        base = start + k * CH
         for side in (0, 1):
             cols = pl.ds(side * half, half)
             want = row_ref[2:3, cols].astype(jnp.int32) - base
@@ -221,23 +230,29 @@
         copy.wait()
 
 
-def tail_kernel(inv_n, core_ref, tail_ref, ha_ref, hb_ref, hc_ref, hd_ref, row_ref, rowx_ref, _, out_ref, g_ref):
+def tail_kernel(inv_n, vocab_loc, tail_ref, ha_ref, hb_ref, hc_ref, hd_ref, row_ref, rowx_ref, *refs):
+    sums, (_, out_ref, sum_ref, loss_ref, g_ref) = refs[:4], refs[4:]
     half = ha_ref.shape[0]
+    _, _, tail_base = seat(vocab_loc)
+    both = (sums[0][...] + sums[1][...]) + (sums[2][...] + sums[3][...])
+    sum_ref[...] = both[0:1]
+    loss_ref[0, 0] = jnp.sum(both[1:2, 0:128]) * (inv_n / 256)
     grad = jnp.zeros(out_ref.shape, F32)
     ids = rows_of(TAIL, half, 0)
     for h_ref, r_ref, side in ((ha_ref, row_ref, 0), (hb_ref, row_ref, 1), (hc_ref, rowx_ref, 0), (hd_ref, rowx_ref, 1)):
         cols = pl.ds(side * half, half)
         logit = dot(tail_ref[...], h_ref[...], NT)
-        g_ref[...] = weights(logit, r_ref[0:1, cols], ids + core_ref[2] == r_ref[2:3, cols].astype(jnp.int32), inv_n)
+        g_ref[...] = weights(logit, r_ref[0:1, cols], ids + tail_base == r_ref[2:3, cols].astype(jnp.int32), inv_n)
         grad += dot(g_ref[...], h_ref[...], NN)
     out_ref[...] = grad
 
 
-def last_kernel(places, core_ref, _, *refs):
+def last_kernel(places, _, *refs):
     srcs, out_ref, sems = refs[:len(places)], refs[len(places)], refs[len(places) + 1:]
+    core, _, _ = seat(out_ref.shape[0])
     copies = []
     for src, sem, (other, place) in zip(srcs, sems, places):
-        side = 1 - core_ref[0] if other else core_ref[0]
+        side = 1 - core if other else core
         copies.append(pltpu.make_async_copy(src, out_ref.at[rows_at(side, *place)], sem))
     for copy in copies:
         copy.start()
@@ -269,10 +284,9 @@
             vocab_loc = emb_loc.shape[0]
             per_core = sum(PIECES)
             tail_rows = vocab_loc - 2 * per_core * CH
-            my_tp, my_dp = lax.axis_index('tp'), lax.axis_index('dp')
+            my_dp = lax.axis_index('dp')
             core = lax.rem(my_dp, 2)
-            start = my_tp * vocab_loc
-            core_arg = jnp.stack([core, start + core * (per_core * CH), start + 2 * per_core * CH])
+            core_arg = core.reshape(1)
             swap = [(i, i ^ 1) for i in range(n_dp)]
             cross = [(i, i ^ 2) for i in range(n_dp)]
             cross_swap = [(i, i ^ 3) for i in range(n_dp)]
@@ -346,24 +360,23 @@
             row_near, row_far, scaled_far, scaled_far_sib, dh_own, dh_sib = tie(
                 (row_near, row_far, scaled_far, scaled_far_sib, dh_own, dh_sib))
             dh_got = swapped(dh_sib, 'dp', swap)
-            loss_far = swapped(loss_chip, 'dp', cross)
 
             def piece_call(first, count, mark, out, bufs, prev, own, late, got, far, job, job_args, job_outs):
                 extra = ([] if out is None else [out, *bufs, own]) + ([] if got is None else [got]) + job_args
                 specs = ([] if out is None else [HB, VM, VM, VM]) + ([] if got is None else [VM]) + [VM] * len(job_args)
                 return pl.pallas_call(
                     functools.partial(grad_kernel, job, first, count, prev, late, inv_n),
-                    in_specs=[pl.BlockSpec(memory_space=pltpu.SMEM), HB, HB] + [VM] * 7 + specs,
+                    in_specs=[HB, HB] + [VM] * 7 + specs,
                     out_specs=[HB] + [VM] * (4 + len(job_outs)),
                     scratch_shapes=[pltpu.VMEM((CH, 2 * half), BF16), pltpu.VMEM((CH, 2 * half), BF16), pltpu.VMEM((CH, 2 * half), F32)]
                     + [pltpu.SemaphoreType.DMA] * 4,
                     out_shape=[jax.ShapeDtypeStruct((vocab_loc, d), F32), jax.ShapeDtypeStruct((2, CH, d), BF16),
                                jax.ShapeDtypeStruct((2, CH, 2 * half), F32), pltpu.VMEM((count * CH, d), F32),
                                jax.ShapeDtypeStruct((8, 128), F32)] + job_outs,
-                    input_output_aliases={} if out is None else {10: 0, 11: 1, 12: 2},
+                    input_output_aliases={} if out is None else {9: 0, 10: 1, 11: 2},
                     compiler_params=params(8 if job is None else 10),
                     cost_estimate=cost(flops_unit * count * 6, count * CH * (2 * d + 8 * half + 8 * d)),
-                )(core_arg, emb_loc, logits, ha, hb, *far, row_near, row_far, mark, *extra)
+                )(emb_loc, logits, ha, hb, *far, row_near, row_far, mark, *extra)
 
             out, bufs, first, own, prev, arrived = None, (), 0, None, None, []
             mark = jnp.zeros((8, 128), F32)
@@ -386,7 +399,6 @@
                 if k == 0:
                     far = made
                 if k == ADD_AT:
-                    loss_far, mark = tie((loss_far, mark))
                     dh_chip, mark = tie((made[0], mark))
                     dh_far = swapped(dh_chip, 'tp', flip)
                 if k == FINISH_AT:
@@ -395,41 +407,38 @@
                     grad_r, grad_w = pl.pallas_call(
                         finish_kernel,
                         grid=(4,),
-                        in_specs=[VM, pl.BlockSpec((half // 4, 128), lambda i: (i, 0)), blk_rows, blk_rows, blk_rows],
+                        in_specs=[VM, pl.BlockSpec((half // 4, 128), lambda i: (i, 0)), VM, blk_rows, blk_rows, blk_rows],
                         out_specs=[blk_rows, VM],
                         scratch_shapes=[pltpu.VMEM((8, d), F32)],
-                        out_shape=[jax.ShapeDtypeStruct((half, d), F32), jax.ShapeDtypeStruct((1, d), F32)],
+                        out_shape=[jax.ShapeDtypeStruct((half, d), F32), jax.ShapeDtypeStruct((2, d), F32)],
                         compiler_params=params(8),
                         cost_estimate=cost(1e7, half * d * 16),
-                    )(norm_row, inv_rms, scaled, dh_chip, dh_far)
+                    )(norm_row, inv_rms, loss_chip, scaled, dh_chip, dh_far)
                     grad_w, mark = tie((grad_w, mark))
                     gw = [swapped(grad_w, 'dp', swap), swapped(grad_w, 'dp', cross), swapped(grad_w, 'dp', cross_swap)]
-            loss_mean = ((loss_chip + loss_far) * inv_n)[0, 0]
-            grad_w = ((grad_w + gw[0]) + (gw[1] + gw[2])).reshape(d)
             hc, hd = far
 
-            out = pl.pallas_call(
-                functools.partial(tail_kernel, inv_n),
-                grid_spec=pltpu.PrefetchScalarGridSpec(
-                    num_scalar_prefetch=1, grid=(1,), in_specs=[VM] * 7 + [HB],
-                    out_specs=pl.BlockSpec((TAIL, d), lambda i, c: (2 * per_core * CH // TAIL, 0)),
-                    scratch_shapes=[pltpu.VMEM((TAIL, half), BF16)]),
-                out_shape=jax.ShapeDtypeStruct((vocab_loc, d), F32),
-                input_output_aliases={8: 0},
+            out, grad_w, loss_mean = pl.pallas_call(
+                functools.partial(tail_kernel, inv_n, vocab_loc),
+                grid=(1,), in_specs=[VM] * 11 + [HB],
+                out_specs=[pl.BlockSpec((TAIL, d), lambda i: (2 * per_core * CH // TAIL, 0)), VM, pl.BlockSpec(memory_space=pltpu.SMEM)],
+                scratch_shapes=[pltpu.VMEM((TAIL, half), BF16)],
+                out_shape=[jax.ShapeDtypeStruct((vocab_loc, d), F32), jax.ShapeDtypeStruct((1, d), F32), jax.ShapeDtypeStruct((1, 1), F32)],
+                input_output_aliases={11: 0},
                 compiler_params=params(14),
                 cost_estimate=cost(2.0 * TAIL * d * half * 8, 4 * TAIL * d),
-            )(core_arg, emb_tail, ha, hb, hc, hd, row_near, row_far, out)
+            )(emb_tail, ha, hb, hc, hd, row_near, row_far, grad_w, *gw, out)
             for parts in ([(False, prev, own), (True, *arrived[-2])], [(True, *arrived[-1])]):
                 out = pl.pallas_call(
                     functools.partial(last_kernel, [p[:2] for p in parts]),
-                    in_specs=[pl.BlockSpec(memory_space=pltpu.SMEM), HB] + [VM] * len(parts), out_specs=HB,
+                    in_specs=[HB] + [VM] * len(parts), out_specs=HB,
                     scratch_shapes=[pltpu.SemaphoreType.DMA] * len(parts),
                     out_shape=jax.ShapeDtypeStruct((vocab_loc, d), F32),
-                    input_output_aliases={1: 0},
+                    input_output_aliases={0: 0},
                     compiler_params=params(8),
                     cost_estimate=cost(1e6, sum(4 * p[1][1] * CH * d for p in parts)),
-                )(core_arg, out, *[p[2] for p in parts])
-            return loss_mean, grad_r.reshape(n_batch, n_seq, d), out, grad_w
+                )(out, *[p[2] for p in parts])
+            return loss_mean.reshape(()), grad_r.reshape(n_batch, n_seq, d), out, grad_w.reshape(d)
 
         sharded = jax.shard_map(
             local_part, mesh=mesh,

time: 300 us -> 288 us (0.960)
  Pallas kernels: 208 us -> 201 us
    pallas_call x10, Pallas kernels: 115 us -> 111 us  [piece_call(): pl.pallas_call(functools.partial(grad_kernel, job, first, count, prev, la...]
    ppermute x9 -> x8, waiting for transfers between devices: 64.3 us -> 62.6 us  [swapped(): return lax.ppermute(value, axis, perm)]
    ppermute x9 -> x8, starting transfers between devices: 7.25 us -> 6.73 us  [swapped(): return lax.ppermute(value, axis, perm)]
  transfers between devices with their start and end apart: 24 -> 23, of which waited for: 6 -> 5; matrix products, arithmetic and copies ran while one was open for 1% -> 1% of each run, Pallas kernels for 64% -> 64%
where the time goes in v5:
time: 288 us; the launch traced here: 287 us
  Pallas kernels  201 us (70%)
  waiting for transfers between devices  66.4 us (23%)
  starting transfers between devices  12.8 us (4%)
  local copies, waits for them, and re-layouts  5.81 us (2%)
    pallas_call x10, Pallas kernels, piece_call(): pl.pallas_call(functools.partial(grad_kernel, job, first, count, prev, la...  111 us
    ppermute x8, waiting for transfers between devices, swapped(): return lax.ppermute(value, axis, perm)  62.6 us
    pallas_call x1, Pallas kernels, local_part(): pl.pallas_call(functools.partial(stats_kernel, tail_rows), grid_spec=pltp...  44.4 us
    pallas_call x1, Pallas kernels, local_part(): pl.pallas_call(functools.partial(dh_kernel, tail_rows, inv_n), grid_spec=...  35.2 us
    ppermute x8, starting transfers between devices, swapped(): return lax.ppermute(value, axis, perm)  6.73 us
  transfers between devices with their start and end apart: 23, of which 5 were waited for; matrix products, arithmetic and copies ran while one was open for 1% of the time, Pallas kernels for 64%

profile of v5, /device:TPU:0, one launch (start us, length us, event | category | flops | bytes accessed | tf_op | source)
XLA Modules:
  0.0 286.9 jit_solution(17726755762156757445)
XLA Ops:
  0.6 1.6 copy-done
  2.2 1.2 copy-done.3
  3.5 0.7 copy-done.4
  4.1 0.7 shard_map.84
  4.9 0.9 collective-permute-start
  5.7 2.5 collective-permute-start.5
  8.4 0.7 constant_dynamic-update-slice_fusion.1
  9.1 0.9 slice.61
  10.7 44.4 %shard_map.85 = (f32[12544,1024]{1,0:T(8,128)}, f32[64,1024]{1,0:T(8,128)S(1)}, f32[8,1024]{1,0:T(8,128)S(1)}, bf16[512,1024]{1,0:T(8,128)(2,1)S(1)}) custom-call(s32[1]{0:T(128)} %bitcast.3.core_ref, bf16[25140,1024]{1,0:T(8,128)(2,1)} %emb_ref.23, bf16[64,1024]{1,0:T(8,128)(2,1)S(1)} %pad.8.tail_ref, ...), custom_call_target="tpu_custom_call" | custom-call | flops 26306674688 | bytes 77070336 | tf_op jit(solution)/shard_map/pallas_call | solution.py:316
  55.4 2.3 collective-permute-start.4
  57.8 1.4 collective-permute-done.4
  59.2 2.3 collective-permute-done.3
  61.6 1.5 collective-permute-start.6
  63.1 35.2 %shard_map.86 = (f32[512,1024]{1,0:T(8,128)S(1)}, f32[512,1024]{1,0:T(8,128)S(1)}, f32[8,128]{1,0:T(8,128)S(1)}) custom-call(s32[1]{0:T(128)} %bitcast.3.core_ref, bf16[25140,1024]{1,0:T(8,128)(2,1)} %emb_ref.23, f32[12544,1024]{1,0:T(8,128)} %get-tuple-element.88.log_ref, bf16[64,1024]{1,0:T(8,128)(2,1)S(1)} %pad.8.tail_ref, ...), custom_call_target="tpu_custom_call" | custom-call | flops 26306674688 | bytes 77070336 | tf_op jit(solution)/shard_map/pallas_call | solution.py:346
  98.4 15.1 %shard_map.87 = (f32[25140,1024]{1,0:T(8,128)}, bf16[2,256,1024]{2,1,0:T(8,128)(2,1)S(1)}, f32[2,256,1024]{2,1,0:T(8,128)S(1)}, f32[1536,1024]{1,0:T(8,128)S(1)}...) custom-call(bf16[25140,1024]{1,0:T(8,128)(2,1)} %emb_ref.23, ...), custom_call_target="tpu_custom_call" | custom-call | flops 9663676416 | bytes 22020096 | tf_op jit(solution)/shard_map/pallas_call | solution.py:367
  114.1 12.6 %collective-permute-done.8.refs_5_ = f32[512,1024]{1,0:T(8,128)S(1)} collective-permute-done((f32[512,1024]{1,0:T(8,128)S(1)}, f32[512,1024]{1,0:T(8,128)S(1)}, u32[]{:S(2)}, u32[]{:S(2)}) %collective-permute-start.8) | collective-permute-done | bytes 2097184 | tf_op jit(solution)/shard_map/ppermute | solution.py:272
  126.7 12.7 %shard_map.88 = (f32[25140,1024]{1,0:T(8,128)}, bf16[2,256,1024]{2,1,0:T(8,128)(2,1)S(1)}, f32[2,256,1024]{2,1,0:T(8,128)S(1)}, f32[1536,1024]{1,0:T(8,128)S(1)}...) custom-call(bf16[25140,1024]{1,0:T(8,128)(2,1)} %emb_ref.23, ...), custom_call_target="tpu_custom_call", output_to_operand_aliasing={{0}: (9, {}), {1}: (10, {}), {2}: (11, {})} | custom-call | flops 9663676416 | bytes 22020096 | tf_op jit(solution)/shard_map/pallas_call | solution.py:367
  139.6 12.9 %shard_map.89 = (f32[25140,1024]{1,0:T(8,128)}, bf16[2,256,1024]{2,1,0:T(8,128)(2,1)S(1)}, f32[2,256,1024]{2,1,0:T(8,128)S(1)}, f32[1536,1024]{1,0:T(8,128)S(1)}, f32[8,128]{1,0:T(8,128)S(1)}) custom-call(bf16[25140,1024]{1,0:T(8,128)(2,1)} %emb_ref.23, ...), custom_call_target="tpu_custom_call", output_to_operand_aliasing={{0}: (9, {}), {1}: (10, {}), {2}: (11, {})} | custom-call | flops 9663676416 | bytes 22020096 | tf_op jit(solution)/shard_map/pallas_call | solution.py:367
  152.9 10.9 %shard_map.90 = (f32[25140,1024]{1,0:T(8,128)}, bf16[2,256,1024]{2,1,0:T(8,128)(2,1)S(1)}, f32[2,256,1024]{2,1,0:T(8,128)S(1)}, f32[1280,1024]{1,0:T(8,128)S(1)}, f32[8,128]{1,0:T(8,128)S(1)}) custom-call(bf16[25140,1024]{1,0:T(8,128)(2,1)} %emb_ref.23, ...), custom_call_target="tpu_custom_call", output_to_operand_aliasing={{0}: (9, {}), {1}: (10, {}), {2}: (11, {})} | custom-call | flops 8053063680 | bytes 18350080 | tf_op jit(solution)/shard_map/pallas_call | solution.py:367
  164.0 10.9 %shard_map.91 = (f32[25140,1024]{1,0:T(8,128)}, bf16[2,256,1024]{2,1,0:T(8,128)(2,1)S(1)}, f32[2,256,1024]{2,1,0:T(8,128)S(1)}, f32[1280,1024]{1,0:T(8,128)S(1)}, f32[8,128]{1,0:T(8,128)S(1)}) custom-call(bf16[25140,1024]{1,0:T(8,128)(2,1)} %emb_ref.23, ...), custom_call_target="tpu_custom_call", output_to_operand_aliasing={{0}: (9, {}), {1}: (10, {}), {2}: (11, {})} | custom-call | flops 8053063680 | bytes 18350080 | tf_op jit(solution)/shard_map/pallas_call | solution.py:367
  175.3 12.0 %shard_map.92 = (f32[25140,1024]{1,0:T(8,128)}, bf16[2,256,1024]{2,1,0:T(8,128)(2,1)S(1)}, f32[2,256,1024]{2,1,0:T(8,128)S(1)}, f32[1280,1024]{1,0:T(8,128)S(1)}, f32[8,128]{1,0:T(8,128)S(1)}) custom-call(bf16[25140,1024]{1,0:T(8,128)(2,1)} %emb_ref.23, ...), custom_call_target="tpu_custom_call", output_to_operand_aliasing={{0}: (9, {}), {1}: (10, {}), {2}: (11, {})} | custom-call | flops 8053063680 | bytes 18350080 | tf_op jit(solution)/shard_map/pallas_call | solution.py:367
  188.1 47.3 %collective-permute-done.9.far_ref = f32[512,1024]{1,0:T(8,128)S(1)} collective-permute-done((f32[512,1024]{1,0:T(8,128)S(1)}, f32[512,1024]{1,0:T(8,128)S(1)}, u32[]{:S(2)}, u32[]{:S(2)}) %collective-permute-start.9) | collective-permute-done | bytes 2097184 | tf_op jit(solution)/shard_map/ppermute | solution.py:272
  235.4 2.4 shard_map.93
  237.8 10.9 %shard_map.94 = (f32[25140,1024]{1,0:T(8,128)}, bf16[2,256,1024]{2,1,0:T(8,128)(2,1)S(1)}, f32[2,256,1024]{2,1,0:T(8,128)S(1)}, f32[1280,1024]{1,0:T(8,128)S(1)}, f32[8,128]{1,0:T(8,128)S(1)}) custom-call(bf16[25140,1024]{1,0:T(8,128)(2,1)} %emb_ref.23, ...), custom_call_target="tpu_custom_call", output_to_operand_aliasing={{0}: (9, {}), {1}: (10, {}), {2}: (11, {})} | custom-call | flops 8053063680 | bytes 18350080 | tf_op jit(solution)/shard_map/pallas_call | solution.py:367
  248.8 11.2 %shard_map.95 = (f32[25140,1024]{1,0:T(8,128)}, bf16[2,256,1024]{2,1,0:T(8,128)(2,1)S(1)}, f32[2,256,1024]{2,1,0:T(8,128)S(1)}, f32[1280,1024]{1,0:T(8,128)S(1)}, f32[8,128]{1,0:T(8,128)S(1)}) custom-call(bf16[25140,1024]{1,0:T(8,128)(2,1)} %emb_ref.23, ...), custom_call_target="tpu_custom_call", output_to_operand_aliasing={{0}: (9, {}), {1}: (10, {}), {2}: (11, {})} | custom-call | flops 8053063680 | bytes 18350080 | tf_op jit(solution)/shard_map/pallas_call | solution.py:367
  260.3 9.0 %shard_map.96 = (f32[25140,1024]{1,0:T(8,128)}, bf16[2,256,1024]{2,1,0:T(8,128)(2,1)S(1)}, f32[2,256,1024]{2,1,0:T(8,128)S(1)}, f32[1024,1024]{1,0:T(8,128)S(1)}, f32[8,128]{1,0:T(8,128)S(1)}) custom-call(bf16[25140,1024]{1,0:T(8,128)(2,1)} %emb_ref.23, ...), custom_call_target="tpu_custom_call", output_to_operand_aliasing={{0}: (9, {}), {1}: (10, {}), {2}: (11, {})} | custom-call | flops 6442450944 | bytes 14680064 | tf_op jit(solution)/shard_map/pallas_call | solution.py:367
  269.6 5.1 %shard_map.97 = (f32[25140,1024]{1,0:T(8,128)}, bf16[2,256,1024]{2,1,0:T(8,128)(2,1)S(1)}, f32[2,256,1024]{2,1,0:T(8,128)S(1)}, f32[512,1024]{1,0:T(8,128)S(1)}, f32[8,128]{1,0:T(8,128)}) custom-call(bf16[25140,1024]{1,0:T(8,128)(2,1)} %emb_ref.23, ...), custom_call_target="tpu_custom_call", output_to_operand_aliasing={{0}: (9, {}), {1}: (10, {}), {2}: (11, {})} | custom-call | flops 3221225472 | bytes 7340032 | tf_op jit(solution)/shard_map/pallas_call | solution.py:367
  275.8 1.1 collective-permute-start.16
  276.8 2.6 collective-permute-done.14.refs_1_
  279.5 3.1 %shard_map.98 = (f32[25140,1024]{1,0:T(8,128)}, f32[1,1024]{1,0:T(1,128)}, f32[1,1]{1,0:T(1,128)}) custom-call(bf16[64,1024]{1,0:T(8,128)(2,1)S(1)} %pad.8.tail_ref, bf16[512,1024]{1,0:T(8,128)(2,1)S(1)} %get-tuple-element.85.ha_ref.hc_ref, bf16[512,1024]{1,0:T(8,128)(2,1)S(1)} %get-tuple-element.87.hb_ref.hd_ref, ...), custom_call_target="tpu_custom_call", output_to_operand_aliasing={{0}: (11, {})} | custom-call | flops 536870912 | bytes 262144 | tf_op jit(solution)/shard_map/pallas_call | solution.py:421
  282.6 2.7 shard_map.99._
  285.4 1.3 shard_map.100
  (57 shorter events, 5.5 us)
Async XLA Ops:
  0.6 1.6 copy-start
  2.2 1.2 copy-start.3
  3.4 0.7 copy-start.4
  4.8 50.3 %copy-start.1 = (f32[512,1024]{1,0:T(8,128)}, f32[512,1024]{1,0:T(8,128)S(1)}, u32[]{:S(2)}) copy-start(f32[512,1024]{1,0:T(8,128)S(1)} %get-tuple-element.86.scaled_ref) | copy-start | bytes 6291460
  4.9 5.2 %collective-permute-start = (f32[512,1024]{1,0:T(8,128)S(1)}, f32[512,1024]{1,0:T(8,128)}, u32[]{:S(2)}, u32[]{:S(2)}) collective-permute-start(f32[512,1024]{1,0:T(8,128)S(1)} %get-tuple-element.86.scaled_ref), channel_id=1, source_target_pairs={{0,1},{1,0},{2,3},{3,2},{4,5},{5,4},{6,7},{7,6}} | collective-permute-start | bytes 6291464 | tf_op jit(solution)/shard_map/ppermute | solution.py:308
  5.7 55.9 %collective-permute-start.5 = (f32[512,1024]{1,0:T(8,128)S(1)}, f32[512,1024]{1,0:T(8,128)}, u32[]{:S(2)}, u32[]{:S(2)}) collective-permute-start(f32[512,1024]{1,0:T(8,128)S(1)} %get-tuple-element.86.scaled_ref), channel_id=1, source_target_pairs={{0,2},{1,3},{2,0},{3,1},{4,6},{5,7},{6,4},{7,5}} | collective-permute-start | bytes 6291464 | tf_op jit(solution)/shard_map/ppermute | solution.py:272
  8.2 1.8 collective-permute-start.1
  10.1 0.7 copy-start.5
  55.1 2.7 collective-permute-start.2
  55.4 3.7 %collective-permute-start.4 = (f32[3,1024]{1,0:T(4,128)S(1)}, f32[3,1024]{1,0:T(4,128)S(1)}, u32[]{:S(2)}, u32[]{:S(2)}) collective-permute-start(f32[3,1024]{1,0:T(4,128)S(1)} %slice.64), channel_id=1, source_target_pairs={{0,5},{1,4},{2,7},{3,6},{4,1},{5,0},{6,3},{7,2}} | collective-permute-start | bytes 36872 | tf_op jit(solution)/shard_map/ppermute | solution.py:335
  57.7 3.7 %collective-permute-start.3 = (f32[3,1024]{1,0:T(4,128)S(1)}, f32[3,1024]{1,0:T(4,128)S(1)}, u32[]{:S(2)}, u32[]{:S(2)}) collective-permute-start(f32[3,1024]{1,0:T(4,128)S(1)} %slice.64), channel_id=1, source_target_pairs={{0,4},{4,0},{1,5},{5,1},{2,6},{6,2},{3,7},{7,3}} | collective-permute-start | bytes 36872 | tf_op jit(solution)/shard_map/ppermute | solution.py:334
  61.6 36.8 %collective-permute-start.7 = (f32[512,1024]{1,0:T(8,128)}, f32[512,1024]{1,0:T(8,128)S(1)}, u32[]{:S(2)}, u32[]{:S(2)}) collective-permute-start(f32[512,1024]{1,0:T(8,128)} %collective-permute-done.5.refs_1_), channel_id=1, source_target_pairs={{0,1},{1,0},{2,3},{3,2},{4,5},{5,4},{6,7},{7,6}} | collective-permute-start | bytes 6291464 | tf_op jit(solution)/shard_map/ppermute | solution.py:272
  61.6 36.7 %collective-permute-start.6 = (f32[8,1024]{1,0:T(8,128)S(1)}, f32[8,1024]{1,0:T(8,128)S(1)}, u32[]{:S(2)}, u32[]{:S(2)}) collective-permute-start(f32[8,1024]{1,0:T(8,128)S(1)} %select_maximum_fusion.row_ref), channel_id=1, source_target_pairs={{0,2},{1,3},{2,0},{3,1},{4,6},{5,7},{6,4},{7,5}} | collective-permute-start | bytes 98312 | tf_op jit(solution)/shard_map/ppermute | solution.py:272
  113.5 26.1 %collective-permute-start.10 = (f32[1536,1024]{1,0:T(8,128)S(1)}, f32[1536,1024]{1,0:T(8,128)S(1)}, u32[]{:S(2)}, u32[]{:S(2)}) collective-permute-start(f32[1536,1024]{1,0:T(8,128)S(1)} %get-tuple-element.109.refs_3_), channel_id=1, source_target_pairs={{0,1},{1,0},{2,3},{3,2},{4,5},{5,4},{6,7},{7,6}} | collective-permute-start | bytes 18874376 | tf_op jit(solution)/shard_map/ppermute | solution.py:397
  113.7 13.0 %collective-permute-start.8 = (f32[512,1024]{1,0:T(8,128)S(1)}, f32[512,1024]{1,0:T(8,128)S(1)}, u32[]{:S(2)}, u32[]{:S(2)}) collective-permute-start(f32[512,1024]{1,0:T(8,128)S(1)} %get-tuple-element.103), channel_id=1, source_target_pairs={{0,1},{1,0},{2,3},{3,2},{4,5},{5,4},{6,7},{7,6}} | collective-permute-start | bytes 6291464 | tf_op jit(solution)/shard_map/ppermute | solution.py:272
  139.4 13.5 %collective-permute-start.11 = (f32[1536,1024]{1,0:T(8,128)S(1)}, f32[1536,1024]{1,0:T(8,128)S(1)}, u32[]{:S(2)}, u32[]{:S(2)}) collective-permute-start(f32[1536,1024]{1,0:T(8,128)S(1)} %get-tuple-element.119.refs_3_), channel_id=1, source_target_pairs={{0,1},{1,0},{2,3},{3,2},{4,5},{5,4},{6,7},{7,6}} | collective-permute-start | bytes 18874376 | tf_op jit(solution)/shard_map/ppermute | solution.py:397
  152.5 11.5 %collective-permute-start.12 = (f32[1536,1024]{1,0:T(8,128)S(1)}, f32[1536,1024]{1,0:T(8,128)S(1)}, u32[]{:S(2)}, u32[]{:S(2)}) collective-permute-start(f32[1536,1024]{1,0:T(8,128)S(1)} %get-tuple-element.124.refs_3_), channel_id=1, source_target_pairs={{0,1},{1,0},{2,3},{3,2},{4,5},{5,4},{6,7},{7,6}} | collective-permute-start | bytes 18874376 | tf_op jit(solution)/shard_map/ppermute | solution.py:397
  163.8 11.5 %collective-permute-start.13 = (f32[1280,1024]{1,0:T(8,128)S(1)}, f32[1280,1024]{1,0:T(8,128)S(1)}, u32[]{:S(2)}, u32[]{:S(2)}) collective-permute-start(f32[1280,1024]{1,0:T(8,128)S(1)} %get-tuple-element.129.refs_3_), channel_id=1, source_target_pairs={{0,1},{1,0},{2,3},{3,2},{4,5},{5,4},{6,7},{7,6}} | collective-permute-start | bytes 15728648 | tf_op jit(solution)/shard_map/ppermute | solution.py:397
  175.0 62.9 %collective-permute-start.17 = (f32[1280,1024]{1,0:T(8,128)S(1)}, f32[1280,1024]{1,0:T(8,128)S(1)}, u32[]{:S(2)}, u32[]{:S(2)}) collective-permute-start(f32[1280,1024]{1,0:T(8,128)S(1)} %get-tuple-element.134.refs_3_), channel_id=1, source_target_pairs={{0,1},{1,0},{2,3},{3,2},{4,5},{5,4},{6,7},{7,6}} | collective-permute-start | bytes 15728648 | tf_op jit(solution)/shard_map/ppermute | solution.py:397
  175.3 60.1 %copy-start.2 = (f32[512,1024]{1,0:T(8,128)S(1)}, f32[512,1024]{1,0:T(8,128)}, u32[]{:S(2)}) copy-start(f32[512,1024]{1,0:T(8,128)} %copy-done.1) | copy-start | bytes 6291460
  175.3 60.1 %copy-start.6 = (f32[1024]{0:T(1024)S(1)}, f32[1024]{0:T(1024)}, u32[]{:S(2)}) copy-start(f32[1024]{0:T(1024)} %param.9) | copy-start | bytes 12292
  187.4 61.5 %collective-permute-start.18 = (f32[1280,1024]{1,0:T(8,128)S(1)}, f32[1280,1024]{1,0:T(8,128)S(1)}, u32[]{:S(2)}, u32[]{:S(2)}) collective-permute-start(f32[1280,1024]{1,0:T(8,128)S(1)} %get-tuple-element.144.refs_3_), channel_id=1, source_target_pairs={{0,1},{1,0},{2,3},{3,2},{4,5},{5,4},{6,7},{7,6}} | collective-permute-start | bytes 15728648 | tf_op jit(solution)/shard_map/ppermute | solution.py:397
  187.6 47.9 %collective-permute-start.9 = (f32[512,1024]{1,0:T(8,128)S(1)}, f32[512,1024]{1,0:T(8,128)S(1)}, u32[]{:S(2)}, u32[]{:S(2)}) collective-permute-start(f32[512,1024]{1,0:T(8,128)S(1)} %get-tuple-element.114.near_ref), channel_id=1, source_target_pairs={{0,4},{4,0},{1,5},{5,1},{2,6},{6,2},{3,7},{7,3}} | collective-permute-start | bytes 6291464 | tf_op jit(solution)/shard_map/ppermute | solution.py:272
  248.8 11.5 %collective-permute-start.19 = (f32[1280,1024]{1,0:T(8,128)S(1)}, f32[1280,1024]{1,0:T(8,128)S(1)}, u32[]{:S(2)}, u32[]{:S(2)}) collective-permute-start(f32[1280,1024]{1,0:T(8,128)S(1)} %get-tuple-element.149.refs_3_), channel_id=1, source_target_pairs={{0,1},{1,0},{2,3},{3,2},{4,5},{5,4},{6,7},{7,6}} | collective-permute-start | bytes 15728648 | tf_op jit(solution)/shard_map/ppermute | solution.py:397
  260.0 9.6 %collective-permute-start.20 = (f32[1280,1024]{1,0:T(8,128)S(1)}, f32[1280,1024]{1,0:T(8,128)S(1)}, u32[]{:S(2)}, u32[]{:S(2)}) collective-permute-start(f32[1280,1024]{1,0:T(8,128)S(1)} %get-tuple-element.154.refs_3_), channel_id=1, source_target_pairs={{0,1},{1,0},{2,3},{3,2},{4,5},{5,4},{6,7},{7,6}} | collective-permute-start | bytes 15728648 | tf_op jit(solution)/shard_map/ppermute | solution.py:397
  269.3 13.3 %collective-permute-start.21 = (f32[1024,1024]{1,0:T(8,128)S(1)}, f32[1024,1024]{1,0:T(8,128)S(1)}, u32[]{:S(2)}, u32[]{:S(2)}) collective-permute-start(f32[1024,1024]{1,0:T(8,128)S(1)} %get-tuple-element.159.refs_3_), channel_id=1, source_target_pairs={{0,1},{1,0},{2,3},{3,2},{4,5},{5,4},{6,7},{7,6}} | collective-permute-start | bytes 12582920 | tf_op jit(solution)/shard_map/ppermute | solution.py:397
  274.7 10.6 %collective-permute-start.22 = (f32[512,1024]{1,0:T(8,128)S(1)}, f32[512,1024]{1,0:T(8,128)S(1)}, u32[]{:S(2)}, u32[]{:S(2)}) collective-permute-start(f32[512,1024]{1,0:T(8,128)S(1)} %get-tuple-element.164.refs_0_), channel_id=1, source_target_pairs={{0,1},{1,0},{2,3},{3,2},{4,5},{5,4},{6,7},{7,6}} | collective-permute-start | bytes 6291464 | tf_op jit(solution)/shard_map/ppermute | solution.py:397
  275.0 4.5 %collective-permute-start.14 = (f32[2,1024]{1,0:T(2,128)S(1)}, f32[2,1024]{1,0:T(2,128)S(1)}, u32[]{:S(2)}, u32[]{:S(2)}) collective-permute-start(f32[2,1024]{1,0:T(2,128)S(1)} %get-tuple-element.139.refs_0_), channel_id=1, source_target_pairs={{0,1},{1,0},{2,3},{3,2},{4,5},{5,4},{6,7},{7,6}} | collective-permute-start | bytes 24584 | tf_op jit(solution)/shard_map/ppermute | solution.py:272
  275.2 4.2 %collective-permute-start.15 = (f32[2,1024]{1,0:T(2,128)S(1)}, f32[2,1024]{1,0:T(2,128)S(1)}, u32[]{:S(2)}, u32[]{:S(2)}) collective-permute-start(f32[2,1024]{1,0:T(2,128)S(1)} %get-tuple-element.139.refs_0_), channel_id=1, source_target_pairs={{0,2},{1,3},{2,0},{3,1},{4,6},{5,7},{6,4},{7,5}} | collective-permute-start | bytes 24584 | tf_op jit(solution)/shard_map/ppermute | solution.py:272
  275.8 3.7 %collective-permute-start.16 = (f32[2,1024]{1,0:T(2,128)S(1)}, f32[2,1024]{1,0:T(2,128)S(1)}, u32[]{:S(2)}, u32[]{:S(2)}) collective-permute-start(f32[2,1024]{1,0:T(2,128)S(1)} %get-tuple-element.139.refs_0_), channel_id=1, source_target_pairs={{0,3},{1,2},{2,1},{3,0},{4,7},{5,6},{6,5},{7,4}} | collective-permute-start | bytes 24584 | tf_op jit(solution)/shard_map/ppermute | solution.py:272

commit v6 on v5

--- a/solution.py
+++ b/solution.py
@@ -12,7 +12,7 @@
 CH = 256
 STEP = 7
 GROUPS = (1, 2, 2, 2)
-PIECES = (6, 6, 6, 5, 5, 5, 5, 5, 4, 2)
+PIECES = (5, 6, 5, 6, 5, 6, 5, 5, 4, 2)
 ADD_AT, FINISH_AT = 1, 5
 TAIL = 64
 F32, BF16 = jnp.float32, jnp.bfloat16
@@ -52,7 +52,7 @@
     inv_ref[...] = jnp.broadcast_to(inv, inv_ref.shape)
 
 
-def stats_kernel(tail_rows, core_ref, emb_ref, tail_ref, ha_ref, sib_ref, norm_ref, tgt_ref, log_ref, logt_ref, stat_ref, hb_ref, top, total, hits):
+def stats_kernel(tail_rows, core_ref, emb_ref, tail_ref, ha_ref, sib_ref, norm_ref, tgt_ref, log_ref, logt_ref, stat_ref, hb_ref, top, total, hits, wa_ref, wb_ref):
     step = pl.program_id(0)
     core, base, tail_base = seat(2 * sum(PIECES) * CH + tail_rows)
     half = ha_ref.shape[0]
@@ -63,6 +63,8 @@
         total[...] = jnp.zeros_like(total)
         hits[...] = jnp.zeros_like(hits)
         hb_ref[...] = (sib_ref[...] * norm_ref[...]).astype(BF16)
+        wa_ref[...] = ha_ref[...].T
+        wb_ref[...] = hb_ref[...].T
 
     def fold(cols, logit, hit):
         split = logit.reshape(-1, 8, half)
@@ -73,20 +75,20 @@
 
     for k in range(STEP):
         rows = pl.ds(k * CH, CH)
-        for side, h_ref in ((0, ha_ref), (1, hb_ref)):
-            cols = pl.ds(side * half, half)
-            logit = dot(emb_ref[rows, :], h_ref[...], NT)
+        for side, h_ref in ((0, wa_ref), (1, wb_ref)):
+            cols = pl.ds(side * half, half)
+            logit = dot(emb_ref[rows, :], h_ref[...], NN)
             log_ref[rows, cols] = logit
             want = tgt_ref[0:1, cols] - (base + (step * STEP + k) * CH)
             fold(cols, logit, rows_of(CH, half, 0) == want)
 
     @pl.when(step == pl.num_programs(0) - 1)
     def _():
-        for side, h_ref in ((0, ha_ref), (1, hb_ref)):
+        for side, h_ref in ((0, wa_ref), (1, wb_ref)):
             cols = pl.ds(side * half, half)
             ids = rows_of(TAIL, half, 0)
             live = jnp.logical_and(ids < tail_rows, core == 0)
-            logit = jnp.where(live, dot(tail_ref[...], h_ref[...], NT), -jnp.inf)
+            logit = jnp.where(live, dot(tail_ref[...], h_ref[...], NN), -jnp.inf)
             logt_ref[:, cols] = logit
             fold(cols, logit, jnp.logical_and(ids + tail_base == tgt_ref[0:1, cols], live))
         peak = jnp.max(top[...], axis=0, keepdims=True)
@@ -130,7 +132,7 @@
             d_ref[...] += dot(gt_ref[:, cols], tail_ref[...], TN)
 
 
-JOBS = {None: (0, 0), 'act': (3, 2), 'add': (2, 1)}
+JOBS = {None: (0, 0), 'act': (3, 4), 'add': (2, 1)}
 
 
 def finish_kernel(norm_ref, inv_ref, loss_ref, scaled_ref, near_ref, far_ref, grad_ref, sum_ref, total_ref):
@@ -152,7 +154,7 @@
     return pl.ds(pl.multiple_of((core * sum(PIECES) + first) * CH, CH), count * CH)
 
 
-def grad_kernel(job, first, count, prev, late, inv_n, emb_ref, log_ref, ha_ref, hb_ref, hc_ref, hd_ref, row_ref, rowx_ref, mark_ref, *refs):
+def grad_kernel(job, first, count, prev, late, inv_n, emb_ref, log_ref, ha_ref, hb_ref, hc_ref, hd_ref, xc_ref, xd_ref, row_ref, rowx_ref, mark_ref, *refs):
     per_core = sum(PIECES)
     refs = list(refs)
     if prev:
@@ -180,17 +182,19 @@
     if not prev:
         for copy in fetch(jnp.int32(first)):
             copy.start()
-        for copy in fetch(jnp.int32(first)):
-            copy.wait()
     for copy in writes:
         copy.start()
     if job == 'act':
         norm_ref, *src = jobs_in
-        for src_ref, dst_ref in zip(src, jobs_out):
+        for src_ref, dst_ref, turn_ref in zip(src, jobs_out[:2], jobs_out[2:]):
             dst_ref[...] = (src_ref[...] * norm_ref[...]).astype(BF16)
-        hc_ref, hd_ref = jobs_out
+            turn_ref[...] = dst_ref[...].T
+        hc_ref, hd_ref, xc_ref, xd_ref = jobs_out
     if job == 'add':
         jobs_out[0][...] = jobs_in[0][...] + jobs_in[1][...]
+    if not prev:
+        for copy in fetch(jnp.int32(first)):
+            copy.wait()
 
     def step(i, carry):
         k = first + i
@@ -208,9 +212,9 @@
             cols = pl.ds(side * half, half)
             want = row_ref[2:3, cols].astype(jnp.int32) - base
             ga_ref[:, cols] = weights(log_buf[slot, :, cols], row_ref[0:1, cols], rows_of(CH, half, 0) == want, inv_n)
-        for side, h_ref in ((0, hc_ref), (1, hd_ref)):
-            cols = pl.ds(side * half, half)
-            lx_ref[:, cols] = dot(emb_buf[slot], h_ref[...], NT)
+        for side, h_ref in ((0, xc_ref), (1, xd_ref)):
+            cols = pl.ds(side * half, half)
+            lx_ref[:, cols] = dot(emb_buf[slot], h_ref[...], NN)
         piece_ref[rows, :] = dot(ga_ref[:, pl.ds(0, half)], ha_ref[...], NN) + dot(ga_ref[:, pl.ds(half, half)], hb_ref[...], NN)
         for side in (0, 1):
             cols = pl.ds(side * half, half)
@@ -319,7 +323,7 @@
                     num_scalar_prefetch=1, grid=(steps,),
                     in_specs=[pl.BlockSpec((blk, d), lambda i, c: (c[0] * steps + i, 0)), VM, VM, VM, VM, VM],
                     out_specs=[pl.BlockSpec((blk, 2 * half), lambda i, c: (i, 0)), VM, VM, VM],
-                    scratch_shapes=[pltpu.VMEM((8, 2 * half), F32)] * 3),
+                    scratch_shapes=[pltpu.VMEM((8, 2 * half), F32)] * 3 + [pltpu.VMEM((d, half), BF16)] * 2),
                 out_shape=[jax.ShapeDtypeStruct((per_core * CH, 2 * half), F32),
                            jax.ShapeDtypeStruct((TAIL, 2 * half), F32), jax.ShapeDtypeStruct((8, 2 * half), F32), jax.ShapeDtypeStruct((half, d), BF16)],
                 compiler_params=params(30),
@@ -366,27 +370,27 @@
                 specs = ([] if out is None else [HB, VM, VM, VM]) + ([] if got is None else [VM]) + [VM] * len(job_args)
                 return pl.pallas_call(
                     functools.partial(grad_kernel, job, first, count, prev, late, inv_n),
-                    in_specs=[HB, HB] + [VM] * 7 + specs,
+                    in_specs=[HB, HB] + [VM] * 9 + specs,
                     out_specs=[HB] + [VM] * (4 + len(job_outs)),
                     scratch_shapes=[pltpu.VMEM((CH, 2 * half), BF16), pltpu.VMEM((CH, 2 * half), BF16), pltpu.VMEM((CH, 2 * half), F32)]
                     + [pltpu.SemaphoreType.DMA] * 4,
                     out_shape=[jax.ShapeDtypeStruct((vocab_loc, d), F32), jax.ShapeDtypeStruct((2, CH, d), BF16),
                                jax.ShapeDtypeStruct((2, CH, 2 * half), F32), pltpu.VMEM((count * CH, d), F32),
                                jax.ShapeDtypeStruct((8, 128), F32)] + job_outs,
-                    input_output_aliases={} if out is None else {9: 0, 10: 1, 11: 2},
+                    input_output_aliases={} if out is None else {11: 0, 12: 1, 13: 2},
                     compiler_params=params(8 if job is None else 10),
                     cost_estimate=cost(flops_unit * count * 6, count * CH * (2 * d + 8 * half + 8 * d)),
                 )(emb_loc, logits, ha, hb, *far, row_near, row_far, mark, *extra)
 
             out, bufs, first, own, prev, arrived = None, (), 0, None, None, []
             mark = jnp.zeros((8, 128), F32)
-            far = (ha, hb)
+            far = (ha, hb, ha, hb)
             for k, count in enumerate(PIECES):
                 late, got = arrived[k - 2] if k >= 2 else (None, None)
                 job, job_args, job_outs = None, [], []
                 if k == 0:
                     job, job_args = 'act', [norm_row, scaled_far, scaled_far_sib]
-                    job_outs = [jax.ShapeDtypeStruct((half, d), BF16)] * 2
+                    job_outs = [jax.ShapeDtypeStruct((half, d), BF16)] * 2 + [jax.ShapeDtypeStruct((d, half), BF16)] * 2
                 if k == ADD_AT:
                     dh_got, mark = tie((dh_got, mark))
                     job, job_args, job_outs = 'add', [dh_own, dh_got], [jax.ShapeDtypeStruct((half, d), F32)]
@@ -403,20 +407,20 @@
                     dh_far = swapped(dh_chip, 'tp', flip)
                 if k == FINISH_AT:
                     dh_far, mark = tie((dh_far, mark))
-                    blk_rows = pl.BlockSpec((half // 4, d), lambda i: (i, 0))
+                    blk_rows = pl.BlockSpec((half // 8, d), lambda i: (i, 0))
                     grad_r, grad_w = pl.pallas_call(
                         finish_kernel,
-                        grid=(4,),
-                        in_specs=[VM, pl.BlockSpec((half // 4, 128), lambda i: (i, 0)), VM, blk_rows, blk_rows, blk_rows],
+                        grid=(8,),
+                        in_specs=[VM, pl.BlockSpec((half // 8, 128), lambda i: (i, 0)), VM, blk_rows, blk_rows, blk_rows],
                         out_specs=[blk_rows, VM],
                         scratch_shapes=[pltpu.VMEM((8, d), F32)],
                         out_shape=[jax.ShapeDtypeStruct((half, d), F32), jax.ShapeDtypeStruct((2, d), F32)],
-                        compiler_params=params(8),
+                        compiler_params=params(4),
                         cost_estimate=cost(1e7, half * d * 16),
                     )(norm_row, inv_rms, loss_chip, scaled, dh_chip, dh_far)
                     grad_w, mark = tie((grad_w, mark))
                     gw = [swapped(grad_w, 'dp', swap), swapped(grad_w, 'dp', cross), swapped(grad_w, 'dp', cross_swap)]
-            hc, hd = far
+            hc, hd = far[:2]
 
             out, grad_w, loss_mean = pl.pallas_call(
                 functools.partial(tail_kernel, inv_n, vocab_loc),
@@ -428,7 +432,7 @@
                 compiler_params=params(14),
                 cost_estimate=cost(2.0 * TAIL * d * half * 8, 4 * TAIL * d),
             )(emb_tail, ha, hb, hc, hd, row_near, row_far, grad_w, *gw, out)
-            for parts in ([(False, prev, own), (True, *arrived[-2])], [(True, *arrived[-1])]):
+            for parts in ([(False, prev, own), (True, *arrived[-2]), (True, *arrived[-1])],):
                 out = pl.pallas_call(
                     functools.partial(last_kernel, [p[:2] for p in parts]),
                     in_specs=[HB] + [VM] * len(parts), out_specs=HB,

time: 288 us -> 292 us (1.014)
  waiting for transfers between devices: 66.4 us -> 70.9 us
    ppermute x10, waiting for transfers between devices: 0.03 us -> 17.2 us  [local_part(): arrived.append((prev, lax.ppermute(piece, 'dp', swap)))]
    ppermute x8, waiting for transfers between devices: 62.6 us -> 50 us  [swapped(): return lax.ppermute(value, axis, perm)]
    pallas_call x10, Pallas kernels: 111 us -> 107 us  [piece_call(): pl.pallas_call(functools.partial(grad_kernel, job, first, count, prev, la...]
    pallas_call x1, Pallas kernels: 2.4 us -> 6.11 us  [local_part(): pl.pallas_call(finish_kernel, grid=(8,), in_specs=[VM, pl.BlockSpec((half...]
  transfers between devices with their start and end apart: 23 -> 23, of which waited for: 5 -> 5; matrix products, arithmetic and copies ran while one was open for 1% -> 1% of each run, Pallas kernels for 64% -> 63%
where the time goes in v6:
time: 292 us; the launch traced here: 291 us
  Pallas kernels  200 us (68%)
  waiting for transfers between devices  70.9 us (24%)
  starting transfers between devices  13 us (4%)
  local copies, waits for them, and re-layouts  5.8 us (2%)
    pallas_call x10, Pallas kernels, piece_call(): pl.pallas_call(functools.partial(grad_kernel, job, first, count, prev, la...  107 us
    ppermute x8, waiting for transfers between devices, swapped(): return lax.ppermute(value, axis, perm)  50 us
    pallas_call x1, Pallas kernels, local_part(): pl.pallas_call(functools.partial(stats_kernel, tail_rows), grid_spec=pltp...  43 us
    pallas_call x1, Pallas kernels, local_part(): pl.pallas_call(functools.partial(dh_kernel, tail_rows, inv_n), grid_spec=...  35.6 us
    ppermute x10, waiting for transfers between devices, local_part(): arrived.append((prev, lax.ppermute(piece, 'dp', swap)))  17.2 us
    ppermute x8, starting transfers between devices, swapped(): return lax.ppermute(value, axis, perm)  6.59 us
    pallas_call x1, Pallas kernels, local_part(): pl.pallas_call(finish_kernel, grid=(8,), in_specs=[VM, pl.BlockSpec((half...  6.11 us
  transfers between devices with their start and end apart: 23, of which 5 were waited for; matrix products, arithmetic and copies ran while one was open for 1% of the time, Pallas kernels for 63%

profile of v6, /device:TPU:0, one launch (start us, length us, event | category | flops | bytes accessed | tf_op | source)
XLA Modules:
  0.0 290.9 jit_solution(7920894110599664617)
XLA Ops:
  0.6 1.6 copy-done
  2.2 1.2 copy-done.1
  3.5 0.7 copy-done.2
  4.1 2.2 shard_map.84
  6.3 0.8 collective-permute-start
  7.1 2.5 collective-permute-start.5
  9.8 0.7 constant_dynamic-update-slice_fusion.1
  10.5 0.9 slice.61
  11.5 0.7 copy-done.3
  12.2 43.0 %shard_map.85 = (f32[12544,1024]{1,0:T(8,128)}, f32[64,1024]{1,0:T(8,128)S(1)}, f32[8,1024]{1,0:T(8,128)S(1)}, bf16[512,1024]{1,0:T(8,128)(2,1)S(1)}) custom-call(s32[1]{0:T(128)} %bitcast.3.core_ref, bf16[25140,1024]{1,0:T(8,128)(2,1)} %emb_ref.23, bf16[64,1024]{1,0:T(8,128)(2,1)S(1)} %pad.8.tail_ref, ...), custom_call_target="tpu_custom_call" | custom-call | flops 26306674688 | bytes 77070336 | tf_op jit(solution)/shard_map/pallas_call | solution.py:320
  55.5 2.5 collective-permute-start.4
  58.1 1.4 collective-permute-done.4
  59.5 2.3 collective-permute-done.3
  61.9 1.5 collective-permute-start.6
  63.4 35.6 %shard_map.86 = (f32[512,1024]{1,0:T(8,128)S(1)}, f32[512,1024]{1,0:T(8,128)S(1)}, f32[8,128]{1,0:T(8,128)S(1)}) custom-call(s32[1]{0:T(128)} %bitcast.3.core_ref, bf16[25140,1024]{1,0:T(8,128)(2,1)} %emb_ref.23, f32[12544,1024]{1,0:T(8,128)} %get-tuple-element.90.log_ref, bf16[64,1024]{1,0:T(8,128)(2,1)S(1)} %pad.8.tail_ref, ...), custom_call_target="tpu_custom_call" | custom-call | flops 26306674688 | bytes 77070336 | tf_op jit(solution)/shard_map/pallas_call | solution.py:350
  99.3 11.5 %shard_map.87 = (f32[25140,1024]{1,0:T(8,128)}, bf16[2,256,1024]{2,1,0:T(8,128)(2,1)S(1)}, f32[2,256,1024]{2,1,0:T(8,128)S(1)}, f32[1280,1024]{1,0:T(8,128)S(1)}...) custom-call(bf16[25140,1024]{1,0:T(8,128)(2,1)} %emb_ref.23, ...), custom_call_target="tpu_custom_call" | custom-call | flops 8053063680 | bytes 18350080 | tf_op jit(solution)/shard_map/pallas_call | solution.py:371
  110.9 12.3 %shard_map.88 = (f32[25140,1024]{1,0:T(8,128)}, bf16[2,256,1024]{2,1,0:T(8,128)(2,1)S(1)}, f32[2,256,1024]{2,1,0:T(8,128)S(1)}, f32[1536,1024]{1,0:T(8,128)S(1)}...) custom-call(bf16[25140,1024]{1,0:T(8,128)(2,1)} %emb_ref.23, ...), custom_call_target="tpu_custom_call", output_to_operand_aliasing={{0}: (11, {}), {1}: (12, {}), {2}: (13, {})} | custom-call | flops 9663676416 | bytes 22020096 | tf_op jit(solution)/shard_map/pallas_call | solution.py:371
  123.7 17.1 %collective-permute-done.10.refs_4_ = f32[1280,1024]{1,0:T(8,128)S(1)} collective-permute-done((f32[1280,1024]{1,0:T(8,128)S(1)}, f32[1280,1024]{1,0:T(8,128)S(1)}, u32[]{:S(2)}, u32[]{:S(2)}) %collective-permute-start.10) | collective-permute-done | bytes 5242912 | tf_op jit(solution)/shard_map/ppermute | solution.py:401
  140.9 10.8 %shard_map.89 = (f32[25140,1024]{1,0:T(8,128)}, bf16[2,256,1024]{2,1,0:T(8,128)(2,1)S(1)}, f32[2,256,1024]{2,1,0:T(8,128)S(1)}, f32[1280,1024]{1,0:T(8,128)S(1)}, f32[8,128]{1,0:T(8,128)S(1)}) custom-call(bf16[25140,1024]{1,0:T(8,128)(2,1)} %emb_ref.23, ...), custom_call_target="tpu_custom_call", output_to_operand_aliasing={{0}: (11, {}), {1}: (12, {}), {2}: (13, {})} | custom-call | flops 8053063680 | bytes 18350080 | tf_op jit(solution)/shard_map/pallas_call | solution.py:371
  152.0 12.7 %shard_map.90 = (f32[25140,1024]{1,0:T(8,128)}, bf16[2,256,1024]{2,1,0:T(8,128)(2,1)S(1)}, f32[2,256,1024]{2,1,0:T(8,128)S(1)}, f32[1536,1024]{1,0:T(8,128)S(1)}, f32[8,128]{1,0:T(8,128)S(1)}) custom-call(bf16[25140,1024]{1,0:T(8,128)(2,1)} %emb_ref.23, ...), custom_call_target="tpu_custom_call", output_to_operand_aliasing={{0}: (11, {}), {1}: (12, {}), {2}: (13, {})} | custom-call | flops 9663676416 | bytes 22020096 | tf_op jit(solution)/shard_map/pallas_call | solution.py:371
  164.9 10.8 %shard_map.91 = (f32[25140,1024]{1,0:T(8,128)}, bf16[2,256,1024]{2,1,0:T(8,128)(2,1)S(1)}, f32[2,256,1024]{2,1,0:T(8,128)S(1)}, f32[1280,1024]{1,0:T(8,128)S(1)}, f32[8,128]{1,0:T(8,128)S(1)}) custom-call(bf16[25140,1024]{1,0:T(8,128)(2,1)} %emb_ref.23, ...), custom_call_target="tpu_custom_call", output_to_operand_aliasing={{0}: (11, {}), {1}: (12, {}), {2}: (13, {})} | custom-call | flops 8053063680 | bytes 18350080 | tf_op jit(solution)/shard_map/pallas_call | solution.py:371
  176.1 12.7 %shard_map.92 = (f32[25140,1024]{1,0:T(8,128)}, bf16[2,256,1024]{2,1,0:T(8,128)(2,1)S(1)}, f32[2,256,1024]{2,1,0:T(8,128)S(1)}, f32[1536,1024]{1,0:T(8,128)S(1)}, f32[8,128]{1,0:T(8,128)S(1)}) custom-call(bf16[25140,1024]{1,0:T(8,128)(2,1)} %emb_ref.23, ...), custom_call_target="tpu_custom_call", output_to_operand_aliasing={{0}: (11, {}), {1}: (12, {}), {2}: (13, {})} | custom-call | flops 9663676416 | bytes 22020096 | tf_op jit(solution)/shard_map/pallas_call | solution.py:371
  189.5 47.3 %collective-permute-done.9.far_ref = f32[512,1024]{1,0:T(8,128)S(1)} collective-permute-done((f32[512,1024]{1,0:T(8,128)S(1)}, f32[512,1024]{1,0:T(8,128)S(1)}, u32[]{:S(2)}, u32[]{:S(2)}) %collective-permute-start.9) | collective-permute-done | bytes 2097184 | tf_op jit(solution)/shard_map/ppermute | solution.py:276
  236.8 6.1 %shard_map.93 = (f32[512,1024]{1,0:T(8,128)}, f32[2,1024]{1,0:T(2,128)S(1)}) custom-call(f32[1,1024]{1,0:T(1,128)S(1)} %bitcast.12, f32[512,128]{1,0:T(8,128)S(1)} %get-tuple-element.103.inv_ref, f32[8,128]{1,0:T(8,128)S(1)} %get-tuple-element.104.loss_ref, f32[512,1024]{1,0:T(8,128)} %get-tuple-element.88.scaled_ref, ...), custom_call_target="tpu_custom_call" | custom-call | flops 10000000 | bytes 8388608 | tf_op jit(solution)/shard_map/pallas_call | solution.py:411
  242.9 10.8 %shard_map.94 = (f32[25140,1024]{1,0:T(8,128)}, bf16[2,256,1024]{2,1,0:T(8,128)(2,1)S(1)}, f32[2,256,1024]{2,1,0:T(8,128)S(1)}, f32[1280,1024]{1,0:T(8,128)S(1)}, f32[8,128]{1,0:T(8,128)S(1)}) custom-call(bf16[25140,1024]{1,0:T(8,128)(2,1)} %emb_ref.23, ...), custom_call_target="tpu_custom_call", output_to_operand_aliasing={{0}: (11, {}), {1}: (12, {}), {2}: (13, {})} | custom-call | flops 8053063680 | bytes 18350080 | tf_op jit(solution)/shard_map/pallas_call | solution.py:371
  253.8 11.0 %shard_map.95 = (f32[25140,1024]{1,0:T(8,128)}, bf16[2,256,1024]{2,1,0:T(8,128)(2,1)S(1)}, f32[2,256,1024]{2,1,0:T(8,128)S(1)}, f32[1280,1024]{1,0:T(8,128)S(1)}, f32[8,128]{1,0:T(8,128)S(1)}) custom-call(bf16[25140,1024]{1,0:T(8,128)(2,1)} %emb_ref.23, ...), custom_call_target="tpu_custom_call", output_to_operand_aliasing={{0}: (11, {}), {1}: (12, {}), {2}: (13, {})} | custom-call | flops 8053063680 | bytes 18350080 | tf_op jit(solution)/shard_map/pallas_call | solution.py:371
  265.1 8.9 %shard_map.96 = (f32[25140,1024]{1,0:T(8,128)}, bf16[2,256,1024]{2,1,0:T(8,128)(2,1)S(1)}, f32[2,256,1024]{2,1,0:T(8,128)S(1)}, f32[1024,1024]{1,0:T(8,128)S(1)}, f32[8,128]{1,0:T(8,128)S(1)}) custom-call(bf16[25140,1024]{1,0:T(8,128)(2,1)} %emb_ref.23, ...), custom_call_target="tpu_custom_call", output_to_operand_aliasing={{0}: (11, {}), {1}: (12, {}), {2}: (13, {})} | custom-call | flops 6442450944 | bytes 14680064 | tf_op jit(solution)/shard_map/pallas_call | solution.py:371
  274.2 5.1 %shard_map.97 = (f32[25140,1024]{1,0:T(8,128)}, bf16[2,256,1024]{2,1,0:T(8,128)(2,1)S(1)}, f32[2,256,1024]{2,1,0:T(8,128)S(1)}, f32[512,1024]{1,0:T(8,128)S(1)}, f32[8,128]{1,0:T(8,128)}) custom-call(bf16[25140,1024]{1,0:T(8,128)(2,1)} %emb_ref.23, ...), custom_call_target="tpu_custom_call", output_to_operand_aliasing={{0}: (11, {}), {1}: (12, {}), {2}: (13, {})} | custom-call | flops 3221225472 | bytes 7340032 | tf_op jit(solution)/shard_map/pallas_call | solution.py:371
  280.4 1.1 collective-permute-start.16
  281.5 2.7 collective-permute-done.14.refs_1_
  284.2 3.1 %shard_map.98 = (f32[25140,1024]{1,0:T(8,128)}, f32[1,1024]{1,0:T(1,128)}, f32[1,1]{1,0:T(1,128)}) custom-call(bf16[64,1024]{1,0:T(8,128)(2,1)S(1)} %pad.8.tail_ref, bf16[512,1024]{1,0:T(8,128)(2,1)S(1)} %get-tuple-element.87.ha_ref.hc_ref.xc_ref, bf16[512,1024]{1,0:T(8,128)(2,1)S(1)} %get-tuple-element.89.hb_ref.hd_ref.xd_ref, ...), custom_call_target="tpu_custom_call", output_to_operand_aliasing={{0}: (11, {})} | custom-call | flops 536870912 | bytes 262144 | tf_op jit(solution)/shard_map/pallas_call | solution.py:425
  287.3 3.4 %shard_map.99 = f32[25140,1024]{1,0:T(8,128)} custom-call(f32[25140,1024]{1,0:T(8,128)} %get-tuple-element.167._, f32[512,1024]{1,0:T(8,128)S(1)} %get-tuple-element.168.refs_0_, f32[1024,1024]{1,0:T(8,128)S(1)} %collective-permute-done.21.refs_1_, f32[512,1024]{1,0:T(8,128)S(1)} %collective-permute-done.22.refs_2_), custom_call_target="tpu_custom_call", output_to_operand_aliasing={{}: (0, {})} | custom-call | flops 1000000 | bytes 8388608 | tf_op jit(solution)/shard_map/pallas_call | solution.py:436
  (52 shorter events, 4.8 us)
Async XLA Ops:
  0.6 1.6 copy-start
  2.2 1.2 copy-start.1
  3.4 0.7 copy-start.2
  6.3 5.2 %collective-permute-start = (f32[512,1024]{1,0:T(8,128)}, f32[512,1024]{1,0:T(8,128)}, u32[]{:S(2)}, u32[]{:S(2)}) collective-permute-start(f32[512,1024]{1,0:T(8,128)} %get-tuple-element.88.scaled_ref), channel_id=1, source_target_pairs={{0,1},{1,0},{2,3},{3,2},{4,5},{5,4},{6,7},{7,6}} | collective-permute-start | bytes 6291464 | tf_op jit(solution)/shard_map/ppermute | solution.py:312
  7.1 54.7 %collective-permute-start.5 = (f32[512,1024]{1,0:T(8,128)}, f32[512,1024]{1,0:T(8,128)S(1)}, u32[]{:S(2)}, u32[]{:S(2)}) collective-permute-start(f32[512,1024]{1,0:T(8,128)} %get-tuple-element.88.scaled_ref), channel_id=1, source_target_pairs={{0,2},{1,3},{2,0},{3,1},{4,6},{5,7},{6,4},{7,5}} | collective-permute-start | bytes 6291464 | tf_op jit(solution)/shard_map/ppermute | solution.py:276
  9.6 1.8 collective-permute-start.1
  11.5 0.7 copy-start.3
  55.2 2.8 collective-permute-start.2
  55.5 3.9 %collective-permute-start.4 = (f32[3,1024]{1,0:T(4,128)S(1)}, f32[3,1024]{1,0:T(4,128)S(1)}, u32[]{:S(2)}, u32[]{:S(2)}) collective-permute-start(f32[3,1024]{1,0:T(4,128)S(1)} %slice.64), channel_id=1, source_target_pairs={{0,5},{1,4},{2,7},{3,6},{4,1},{5,0},{6,3},{7,2}} | collective-permute-start | bytes 36872 | tf_op jit(solution)/shard_map/ppermute | solution.py:339
  58.0 3.7 %collective-permute-start.3 = (f32[3,1024]{1,0:T(4,128)S(1)}, f32[3,1024]{1,0:T(4,128)S(1)}, u32[]{:S(2)}, u32[]{:S(2)}) collective-permute-start(f32[3,1024]{1,0:T(4,128)S(1)} %slice.64), channel_id=1, source_target_pairs={{0,4},{4,0},{1,5},{5,1},{2,6},{6,2},{3,7},{7,3}} | collective-permute-start | bytes 36872 | tf_op jit(solution)/shard_map/ppermute | solution.py:338
  61.9 37.2 %collective-permute-start.7 = (f32[512,1024]{1,0:T(8,128)S(1)}, f32[512,1024]{1,0:T(8,128)S(1)}, u32[]{:S(2)}, u32[]{:S(2)}) collective-permute-start(f32[512,1024]{1,0:T(8,128)S(1)} %collective-permute-done.5.refs_1_), channel_id=1, source_target_pairs={{0,1},{1,0},{2,3},{3,2},{4,5},{5,4},{6,7},{7,6}} | collective-permute-start | bytes 6291464 | tf_op jit(solution)/shard_map/ppermute | solution.py:276
  61.9 37.2 %collective-permute-start.6 = (f32[8,1024]{1,0:T(8,128)S(1)}, f32[8,1024]{1,0:T(8,128)S(1)}, u32[]{:S(2)}, u32[]{:S(2)}) collective-permute-start(f32[8,1024]{1,0:T(8,128)S(1)} %select_maximum_fusion.row_ref), channel_id=1, source_target_pairs={{0,2},{1,3},{2,0},{3,1},{4,6},{5,7},{6,4},{7,5}} | collective-permute-start | bytes 98312 | tf_op jit(solution)/shard_map/ppermute | solution.py:276
  63.4 35.9 %copy-start.4 = (f32[1024]{0:T(1024)S(1)}, f32[1024]{0:T(1024)}, u32[]{:S(2)}) copy-start(f32[1024]{0:T(1024)} %param.9) | copy-start | bytes 12292
  99.1 11.8 %collective-permute-start.8 = (f32[512,1024]{1,0:T(8,128)S(1)}, f32[512,1024]{1,0:T(8,128)S(1)}, u32[]{:S(2)}, u32[]{:S(2)}) collective-permute-start(f32[512,1024]{1,0:T(8,128)S(1)} %get-tuple-element.107), channel_id=1, source_target_pairs={{0,1},{1,0},{2,3},{3,2},{4,5},{5,4},{6,7},{7,6}} | collective-permute-start | bytes 6291464 | tf_op jit(solution)/shard_map/ppermute | solution.py:276
  123.2 28.8 %collective-permute-start.11 = (f32[1536,1024]{1,0:T(8,128)S(1)}, f32[1536,1024]{1,0:T(8,128)S(1)}, u32[]{:S(2)}, u32[]{:S(2)}) collective-permute-start(f32[1536,1024]{1,0:T(8,128)S(1)} %get-tuple-element.123.refs_3_), channel_id=1, source_target_pairs={{0,1},{1,0},{2,3},{3,2},{4,5},{5,4},{6,7},{7,6}} | collective-permute-start | bytes 18874376 | tf_op jit(solution)/shard_map/ppermute | solution.py:401
  123.6 17.3 %collective-permute-start.10 = (f32[1280,1024]{1,0:T(8,128)S(1)}, f32[1280,1024]{1,0:T(8,128)S(1)}, u32[]{:S(2)}, u32[]{:S(2)}) collective-permute-start(f32[1280,1024]{1,0:T(8,128)S(1)} %get-tuple-element.113.refs_3_), channel_id=1, source_target_pairs={{0,1},{1,0},{2,3},{3,2},{4,5},{5,4},{6,7},{7,6}} | collective-permute-start | bytes 15728648 | tf_op jit(solution)/shard_map/ppermute | solution.py:401
  151.7 13.2 %collective-permute-start.12 = (f32[1280,1024]{1,0:T(8,128)S(1)}, f32[1280,1024]{1,0:T(8,128)S(1)}, u32[]{:S(2)}, u32[]{:S(2)}) collective-permute-start(f32[1280,1024]{1,0:T(8,128)S(1)} %get-tuple-element.128.refs_3_), channel_id=1, source_target_pairs={{0,1},{1,0},{2,3},{3,2},{4,5},{5,4},{6,7},{7,6}} | collective-permute-start | bytes 15728648 | tf_op jit(solution)/shard_map/ppermute | solution.py:401
  164.7 11.3 %collective-permute-start.13 = (f32[1536,1024]{1,0:T(8,128)S(1)}, f32[1536,1024]{1,0:T(8,128)S(1)}, u32[]{:S(2)}, u32[]{:S(2)}) collective-permute-start(f32[1536,1024]{1,0:T(8,128)S(1)} %get-tuple-element.133.refs_3_), channel_id=1, source_target_pairs={{0,1},{1,0},{2,3},{3,2},{4,5},{5,4},{6,7},{7,6}} | collective-permute-start | bytes 18874376 | tf_op jit(solution)/shard_map/ppermute | solution.py:401
  175.7 67.2 %collective-permute-start.17 = (f32[1280,1024]{1,0:T(8,128)S(1)}, f32[1280,1024]{1,0:T(8,128)S(1)}, u32[]{:S(2)}, u32[]{:S(2)}) collective-permute-start(f32[1280,1024]{1,0:T(8,128)S(1)} %get-tuple-element.138.refs_3_), channel_id=1, source_target_pairs={{0,1},{1,0},{2,3},{3,2},{4,5},{5,4},{6,7},{7,6}} | collective-permute-start | bytes 15728648 | tf_op jit(solution)/shard_map/ppermute | solution.py:401
  188.7 65.0 %collective-permute-start.18 = (f32[1536,1024]{1,0:T(8,128)S(1)}, f32[1536,1024]{1,0:T(8,128)S(1)}, u32[]{:S(2)}, u32[]{:S(2)}) collective-permute-start(f32[1536,1024]{1,0:T(8,128)S(1)} %get-tuple-element.148.refs_3_), channel_id=1, source_target_pairs={{0,1},{1,0},{2,3},{3,2},{4,5},{5,4},{6,7},{7,6}} | collective-permute-start | bytes 18874376 | tf_op jit(solution)/shard_map/ppermute | solution.py:401
  189.0 47.9 %collective-permute-start.9 = (f32[512,1024]{1,0:T(8,128)S(1)}, f32[512,1024]{1,0:T(8,128)S(1)}, u32[]{:S(2)}, u32[]{:S(2)}) collective-permute-start(f32[512,1024]{1,0:T(8,128)S(1)} %get-tuple-element.118.near_ref), channel_id=1, source_target_pairs={{0,4},{4,0},{1,5},{5,1},{2,6},{6,2},{3,7},{7,3}} | collective-permute-start | bytes 6291464 | tf_op jit(solution)/shard_map/ppermute | solution.py:276
  253.7 11.3 %collective-permute-start.19 = (f32[1280,1024]{1,0:T(8,128)S(1)}, f32[1280,1024]{1,0:T(8,128)S(1)}, u32[]{:S(2)}, u32[]{:S(2)}) collective-permute-start(f32[1280,1024]{1,0:T(8,128)S(1)} %get-tuple-element.153.refs_3_), channel_id=1, source_target_pairs={{0,1},{1,0},{2,3},{3,2},{4,5},{5,4},{6,7},{7,6}} | collective-permute-start | bytes 15728648 | tf_op jit(solution)/shard_map/ppermute | solution.py:401
  264.8 9.4 %collective-permute-start.20 = (f32[1280,1024]{1,0:T(8,128)S(1)}, f32[1280,1024]{1,0:T(8,128)S(1)}, u32[]{:S(2)}, u32[]{:S(2)}) collective-permute-start(f32[1280,1024]{1,0:T(8,128)S(1)} %get-tuple-element.158.refs_3_), channel_id=1, source_target_pairs={{0,1},{1,0},{2,3},{3,2},{4,5},{5,4},{6,7},{7,6}} | collective-permute-start | bytes 15728648 | tf_op jit(solution)/shard_map/ppermute | solution.py:401
  274.0 13.3 %collective-permute-start.21 = (f32[1024,1024]{1,0:T(8,128)S(1)}, f32[1024,1024]{1,0:T(8,128)S(1)}, u32[]{:S(2)}, u32[]{:S(2)}) collective-permute-start(f32[1024,1024]{1,0:T(8,128)S(1)} %get-tuple-element.163.refs_3_), channel_id=1, source_target_pairs={{0,1},{1,0},{2,3},{3,2},{4,5},{5,4},{6,7},{7,6}} | collective-permute-start | bytes 12582920 | tf_op jit(solution)/shard_map/ppermute | solution.py:401
  279.3 8.0 %collective-permute-start.22 = (f32[512,1024]{1,0:T(8,128)S(1)}, f32[512,1024]{1,0:T(8,128)S(1)}, u32[]{:S(2)}, u32[]{:S(2)}) collective-permute-start(f32[512,1024]{1,0:T(8,128)S(1)} %get-tuple-element.168.refs_0_), channel_id=1, source_target_pairs={{0,1},{1,0},{2,3},{3,2},{4,5},{5,4},{6,7},{7,6}} | collective-permute-start | bytes 6291464 | tf_op jit(solution)/shard_map/ppermute | solution.py:401
  279.6 4.6 %collective-permute-start.14 = (f32[2,1024]{1,0:T(2,128)S(1)}, f32[2,1024]{1,0:T(2,128)S(1)}, u32[]{:S(2)}, u32[]{:S(2)}) collective-permute-start(f32[2,1024]{1,0:T(2,128)S(1)} %get-tuple-element.143.refs_0_), channel_id=1, source_target_pairs={{0,1},{1,0},{2,3},{3,2},{4,5},{5,4},{6,7},{7,6}} | collective-permute-start | bytes 24584 | tf_op jit(solution)/shard_map/ppermute | solution.py:276
  279.8 4.3 %collective-permute-start.15 = (f32[2,1024]{1,0:T(2,128)S(1)}, f32[2,1024]{1,0:T(2,128)S(1)}, u32[]{:S(2)}, u32[]{:S(2)}) collective-permute-start(f32[2,1024]{1,0:T(2,128)S(1)} %get-tuple-element.143.refs_0_), channel_id=1, source_target_pairs={{0,2},{1,3},{2,0},{3,1},{4,6},{5,7},{6,4},{7,5}} | collective-permute-start | bytes 24584 | tf_op jit(solution)/shard_map/ppermute | solution.py:276
  280.4 3.8 %collective-permute-start.16 = (f32[2,1024]{1,0:T(2,128)S(1)}, f32[2,1024]{1,0:T(2,128)S(1)}, u32[]{:S(2)}, u32[]{:S(2)}) collective-permute-start(f32[2,1024]{1,0:T(2,128)S(1)} %get-tuple-element.143.refs_0_), channel_id=1, source_target_pairs={{0,3},{1,2},{2,1},{3,0},{4,7},{5,6},{6,5},{7,4}} | collective-permute-start | bytes 24584 | tf_op jit(solution)/shard_map/ppermute | solution.py:276

commit v7 on v6

--- a/solution.py
+++ b/solution.py
@@ -12,7 +12,7 @@
 CH = 256
 STEP = 7
 GROUPS = (1, 2, 2, 2)
-PIECES = (5, 6, 5, 6, 5, 6, 5, 5, 4, 2)
+PIECES = (5, 5, 5, 6, 5, 6, 5, 6, 4, 2)
 ADD_AT, FINISH_AT = 1, 5
 TAIL = 64
 F32, BF16 = jnp.float32, jnp.bfloat16
@@ -306,7 +306,7 @@
                 in_specs=[pl.BlockSpec((rows, d), lambda i: (i, 0)), pl.BlockSpec((rows, d), lambda i: (i, 0)), VM],
                 out_specs=[pl.BlockSpec((rows, d), lambda i: (i, 0)), pl.BlockSpec((rows, d), lambda i: (i, 0)), pl.BlockSpec((rows, 128), lambda i: (i, 0))],
                 out_shape=[jax.ShapeDtypeStruct((half, d), F32), jax.ShapeDtypeStruct((half, d), BF16), jax.ShapeDtypeStruct((half, 128), F32)],
-                compiler_params=params(14),
+                compiler_params=params(56),
                 cost_estimate=cost(1e7, half * d * 12),
             )(hid_loc.reshape(half, d), res_loc.reshape(half, d), norm_row)
             scaled_sib = lax.ppermute(scaled, 'dp', swap)
@@ -398,7 +398,7 @@
                     first, count, mark, out, bufs, prev, own, late, got, far, job, job_args, job_outs)
                 bufs = (emb_buf, log_buf)
                 own, prev = piece, (first, count)
-                arrived.append((prev, lax.ppermute(piece, 'dp', swap)))
+                arrived.append((prev, swapped(piece, 'dp', swap)))
                 first += count
                 if k == 0:
                     far = made
@@ -407,15 +407,15 @@
                     dh_far = swapped(dh_chip, 'tp', flip)
                 if k == FINISH_AT:
                     dh_far, mark = tie((dh_far, mark))
-                    blk_rows = pl.BlockSpec((half // 8, d), lambda i: (i, 0))
+                    blk_rows = pl.BlockSpec((half // 4, d), lambda i: (i, 0))
                     grad_r, grad_w = pl.pallas_call(
                         finish_kernel,
-                        grid=(8,),
-                        in_specs=[VM, pl.BlockSpec((half // 8, 128), lambda i: (i, 0)), VM, blk_rows, blk_rows, blk_rows],
+                        grid=(4,),
+                        in_specs=[VM, pl.BlockSpec((half // 4, 128), lambda i: (i, 0)), VM, blk_rows, blk_rows, blk_rows],
                         out_specs=[blk_rows, VM],
                         scratch_shapes=[pltpu.VMEM((8, d), F32)],
                         out_shape=[jax.ShapeDtypeStruct((half, d), F32), jax.ShapeDtypeStruct((2, d), F32)],
-                        compiler_params=params(4),
+                        compiler_params=params(5),
                         cost_estimate=cost(1e7, half * d * 16),
                     )(norm_row, inv_rms, loss_chip, scaled, dh_chip, dh_far)
                     grad_w, mark = tie((grad_w, mark))

time: 292 us -> 291 us (level)
    ppermute x8 -> x18, waiting for transfers between devices: 50 us -> 67.3 us  [swapped(): return lax.ppermute(value, axis, perm)]
    ppermute x10 -> x0, waiting for transfers between devices: 17.2 us -> none  [local_part(): arrived.append((prev, lax.ppermute(piece, 'dp', swap)))]
    pallas_call x1, Pallas kernels: 6.11 us -> 2.37 us  [local_part(): pl.pallas_call(finish_kernel, grid=(4,), in_specs=[VM, pl.BlockSpec((half...]
    ppermute x8 -> x18, starting transfers between devices: 6.59 us -> 9.11 us  [swapped(): return lax.ppermute(value, axis, perm)]
  transfers between devices with their start and end apart: 23 -> 23, of which waited for: 5 -> 6; matrix products, arithmetic and copies ran while one was open for 1% -> 1% of each run, Pallas kernels for 63% -> 62%
where the time goes in v7:
time: 291 us; the launch traced here: 290 us
  Pallas kernels  201 us (69%)
  waiting for transfers between devices  71 us (24%)
  starting transfers between devices  13 us (4%)
  local copies, waits for them, and re-layouts  3.57 us (1%)
    pallas_call x10, Pallas kernels, piece_call(): pl.pallas_call(functools.partial(grad_kernel, job, first, count, prev, la...  109 us
    ppermute x18, waiting for transfers between devices, swapped(): return lax.ppermute(value, axis, perm)  67.3 us
    pallas_call x1, Pallas kernels, local_part(): pl.pallas_call(functools.partial(stats_kernel, tail_rows), grid_spec=pltp...  43.1 us
    pallas_call x1, Pallas kernels, local_part(): pl.pallas_call(functools.partial(dh_kernel, tail_rows, inv_n), grid_spec=...  35.8 us
    ppermute x18, starting transfers between devices, swapped(): return lax.ppermute(value, axis, perm)  9.11 us
  transfers between devices with their start and end apart: 23, of which 6 were waited for; matrix products, arithmetic and copies ran while one was open for 1% of the time, Pallas kernels for 62%

profile of v7, /device:TPU:0, one launch (start us, length us, event | category | flops | bytes accessed | tf_op | source)
XLA Modules:
  0.0 289.8 jit_solution(12284852477042434627)
XLA Ops:
  0.6 4.4 %shard_map.84 = (f32[512,1024]{1,0:T(8,128)}, bf16[512,1024]{1,0:T(8,128)(2,1)}, f32[512,128]{1,0:T(8,128)}) custom-call(bf16[512,1024]{1,0:T(8,128)(2,1)} %bitcast.12, f32[512,1024]{1,0:T(8,128)} %bitcast.11, f32[1,1024]{1,0:T(1,128)} %bitcast.7), custom_call_target="tpu_custom_call" | custom-call | flops 10000000 | bytes 6291456 | tf_op jit(solution)/shard_map/pallas_call | solution.py:303
  5.1 0.8 collective-permute-start
  5.9 2.5 collective-permute-start.5
  8.6 0.7 constant_dynamic-update-slice_fusion.1
  9.3 0.9 slice.61
  10.3 1.2 copy-done
  11.5 0.7 copy-done.6
  12.2 43.1 %shard_map.85 = (f32[12544,1024]{1,0:T(8,128)}, f32[64,1024]{1,0:T(8,128)S(1)}, f32[8,1024]{1,0:T(8,128)S(1)}, bf16[512,1024]{1,0:T(8,128)(2,1)S(1)}) custom-call(s32[1]{0:T(128)} %bitcast.3.core_ref, bf16[25140,1024]{1,0:T(8,128)(2,1)} %emb_ref.23, bf16[64,1024]{1,0:T(8,128)(2,1)S(1)} %pad.8.tail_ref, bf16[512,1024]{1,0:T(8,128)(2,1)S(1)} %copy-done, ...), custom_call_target="tpu_custom_call" | custom-call | flops 26306674688 | bytes 77070336 | tf_op jit(solution)/shard_map/pallas_call | solution.py:320
  55.6 2.5 collective-permute-start.4
  58.1 1.4 collective-permute-done.4
  59.5 2.3 collective-permute-done.3
  61.9 1.5 collective-permute-start.6
  63.4 35.8 %shard_map.86 = (f32[512,1024]{1,0:T(8,128)S(1)}, f32[512,1024]{1,0:T(8,128)S(1)}, f32[8,128]{1,0:T(8,128)S(1)}) custom-call(s32[1]{0:T(128)} %bitcast.3.core_ref, bf16[25140,1024]{1,0:T(8,128)(2,1)} %emb_ref.23, f32[12544,1024]{1,0:T(8,128)} %get-tuple-element.90.log_ref, bf16[64,1024]{1,0:T(8,128)(2,1)S(1)} %pad.8.tail_ref, ...), custom_call_target="tpu_custom_call" | custom-call | flops 26306674688 | bytes 77070336 | tf_op jit(solution)/shard_map/pallas_call | solution.py:350
  99.5 11.6 %shard_map.87 = (f32[25140,1024]{1,0:T(8,128)}, bf16[2,256,1024]{2,1,0:T(8,128)(2,1)S(1)}, f32[2,256,1024]{2,1,0:T(8,128)S(1)}, f32[1280,1024]{1,0:T(8,128)S(1)}...) custom-call(bf16[25140,1024]{1,0:T(8,128)(2,1)} %emb_ref.23, ...), custom_call_target="tpu_custom_call" | custom-call | flops 8053063680 | bytes 18350080 | tf_op jit(solution)/shard_map/pallas_call | solution.py:371
  111.4 10.6 %shard_map.88 = (f32[25140,1024]{1,0:T(8,128)}, bf16[2,256,1024]{2,1,0:T(8,128)(2,1)S(1)}, f32[2,256,1024]{2,1,0:T(8,128)S(1)}, f32[1280,1024]{1,0:T(8,128)S(1)}...) custom-call(bf16[25140,1024]{1,0:T(8,128)(2,1)} %emb_ref.23, ...), custom_call_target="tpu_custom_call", output_to_operand_aliasing={{0}: (11, {}), {1}: (12, {}), {2}: (13, {})} | custom-call | flops 8053063680 | bytes 18350080 | tf_op jit(solution)/shard_map/pallas_call | solution.py:371
  122.3 10.9 %shard_map.89 = (f32[25140,1024]{1,0:T(8,128)}, bf16[2,256,1024]{2,1,0:T(8,128)(2,1)S(1)}, f32[2,256,1024]{2,1,0:T(8,128)S(1)}, f32[1280,1024]{1,0:T(8,128)S(1)}, f32[8,128]{1,0:T(8,128)S(1)}) custom-call(bf16[25140,1024]{1,0:T(8,128)(2,1)} %emb_ref.23, ...), custom_call_target="tpu_custom_call", output_to_operand_aliasing={{0}: (11, {}), {1}: (12, {}), {2}: (13, {})} | custom-call | flops 8053063680 | bytes 18350080 | tf_op jit(solution)/shard_map/pallas_call | solution.py:371
  133.1 12.8 %shard_map.90 = (f32[25140,1024]{1,0:T(8,128)}, bf16[2,256,1024]{2,1,0:T(8,128)(2,1)S(1)}, f32[2,256,1024]{2,1,0:T(8,128)S(1)}, f32[1536,1024]{1,0:T(8,128)S(1)}, f32[8,128]{1,0:T(8,128)S(1)}) custom-call(bf16[25140,1024]{1,0:T(8,128)(2,1)} %emb_ref.23, ...), custom_call_target="tpu_custom_call", output_to_operand_aliasing={{0}: (11, {}), {1}: (12, {}), {2}: (13, {})} | custom-call | flops 9663676416 | bytes 22020096 | tf_op jit(solution)/shard_map/pallas_call | solution.py:371
  146.5 17.1 %collective-permute-done.12.refs_4_ = f32[1280,1024]{1,0:T(8,128)S(1)} collective-permute-done((f32[1280,1024]{1,0:T(8,128)S(1)}, f32[1280,1024]{1,0:T(8,128)S(1)}, u32[]{:S(2)}, u32[]{:S(2)}) %collective-permute-start.12) | collective-permute-done | bytes 5242912 | tf_op jit(solution)/shard_map/ppermute | solution.py:276
  163.6 10.9 %shard_map.91 = (f32[25140,1024]{1,0:T(8,128)}, bf16[2,256,1024]{2,1,0:T(8,128)(2,1)S(1)}, f32[2,256,1024]{2,1,0:T(8,128)S(1)}, f32[1280,1024]{1,0:T(8,128)S(1)}, f32[8,128]{1,0:T(8,128)S(1)}) custom-call(bf16[25140,1024]{1,0:T(8,128)(2,1)} %emb_ref.23, ...), custom_call_target="tpu_custom_call", output_to_operand_aliasing={{0}: (11, {}), {1}: (12, {}), {2}: (13, {})} | custom-call | flops 8053063680 | bytes 18350080 | tf_op jit(solution)/shard_map/pallas_call | solution.py:371
  174.9 14.2 %shard_map.92 = (f32[25140,1024]{1,0:T(8,128)}, bf16[2,256,1024]{2,1,0:T(8,128)(2,1)S(1)}, f32[2,256,1024]{2,1,0:T(8,128)S(1)}, f32[1536,1024]{1,0:T(8,128)S(1)}, f32[8,128]{1,0:T(8,128)S(1)}) custom-call(bf16[25140,1024]{1,0:T(8,128)(2,1)} %emb_ref.23, ...), custom_call_target="tpu_custom_call", output_to_operand_aliasing={{0}: (11, {}), {1}: (12, {}), {2}: (13, {})} | custom-call | flops 9663676416 | bytes 22020096 | tf_op jit(solution)/shard_map/pallas_call | solution.py:371
  189.8 47.3 %collective-permute-done.9.far_ref = f32[512,1024]{1,0:T(8,128)S(1)} collective-permute-done((f32[512,1024]{1,0:T(8,128)S(1)}, f32[512,1024]{1,0:T(8,128)S(1)}, u32[]{:S(2)}, u32[]{:S(2)}) %collective-permute-start.9) | collective-permute-done | bytes 2097184 | tf_op jit(solution)/shard_map/ppermute | solution.py:276
  237.2 2.4 shard_map.93
  239.5 10.9 %shard_map.94 = (f32[25140,1024]{1,0:T(8,128)}, bf16[2,256,1024]{2,1,0:T(8,128)(2,1)S(1)}, f32[2,256,1024]{2,1,0:T(8,128)S(1)}, f32[1280,1024]{1,0:T(8,128)S(1)}, f32[8,128]{1,0:T(8,128)S(1)}) custom-call(bf16[25140,1024]{1,0:T(8,128)(2,1)} %emb_ref.23, ...), custom_call_target="tpu_custom_call", output_to_operand_aliasing={{0}: (11, {}), {1}: (12, {}), {2}: (13, {})} | custom-call | flops 8053063680 | bytes 18350080 | tf_op jit(solution)/shard_map/pallas_call | solution.py:371
  250.5 13.0 %shard_map.95 = (f32[25140,1024]{1,0:T(8,128)}, bf16[2,256,1024]{2,1,0:T(8,128)(2,1)S(1)}, f32[2,256,1024]{2,1,0:T(8,128)S(1)}, f32[1536,1024]{1,0:T(8,128)S(1)}, f32[8,128]{1,0:T(8,128)S(1)}) custom-call(bf16[25140,1024]{1,0:T(8,128)(2,1)} %emb_ref.23, ...), custom_call_target="tpu_custom_call", output_to_operand_aliasing={{0}: (11, {}), {1}: (12, {}), {2}: (13, {})} | custom-call | flops 9663676416 | bytes 22020096 | tf_op jit(solution)/shard_map/pallas_call | solution.py:371
  263.8 8.9 %shard_map.96 = (f32[25140,1024]{1,0:T(8,128)}, bf16[2,256,1024]{2,1,0:T(8,128)(2,1)S(1)}, f32[2,256,1024]{2,1,0:T(8,128)S(1)}, f32[1024,1024]{1,0:T(8,128)S(1)}, f32[8,128]{1,0:T(8,128)S(1)}) custom-call(bf16[25140,1024]{1,0:T(8,128)(2,1)} %emb_ref.23, ...), custom_call_target="tpu_custom_call", output_to_operand_aliasing={{0}: (11, {}), {1}: (12, {}), {2}: (13, {})} | custom-call | flops 6442450944 | bytes 14680064 | tf_op jit(solution)/shard_map/pallas_call | solution.py:371
  273.0 0.7 collective-permute-done.20.refs_4_
  273.7 5.2 %shard_map.97 = (f32[25140,1024]{1,0:T(8,128)}, bf16[2,256,1024]{2,1,0:T(8,128)(2,1)S(1)}, f32[2,256,1024]{2,1,0:T(8,128)S(1)}, f32[512,1024]{1,0:T(8,128)S(1)}, f32[8,128]{1,0:T(8,128)}) custom-call(bf16[25140,1024]{1,0:T(8,128)(2,1)} %emb_ref.23, ...), custom_call_target="tpu_custom_call", output_to_operand_aliasing={{0}: (11, {}), {1}: (12, {}), {2}: (13, {})} | custom-call | flops 3221225472 | bytes 7340032 | tf_op jit(solution)/shard_map/pallas_call | solution.py:371
  279.4 0.5 collective-permute-start.15
  279.9 1.1 collective-permute-start.16
  281.0 2.0 collective-permute-done.14.refs_1_
  283.1 3.1 %shard_map.98 = (f32[25140,1024]{1,0:T(8,128)}, f32[1,1024]{1,0:T(1,128)}, f32[1,1]{1,0:T(1,128)}) custom-call(bf16[64,1024]{1,0:T(8,128)(2,1)S(1)} %copy-done.4, bf16[512,1024]{1,0:T(8,128)(2,1)S(1)} %copy-done.1, bf16[512,1024]{1,0:T(8,128)(2,1)S(1)} %get-tuple-element.89.hb_ref.hd_ref.xd_ref, ...), custom_call_target="tpu_custom_call", output_to_operand_aliasing={{0}: (11, {})} | custom-call | flops 536870912 | bytes 262144 | tf_op jit(solution)/shard_map/pallas_call | solution.py:425
  286.2 3.4 %shard_map.99 = f32[25140,1024]{1,0:T(8,128)} custom-call(f32[25140,1024]{1,0:T(8,128)} %get-tuple-element.167._, f32[512,1024]{1,0:T(8,128)S(1)} %get-tuple-element.168.refs_0_, f32[1024,1024]{1,0:T(8,128)S(1)} %collective-permute-done.21.refs_1_, f32[512,1024]{1,0:T(8,128)S(1)} %collective-permute-done.22.refs_2_), custom_call_target="tpu_custom_call", output_to_operand_aliasing={{}: (0, {})} | custom-call | flops 1000000 | bytes 8388608 | tf_op jit(solution)/shard_map/pallas_call | solution.py:436
  (58 shorter events, 4.3 us)
Async XLA Ops:
  5.1 5.2 %collective-permute-start = (f32[512,1024]{1,0:T(8,128)}, f32[512,1024]{1,0:T(8,128)}, u32[]{:S(2)}, u32[]{:S(2)}) collective-permute-start(f32[512,1024]{1,0:T(8,128)} %get-tuple-element.88.scaled_ref), channel_id=1, source_target_pairs={{0,1},{1,0},{2,3},{3,2},{4,5},{5,4},{6,7},{7,6}} | collective-permute-start | bytes 6291464 | tf_op jit(solution)/shard_map/ppermute | solution.py:312
  5.9 56.0 %collective-permute-start.5 = (f32[512,1024]{1,0:T(8,128)}, f32[512,1024]{1,0:T(8,128)S(1)}, u32[]{:S(2)}, u32[]{:S(2)}) collective-permute-start(f32[512,1024]{1,0:T(8,128)} %get-tuple-element.88.scaled_ref), channel_id=1, source_target_pairs={{0,2},{1,3},{2,0},{3,1},{4,6},{5,7},{6,4},{7,5}} | collective-permute-start | bytes 6291464 | tf_op jit(solution)/shard_map/ppermute | solution.py:276
  8.4 1.8 collective-permute-start.1
  10.2 53.2 %copy-start.3 = (bf16[64,1024]{1,0:T(8,128)(2,1)}, bf16[64,1024]{1,0:T(8,128)(2,1)S(1)}, u32[]{:S(2)}) copy-start(bf16[64,1024]{1,0:T(8,128)(2,1)S(1)} %pad.8.tail_ref) | copy-start | bytes 393220
  10.3 1.2 copy-start
  11.5 0.7 copy-start.6
  55.2 2.8 collective-permute-start.2
  55.6 3.9 %collective-permute-start.4 = (f32[3,1024]{1,0:T(4,128)S(1)}, f32[3,1024]{1,0:T(4,128)S(1)}, u32[]{:S(2)}, u32[]{:S(2)}) collective-permute-start(f32[3,1024]{1,0:T(4,128)S(1)} %slice.64), channel_id=1, source_target_pairs={{0,5},{1,4},{2,7},{3,6},{4,1},{5,0},{6,3},{7,2}} | collective-permute-start | bytes 36872 | tf_op jit(solution)/shard_map/ppermute | solution.py:339
  58.0 3.7 %collective-permute-start.3 = (f32[3,1024]{1,0:T(4,128)S(1)}, f32[3,1024]{1,0:T(4,128)S(1)}, u32[]{:S(2)}, u32[]{:S(2)}) collective-permute-start(f32[3,1024]{1,0:T(4,128)S(1)} %slice.64), channel_id=1, source_target_pairs={{0,4},{4,0},{1,5},{5,1},{2,6},{6,2},{3,7},{7,3}} | collective-permute-start | bytes 36872 | tf_op jit(solution)/shard_map/ppermute | solution.py:338
  61.9 37.3 %collective-permute-start.7 = (f32[512,1024]{1,0:T(8,128)S(1)}, f32[512,1024]{1,0:T(8,128)S(1)}, u32[]{:S(2)}, u32[]{:S(2)}) collective-permute-start(f32[512,1024]{1,0:T(8,128)S(1)} %collective-permute-done.5.refs_1_), channel_id=1, source_target_pairs={{0,1},{1,0},{2,3},{3,2},{4,5},{5,4},{6,7},{7,6}} | collective-permute-start | bytes 6291464 | tf_op jit(solution)/shard_map/ppermute | solution.py:276
  61.9 37.3 %collective-permute-start.6 = (f32[8,1024]{1,0:T(8,128)S(1)}, f32[8,1024]{1,0:T(8,128)S(1)}, u32[]{:S(2)}, u32[]{:S(2)}) collective-permute-start(f32[8,1024]{1,0:T(8,128)S(1)} %select_maximum_fusion.row_ref), channel_id=1, source_target_pairs={{0,2},{1,3},{2,0},{3,1},{4,6},{5,7},{6,4},{7,5}} | collective-permute-start | bytes 98312 | tf_op jit(solution)/shard_map/ppermute | solution.py:276
  63.4 36.0 %copy-start.1 = (bf16[512,1024]{1,0:T(8,128)(2,1)S(1)}, bf16[512,1024]{1,0:T(8,128)(2,1)}, u32[]{:S(2)}) copy-start(bf16[512,1024]{1,0:T(8,128)(2,1)} %get-tuple-element.87.ha_ref.hc_ref.xc_ref) | copy-start | bytes 3145732
  63.4 36.0 %copy-start.7 = (f32[1024]{0:T(1024)S(1)}, f32[1024]{0:T(1024)}, u32[]{:S(2)}) copy-start(f32[1024]{0:T(1024)} %param.9) | copy-start | bytes 12292
  99.2 12.2 %collective-permute-start.8 = (f32[512,1024]{1,0:T(8,128)S(1)}, f32[512,1024]{1,0:T(8,128)S(1)}, u32[]{:S(2)}, u32[]{:S(2)}) collective-permute-start(f32[512,1024]{1,0:T(8,128)S(1)} %get-tuple-element.107), channel_id=1, source_target_pairs={{0,1},{1,0},{2,3},{3,2},{4,5},{5,4},{6,7},{7,6}} | collective-permute-start | bytes 6291464 | tf_op jit(solution)/shard_map/ppermute | solution.py:276
  111.1 11.2 %collective-permute-start.10 = (f32[1280,1024]{1,0:T(8,128)S(1)}, f32[1280,1024]{1,0:T(8,128)S(1)}, u32[]{:S(2)}, u32[]{:S(2)}) collective-permute-start(f32[1280,1024]{1,0:T(8,128)S(1)} %get-tuple-element.113.refs_3_), channel_id=1, source_target_pairs={{0,1},{1,0},{2,3},{3,2},{4,5},{5,4},{6,7},{7,6}} | collective-permute-start | bytes 15728648 | tf_op jit(solution)/shard_map/ppermute | solution.py:276
  122.0 11.1 %collective-permute-start.11 = (f32[1280,1024]{1,0:T(8,128)S(1)}, f32[1280,1024]{1,0:T(8,128)S(1)}, u32[]{:S(2)}, u32[]{:S(2)}) collective-permute-start(f32[1280,1024]{1,0:T(8,128)S(1)} %get-tuple-element.123.refs_3_), channel_id=1, source_target_pairs={{0,1},{1,0},{2,3},{3,2},{4,5},{5,4},{6,7},{7,6}} | collective-permute-start | bytes 15728648 | tf_op jit(solution)/shard_map/ppermute | solution.py:276
  146.0 28.9 %collective-permute-start.13 = (f32[1536,1024]{1,0:T(8,128)S(1)}, f32[1536,1024]{1,0:T(8,128)S(1)}, u32[]{:S(2)}, u32[]{:S(2)}) collective-permute-start(f32[1536,1024]{1,0:T(8,128)S(1)} %get-tuple-element.133.refs_3_), channel_id=1, source_target_pairs={{0,1},{1,0},{2,3},{3,2},{4,5},{5,4},{6,7},{7,6}} | collective-permute-start | bytes 18874376 | tf_op jit(solution)/shard_map/ppermute | solution.py:276
  146.3 17.3 %collective-permute-start.12 = (f32[1280,1024]{1,0:T(8,128)S(1)}, f32[1280,1024]{1,0:T(8,128)S(1)}, u32[]{:S(2)}, u32[]{:S(2)}) collective-permute-start(f32[1280,1024]{1,0:T(8,128)S(1)} %get-tuple-element.128.refs_3_), channel_id=1, source_target_pairs={{0,1},{1,0},{2,3},{3,2},{4,5},{5,4},{6,7},{7,6}} | collective-permute-start | bytes 15728648 | tf_op jit(solution)/shard_map/ppermute | solution.py:276
  174.5 65.0 %collective-permute-start.17 = (f32[1280,1024]{1,0:T(8,128)S(1)}, f32[1280,1024]{1,0:T(8,128)S(1)}, u32[]{:S(2)}, u32[]{:S(2)}) collective-permute-start(f32[1280,1024]{1,0:T(8,128)S(1)} %get-tuple-element.138.refs_3_), channel_id=1, source_target_pairs={{0,1},{1,0},{2,3},{3,2},{4,5},{5,4},{6,7},{7,6}} | collective-permute-start | bytes 15728648 | tf_op jit(solution)/shard_map/ppermute | solution.py:276
  174.8 62.3 %copy-start.2 = (f32[512,1024]{1,0:T(8,128)S(1)}, f32[512,1024]{1,0:T(8,128)}, u32[]{:S(2)}) copy-start(f32[512,1024]{1,0:T(8,128)} %get-tuple-element.88.scaled_ref) | copy-start | bytes 6291460
  174.8 62.3 %copy-start.5 = (f32[512,128]{1,0:T(8,128)S(1)}, f32[512,128]{1,0:T(8,128)}, u32[]{:S(2)}) copy-start(f32[512,128]{1,0:T(8,128)} %get-tuple-element.103.inv_ref) | copy-start | bytes 786436
  189.1 61.4 %collective-permute-start.18 = (f32[1536,1024]{1,0:T(8,128)S(1)}, f32[1536,1024]{1,0:T(8,128)S(1)}, u32[]{:S(2)}, u32[]{:S(2)}) collective-permute-start(f32[1536,1024]{1,0:T(8,128)S(1)} %get-tuple-element.148.refs_3_), channel_id=1, source_target_pairs={{0,1},{1,0},{2,3},{3,2},{4,5},{5,4},{6,7},{7,6}} | collective-permute-start | bytes 18874376 | tf_op jit(solution)/shard_map/ppermute | solution.py:276
  189.3 47.8 %collective-permute-start.9 = (f32[512,1024]{1,0:T(8,128)S(1)}, f32[512,1024]{1,0:T(8,128)S(1)}, u32[]{:S(2)}, u32[]{:S(2)}) collective-permute-start(f32[512,1024]{1,0:T(8,128)S(1)} %get-tuple-element.118.near_ref), channel_id=1, source_target_pairs={{0,4},{4,0},{1,5},{5,1},{2,6},{6,2},{3,7},{7,3}} | collective-permute-start | bytes 6291464 | tf_op jit(solution)/shard_map/ppermute | solution.py:276
  250.4 13.4 %collective-permute-start.19 = (f32[1280,1024]{1,0:T(8,128)S(1)}, f32[1280,1024]{1,0:T(8,128)S(1)}, u32[]{:S(2)}, u32[]{:S(2)}) collective-permute-start(f32[1280,1024]{1,0:T(8,128)S(1)} %get-tuple-element.153.refs_3_), channel_id=1, source_target_pairs={{0,1},{1,0},{2,3},{3,2},{4,5},{5,4},{6,7},{7,6}} | collective-permute-start | bytes 15728648 | tf_op jit(solution)/shard_map/ppermute | solution.py:276
  263.5 10.2 %collective-permute-start.20 = (f32[1536,1024]{1,0:T(8,128)S(1)}, f32[1536,1024]{1,0:T(8,128)S(1)}, u32[]{:S(2)}, u32[]{:S(2)}) collective-permute-start(f32[1536,1024]{1,0:T(8,128)S(1)} %get-tuple-element.158.refs_3_), channel_id=1, source_target_pairs={{0,1},{1,0},{2,3},{3,2},{4,5},{5,4},{6,7},{7,6}} | collective-permute-start | bytes 18874376 | tf_op jit(solution)/shard_map/ppermute | solution.py:276
  272.7 13.5 %collective-permute-start.21 = (f32[1024,1024]{1,0:T(8,128)S(1)}, f32[1024,1024]{1,0:T(8,128)S(1)}, u32[]{:S(2)}, u32[]{:S(2)}) collective-permute-start(f32[1024,1024]{1,0:T(8,128)S(1)} %get-tuple-element.163.refs_3_), channel_id=1, source_target_pairs={{0,1},{1,0},{2,3},{3,2},{4,5},{5,4},{6,7},{7,6}} | collective-permute-start | bytes 12582920 | tf_op jit(solution)/shard_map/ppermute | solution.py:276
  273.7 9.4 %copy-start.4 = (bf16[64,1024]{1,0:T(8,128)(2,1)S(1)}, bf16[64,1024]{1,0:T(8,128)(2,1)}, u32[]{:S(2)}) copy-start(bf16[64,1024]{1,0:T(8,128)(2,1)} %copy-done.3) | copy-start | bytes 393220
  278.8 7.4 %collective-permute-start.22 = (f32[512,1024]{1,0:T(8,128)S(1)}, f32[512,1024]{1,0:T(8,128)S(1)}, u32[]{:S(2)}, u32[]{:S(2)}) collective-permute-start(f32[512,1024]{1,0:T(8,128)S(1)} %get-tuple-element.168.refs_0_), channel_id=1, source_target_pairs={{0,1},{1,0},{2,3},{3,2},{4,5},{5,4},{6,7},{7,6}} | collective-permute-start | bytes 6291464 | tf_op jit(solution)/shard_map/ppermute | solution.py:276
  279.1 3.9 %collective-permute-start.14 = (f32[2,1024]{1,0:T(2,128)S(1)}, f32[2,1024]{1,0:T(2,128)S(1)}, u32[]{:S(2)}, u32[]{:S(2)}) collective-permute-start(f32[2,1024]{1,0:T(2,128)S(1)} %get-tuple-element.143.refs_0_), channel_id=1, source_target_pairs={{0,1},{1,0},{2,3},{3,2},{4,5},{5,4},{6,7},{7,6}} | collective-permute-start | bytes 24584 | tf_op jit(solution)/shard_map/ppermute | solution.py:276
  279.4 3.7 %collective-permute-start.15 = (f32[2,1024]{1,0:T(2,128)S(1)}, f32[2,1024]{1,0:T(2,128)S(1)}, u32[]{:S(2)}, u32[]{:S(2)}) collective-permute-start(f32[2,1024]{1,0:T(2,128)S(1)} %get-tuple-element.143.refs_0_), channel_id=1, source_target_pairs={{0,2},{1,3},{2,0},{3,1},{4,6},{5,7},{6,4},{7,5}} | collective-permute-start | bytes 24584 | tf_op jit(solution)/shard_map/ppermute | solution.py:276
  279.9 3.2 %collective-permute-start.16 = (f32[2,1024]{1,0:T(2,128)S(1)}, f32[2,1024]{1,0:T(2,128)S(1)}, u32[]{:S(2)}, u32[]{:S(2)}) collective-permute-start(f32[2,1024]{1,0:T(2,128)S(1)} %get-tuple-element.143.refs_0_), channel_id=1, source_target_pairs={{0,3},{1,2},{2,1},{3,0},{4,7},{5,6},{6,5},{7,4}} | collective-permute-start | bytes 24584 | tf_op jit(solution)/shard_map/ppermute | solution.py:276
